TPU v7x, 256 devices: a whole 4x4x8 slice. The times are simulated.
256 devices in a mesh: seq: 64 (over x_hi, z, y), tp: 4 (over x_lo, core).
Axes of the slice: x: 4 (x_hi: 2, x_lo: 2; x = x_hi * 2 + x_lo), y: 4, z: 8, core: 2. Of those that a mesh axis runs over, the one named last changes fastest.
Arguments:
- queries: bfloat16 [1, 16384, 4096], P(None, 'seq', 'tp'), may hold values from -13 to 13
- key_rows: bfloat16 [1, 16384, 2048], P(None, 'seq', 'tp'), may hold values from -13 to 13
- value_rows: bfloat16 [1, 16384, 2048], P(None, 'seq', 'tp'), may hold values from -6 to 6
- residual: bfloat16 [1, 16384, 3584], P(None, 'seq', 'tp'), may hold values from -6 to 6
- out_weight: bfloat16 [4096, 3584], P('tp')
- post_scale: float32 [3584], P('tp'), may hold values from 0.1 to 1.9
- lengths: int32 [1], replicated, may hold values from 1024 to 4095
- owners: int32 [1, 64], replicated, may hold values from 0 to 63, each once within a row
Outputs:
- hidden_out: bfloat16 [1, 16384, 3584], P(None, 'seq', 'tp')
- cache_keys: bfloat16 [1, 4096, 2048], P(None, 'seq', 'tp')
- cache_values: bfloat16 [1, 4096, 2048], P(None, 'seq', 'tp')
Inputs may be any that keep to these rules, and one draw needn't show every extreme that they name: Each row of owners names every number from 0 to 63 once.
All inputs are finite; a program needn't handle non-finite values.
Results may differ from a plain program's by a relative error of at most 0.0083.
Values may be sent and summed in bfloat16 or wider, within the bound.
No kernel may reach another device: no remote copies, remote signals or barrier semaphores. Data moves between devices by JAX's collectives and lax.ppermute only.
A program may use at most 64 MiB of HBM per device.

v0:
```python
import jax
import jax.numpy as jnp
from jax import lax
from jax.sharding import PartitionSpec as P

D = 3584
HD = 256
WINDOW = 4096


soft_cap = 50.0
norm_eps = 1e-06


def shifted(x, axis, by):
    peers = lax.axis_size(axis)
    pairs = [(i, i + by) for i in range(peers) if 0 <= i + by < peers]
    return lax.ppermute(x, axis, pairs)


def copy_for_each(x, axis):
    peers = lax.axis_size(axis)
    return lax.all_to_all(jnp.broadcast_to(x[None], (peers, *x.shape)), axis, 0, 0, tiled=True)


def of_everyone(x, axis):
    everything = copy_for_each(x, axis)
    return jnp.sum(everything, axis=0)


def in_one_piece(arrays, axis, split_dim, concat_dim, along):
    both = jnp.concatenate(arrays, axis=along)
    out, at, gathered = (
        lax.all_to_all(both, axis, split_axis=split_dim, concat_axis=concat_dim, tiled=True),
        0,
        [],
    )
    for a in arrays:
        gathered.append(lax.slice_in_dim(out, at, at + a.shape[along], axis=along))
        at += a.shape[along]
    return tuple(gathered)


def attend_block(grouped, block_keys, block_values, query_pos, key_pos, state_pair):
    numerator, denominator = state_pair
    seq_count, query_count, kv_local, group_size, head_size = grouped.shape
    keyed_rows = block_keys.reshape(seq_count, block_keys.shape[1], kv_local, head_size)
    valued_rows = block_values.reshape(seq_count, block_values.shape[1], kv_local, head_size)
    scores = jnp.einsum(
        "sqhgd,skhd->shgqk", grouped, keyed_rows, preferred_element_type=jnp.float32
    ) * head_size ** (-0.5)
    capped = soft_cap * jnp.tanh(scores / soft_cap)
    spread = query_pos[:, None] - key_pos[None, :]
    live_mask = (spread >= 0) & (spread < WINDOW) & (key_pos[None, :] >= 0)
    weights = jnp.where(live_mask, jnp.exp(capped), jnp.zeros_like(capped))
    denominator = denominator + jnp.sum(weights, axis=-1)
    numerator = numerator + jnp.einsum(
        "shgqk,skhd->sqhgd",
        weights.astype(jnp.bfloat16),
        valued_rows,
        preferred_element_type=jnp.float32,
    )
    return (numerator, denominator)


def reorder_blocks(blocked, ordering):
    return blocked[ordering]


def local(queries, key_rows, value_rows, residual, out_weight, post_scale, lengths, owners):
    seq_count, shard_len, query_width = queries.shape
    kv_width = key_rows.shape[2]
    kv_local = kv_width // HD
    group_size = query_width // kv_width
    grouped = queries.reshape(seq_count, shard_len, kv_local, group_size, HD)
    position = lax.axis_index("seq")
    seq_devices = lax.axis_size("seq")
    offsets = jnp.arange(shard_len, dtype=jnp.int32)
    query_pos = position * shard_len + offsets
    numerator = jnp.zeros((seq_count, shard_len, kv_local, group_size, HD), jnp.float32)
    denominator = jnp.zeros((seq_count, kv_local, group_size, shard_len), jnp.float32)
    state_pair = attend_block(
        grouped, key_rows, value_rows, query_pos, query_pos, (numerator, denominator)
    )
    hop_count = min(WINDOW // shard_len, seq_devices - 1)
    arrived = []
    current = (key_rows, value_rows)
    for hop_index in range(1, hop_count + 1):
        current = shifted((current[0], current[1]), "seq", 1)
        arrived.append((hop_index, current))
        if len(arrived) == 2 or hop_index == hop_count:
            ordered = arrived[::-1]
            block_keys = jnp.concatenate([member[1][0] for member in ordered], axis=1)
            block_values = jnp.concatenate([member[1][1] for member in ordered], axis=1)
            block_pos = jnp.concatenate(
                [(position - member[0]) * shard_len + offsets for member in ordered]
            )
            state_pair = attend_block(
                grouped, block_keys, block_values, query_pos, block_pos, state_pair
            )
            arrived = []
    numerator, denominator = state_pair
    attended = (numerator / jnp.transpose(denominator, (0, 3, 1, 2))[..., None]).astype(
        jnp.bfloat16
    )
    partial_value = jnp.dot(
        attended.reshape(seq_count * shard_len, query_width),
        out_weight,
        preferred_element_type=jnp.float32,
    )
    partial_value = partial_value.reshape(seq_count, shard_len, out_weight.shape[1])
    branch = lax.psum_scatter(
        partial_value.astype(jnp.bfloat16), "tp", scatter_dimension=2, tiled=True
    ).astype(jnp.float32)
    squares = of_everyone(jnp.sum(branch * branch, axis=-1), "tp")
    normed = branch * lax.rsqrt(squares / D + norm_eps)[..., None] * post_scale
    hidden_out = (residual.astype(jnp.float32) + normed).astype(jnp.bfloat16)
    block_rows = shard_len // seq_devices
    slot_span = WINDOW // shard_len
    live_rows = (query_pos[None, :] >= lengths[:, None] - WINDOW) & (
        query_pos[None, :] < lengths[:, None]
    )
    kept_keys = jnp.where(live_rows[..., None], key_rows, jnp.zeros_like(key_rows))
    kept_values = jnp.where(live_rows[..., None], value_rows, jnp.zeros_like(value_rows))
    devices = jnp.arange(seq_devices, dtype=jnp.int32)
    matches = owners[:, :, None] == devices[None, None, :]
    inverse = jnp.sum(
        jnp.where(matches, devices[None, :, None], jnp.zeros_like(devices)[None, :, None]), axis=1
    )
    outgoing_keys = jax.vmap(reorder_blocks)(
        kept_keys.reshape(seq_count, seq_devices, block_rows, kv_width), inverse
    )
    outgoing_values = jax.vmap(reorder_blocks)(
        kept_values.reshape(seq_count, seq_devices, block_rows, kv_width), inverse
    )
    incoming = in_one_piece((outgoing_keys, outgoing_values), "seq", 1, 1, 0)
    selector = (
        devices[None, :] % slot_span == jnp.arange(slot_span, dtype=jnp.int32)[:, None]
    ).astype(jnp.bfloat16)
    cache_keys = (
        jnp.einsum("md,sdbf->smbf", selector, incoming[0], preferred_element_type=jnp.float32)
        .astype(jnp.bfloat16)
        .reshape(seq_count, slot_span * block_rows, kv_width)
    )
    cache_values = (
        jnp.einsum("md,sdbf->smbf", selector, incoming[1], preferred_element_type=jnp.float32)
        .astype(jnp.bfloat16)
        .reshape(seq_count, slot_span * block_rows, kv_width)
    )
    return (hidden_out, cache_keys, cache_values)


def solution(mesh):
    placed = (
        P(None, "seq", "tp"),
        P(None, "seq", "tp"),
        P(None, "seq", "tp"),
        P(None, "seq", "tp"),
        P("tp", None),
        P("tp"),
        P(),
        P(),
    )
    return jax.shard_map(
        local,
        mesh=mesh,
        in_specs=placed,
        out_specs=(P(None, "seq", "tp"), P(None, "seq", "tp"), P(None, "seq", "tp")),
        check_vma=False,
    )
```

profile of v0, /device:TPU:1, one launch (start us, length us, event | category | flops | bytes accessed | tf_op | source)
XLA Modules:
  0.0 331.5 jit_solution(3584375279290228663)
XLA Ops:
  36.2 4.7 %collective-permute-start.6 = (bf16[1,256,512]{1,2,0:T(8,128)(2,1)S(1)}, bf16[1,256,512]{1,2,0:T(8,128)(2,1)}, u32[]{:S(2)}, u32[]{:S(2)}) collective-permute-start(bf16[1,256,512]{1,2,0:T(8,128)(2,1)S(1)} %collective-permute-done.3), channel_id=1, source_target_pairs={{0,4},{4,8},{8,12},{12,16},{16,20},{20,24},{24,28},{28,32},{32,36}... | collective-permute-start | bytes 786440 | tf_op jit(solution)/shard_map/ppermute | solution.py:18
  45.6 4.9 %collective-permute-start.7 = (bf16[1,256,512]{1,2,0:T(8,128)(2,1)}, bf16[1,256,512]{1,2,0:T(8,128)(2,1)}, u32[]{:S(2)}, u32[]{:S(2)}) collective-permute-start(bf16[1,256,512]{1,2,0:T(8,128)(2,1)} %collective-permute-done.6), channel_id=1, source_target_pairs={{0,4},{4,8},{8,12},{12,16},{16,20},{20,24},{24,28},{28,32},{32,36}... | collective-permute-start | bytes 786440 | tf_op jit(solution)/shard_map/ppermute | solution.py:18
  57.9 4.8 %collective-permute-start.10 = (bf16[1,256,512]{1,2,0:T(8,128)(2,1)}, bf16[1,256,512]{1,2,0:T(8,128)(2,1)}, u32[]{:S(2)}, u32[]{:S(2)}) collective-permute-start(bf16[1,256,512]{1,2,0:T(8,128)(2,1)} %collective-permute-done.7), channel_id=1, source_target_pairs={{0,4},{4,8},{8,12},{12,16},{16,20},{20,24},{24,28},{28,32},{32,36}... | collective-permute-start | bytes 786440 | tf_op jit(solution)/shard_map/ppermute | solution.py:18
  68.3 4.6 %collective-permute-start.11 = (bf16[1,256,512]{1,2,0:T(8,128)(2,1)}, bf16[1,256,512]{1,2,0:T(8,128)(2,1)}, u32[]{:S(2)}, u32[]{:S(2)}) collective-permute-start(bf16[1,256,512]{1,2,0:T(8,128)(2,1)} %collective-permute-done.10), channel_id=1, source_target_pairs={{0,4},{4,8},{8,12},{12,16},{16,20},{20,24},{24,28},{28,32},{32,36}... | collective-permute-start | bytes 786440 | tf_op jit(solution)/shard_map/ppermute | solution.py:18
  80.7 4.7 %collective-permute-start.14 = (bf16[1,256,512]{1,2,0:T(8,128)(2,1)}, bf16[1,256,512]{1,2,0:T(8,128)(2,1)}, u32[]{:S(2)}, u32[]{:S(2)}) collective-permute-start(bf16[1,256,512]{1,2,0:T(8,128)(2,1)} %collective-permute-done.11), channel_id=1, source_target_pairs={{0,4},{4,8},{8,12},{12,16},{16,20},{20,24},{24,28},{28,32},{32,36}... | collective-permute-start | bytes 786440 | tf_op jit(solution)/shard_map/ppermute | solution.py:18
  86.4 4.4 %collective-permute-start.13 = (bf16[1,256,512]{2,1,0:T(8,128)(2,1)S(1)}, bf16[1,256,512]{2,1,0:T(8,128)(2,1)S(1)}, u32[]{:S(2)}, u32[]{:S(2)}) collective-permute-start(bf16[1,256,512]{2,1,0:T(8,128)(2,1)S(1)} %collective-permute-done.12), channel_id=1, source_target_pairs={{0,4},{4,8},{8,12},{12,16},{16,20},{20,24},{24,28},{28,32},{32,36}... | collective-permute-start | bytes 786440 | tf_op jit(solution)/shard_map/ppermute | solution.py:18
  90.8 5.9 %collective-permute-start.15 = (bf16[1,256,512]{1,2,0:T(8,128)(2,1)}, bf16[1,256,512]{1,2,0:T(8,128)(2,1)}, u32[]{:S(2)}, u32[]{:S(2)}) collective-permute-start(bf16[1,256,512]{1,2,0:T(8,128)(2,1)} %collective-permute-done.14), channel_id=1, source_target_pairs={{0,4},{4,8},{8,12},{12,16},{16,20},{20,24},{24,28},{28,32},{32,36}... | collective-permute-start | bytes 786440 | tf_op jit(solution)/shard_map/ppermute | solution.py:18
  98.1 5.0 %collective-permute-start.16 = (bf16[1,256,512]{2,1,0:T(8,128)(2,1)}, bf16[1,256,512]{2,1,0:T(8,128)(2,1)S(1)}, u32[]{:S(2)}, u32[]{:S(2)}) collective-permute-start(bf16[1,256,512]{2,1,0:T(8,128)(2,1)} %copy-done.11), channel_id=1, source_target_pairs={{0,4},{4,8},{8,12},{12,16},{16,20},{20,24},{24,28},{28,32},{32,36}... | collective-permute-start | bytes 786440 | tf_op jit(solution)/shard_map/ppermute | solution.py:18
  104.2 5.4 %collective-permute-start.18 = (bf16[1,256,512]{1,2,0:T(8,128)(2,1)}, bf16[1,256,512]{1,2,0:T(8,128)(2,1)}, u32[]{:S(2)}, u32[]{:S(2)}) collective-permute-start(bf16[1,256,512]{1,2,0:T(8,128)(2,1)} %collective-permute-done.15), channel_id=1, source_target_pairs={{0,4},{4,8},{8,12},{12,16},{16,20},{20,24},{24,28},{28,32},{32,36}... | collective-permute-start | bytes 786440 | tf_op jit(solution)/shard_map/ppermute | solution.py:18
  111.1 5.4 %collective-permute-start.17 = (bf16[1,256,512]{2,1,0:T(8,128)(2,1)S(1)}, bf16[1,256,512]{2,1,0:T(8,128)(2,1)S(1)}, u32[]{:S(2)}, u32[]{:S(2)}) collective-permute-start(bf16[1,256,512]{2,1,0:T(8,128)(2,1)S(1)} %collective-permute-done.16), channel_id=1, source_target_pairs={{0,4},{4,8},{8,12},{12,16},{16,20},{20,24},{24,28},{28,32},{32,36}... | collective-permute-start | bytes 786440 | tf_op jit(solution)/shard_map/ppermute | solution.py:18
  116.6 5.6 %collective-permute-start.19 = (bf16[1,256,512]{1,2,0:T(8,128)(2,1)}, bf16[1,256,512]{1,2,0:T(8,128)(2,1)}, u32[]{:S(2)}, u32[]{:S(2)}) collective-permute-start(bf16[1,256,512]{1,2,0:T(8,128)(2,1)} %collective-permute-done.18), channel_id=1, source_target_pairs={{0,4},{4,8},{8,12},{12,16},{16,20},{20,24},{24,28},{28,32},{32,36}... | collective-permute-start | bytes 786440 | tf_op jit(solution)/shard_map/ppermute | solution.py:18
  128.1 5.7 %collective-permute-start.22 = (bf16[1,256,512]{1,2,0:T(8,128)(2,1)}, bf16[1,256,512]{1,2,0:T(8,128)(2,1)}, u32[]{:S(2)}, u32[]{:S(2)}) collective-permute-start(bf16[1,256,512]{1,2,0:T(8,128)(2,1)} %collective-permute-done.19), channel_id=1, source_target_pairs={{0,4},{4,8},{8,12},{12,16},{16,20},{20,24},{24,28},{28,32},{32,36}... | collective-permute-start | bytes 786440 | tf_op jit(solution)/shard_map/ppermute | solution.py:18
  138.9 5.7 %collective-permute-start.23 = (bf16[1,256,512]{1,2,0:T(8,128)(2,1)}, bf16[1,256,512]{1,2,0:T(8,128)(2,1)}, u32[]{:S(2)}, u32[]{:S(2)}) collective-permute-start(bf16[1,256,512]{1,2,0:T(8,128)(2,1)} %collective-permute-done.22), channel_id=1, source_target_pairs={{0,4},{4,8},{8,12},{12,16},{16,20},{20,24},{24,28},{28,32},{32,36}... | collective-permute-start | bytes 786440 | tf_op jit(solution)/shard_map/ppermute | solution.py:18
  146.0 5.4 %collective-permute-start.24 = (bf16[1,256,512]{2,1,0:T(8,128)(2,1)}, bf16[1,256,512]{2,1,0:T(8,128)(2,1)S(1)}, u32[]{:S(2)}, u32[]{:S(2)}) collective-permute-start(bf16[1,256,512]{2,1,0:T(8,128)(2,1)} %copy-done.13), channel_id=1, source_target_pairs={{0,4},{4,8},{8,12},{12,16},{16,20},{20,24},{24,28},{28,32},{32,36}... | collective-permute-start | bytes 786440 | tf_op jit(solution)/shard_map/ppermute | solution.py:18
  152.5 4.8 %collective-permute-start.26 = (bf16[1,256,512]{1,2,0:T(8,128)(2,1)}, bf16[1,256,512]{1,2,0:T(8,128)(2,1)S(1)}, u32[]{:S(2)}, u32[]{:S(2)}) collective-permute-start(bf16[1,256,512]{1,2,0:T(8,128)(2,1)} %collective-permute-done.23), channel_id=1, source_target_pairs={{0,4},{4,8},{8,12},{12,16},{16,20},{20,24},{24,28},{28,32},{32,36}... | collective-permute-start | bytes 786440 | tf_op jit(solution)/shard_map/ppermute | solution.py:18
  159.8 4.3 %collective-permute-start.25 = (bf16[1,256,512]{2,1,0:T(8,128)(2,1)S(1)}, bf16[1,256,512]{2,1,0:T(8,128)(2,1)S(1)}, u32[]{:S(2)}, u32[]{:S(2)}) collective-permute-start(bf16[1,256,512]{2,1,0:T(8,128)(2,1)S(1)} %collective-permute-done.24), channel_id=1, source_target_pairs={{0,4},{4,8},{8,12},{12,16},{16,20},{20,24},{24,28},{28,32},{32,36}... | collective-permute-start | bytes 786440 | tf_op jit(solution)/shard_map/ppermute | solution.py:18
  164.0 5.0 %collective-permute-start.27 = (bf16[1,256,512]{1,2,0:T(8,128)(2,1)S(1)}, bf16[1,256,512]{1,2,0:T(8,128)(2,1)S(1)}, u32[]{:S(2)}, u32[]{:S(2)}) collective-permute-start(bf16[1,256,512]{1,2,0:T(8,128)(2,1)S(1)} %collective-permute-done.26), channel_id=1, source_target_pairs={{0,4},{4,8},{8,12},{12,16},{16,20},{20,24},{24,28},{28,32},{32,36}... | collective-permute-start | bytes 786440 | tf_op jit(solution)/shard_map/ppermute | solution.py:18
  171.5 5.5 %collective-permute-start.28 = (bf16[1,256,512]{2,1,0:T(8,128)(2,1)S(1)}, bf16[1,256,512]{2,1,0:T(8,128)(2,1)S(1)}, u32[]{:S(2)}, u32[]{:S(2)}) collective-permute-start(bf16[1,256,512]{2,1,0:T(8,128)(2,1)S(1)} %collective-permute-done.25), channel_id=1, source_target_pairs={{0,4},{4,8},{8,12},{12,16},{16,20},{20,24},{24,28},{28,32},{32,36}... | collective-permute-start | bytes 786440 | tf_op jit(solution)/shard_map/ppermute | solution.py:18
  177.1 5.3 %collective-permute-start.30 = (bf16[1,256,512]{1,2,0:T(8,128)(2,1)S(1)}, bf16[1,256,512]{1,2,0:T(8,128)(2,1)}, u32[]{:S(2)}, u32[]{:S(2)}) collective-permute-start(bf16[1,256,512]{1,2,0:T(8,128)(2,1)S(1)} %collective-permute-done.27), channel_id=1, source_target_pairs={{0,4},{4,8},{8,12},{12,16},{16,20},{20,24},{24,28},{28,32},{32,36}... | collective-permute-start | bytes 786440 | tf_op jit(solution)/shard_map/ppermute | solution.py:18
  184.0 4.4 %collective-permute-start.29 = (bf16[1,256,512]{2,1,0:T(8,128)(2,1)S(1)}, bf16[1,256,512]{2,1,0:T(8,128)(2,1)S(1)}, u32[]{:S(2)}, u32[]{:S(2)}) collective-permute-start(bf16[1,256,512]{2,1,0:T(8,128)(2,1)S(1)} %collective-permute-done.28), channel_id=1, source_target_pairs={{0,4},{4,8},{8,12},{12,16},{16,20},{20,24},{24,28},{28,32},{32,36}... | collective-permute-start | bytes 786440 | tf_op jit(solution)/shard_map/ppermute | solution.py:18
  204.0 8.8 %copy.253 = bf16[1,256,3584]{1,0,2:T(2,128)(2,1)} copy(bf16[1,256,3584]{2,1,0:T(8,128)(2,1)} %fusion) | data formatting | bytes 3670016
  220.2 60.3 %all-to-all-start.1 = ((bf16[2,64,4,512]{3,2,0,1:T(4,128)(2,1)}), bf16[2,64,4,512]{3,2,0,1:T(4,128)(2,1)S(1)}, u32[]{:S(2)}, u32[]{:S(2)}) async-start(bf16[2,64,4,512]{3,2,0,1:T(4,128)(2,1)} %copy.202), calls=%async_computation.1 | async-start | bytes 1048576 | tf_op jit(solution)/shard_map/all_to_all | solution.py:34
  280.5 14.0 %all-to-all-done.1 = bf16[2,64,4,512]{3,2,0,1:T(4,128)(2,1)S(1)} async-done(((bf16[2,64,4,512]{3,2,0,1:T(4,128)(2,1)}), bf16[2,64,4,512]{3,2,0,1:T(4,128)(2,1)S(1)}, u32[]{:S(2)}, u32[]{:S(2)}) %all-to-all-start.1) | async-done | bytes 524320 | tf_op jit(solution)/shard_map/all_to_all | solution.py:34
  294.8 18.3 %reduce-scatter.4.cloned.1.call-done = bf16[896,256]{1,0:T(8,128)(2,1)} async-done(((bf16[3584,256]{1,0:T(8,128)(2,1)}), bf16[896,256]{1,0:T(8,128)(2,1)}) %reduce-scatter.4.cloned.1.call-update) | async-done | bytes 458768
  (212 shorter events, 112.9 us)
Async XLA Ops:
  7.2 305.9 %reduce-scatter.4.cloned.1.call-start = ((), (), s32[]{:S(2)}) async-start(), calls=%async_computation.3 | async-start | bytes 2293760
  7.2 15.6 %collective-permute-start = (bf16[1,256,512]{2,1,0:T(8,128)(2,1)}, bf16[1,256,512]{2,1,0:T(8,128)(2,1)S(1)}, u32[]{:S(2)}, u32[]{:S(2)}) collective-permute-start(bf16[1,256,512]{2,1,0:T(8,128)(2,1)} %param.10), channel_id=1, source_target_pairs={{0,4},{4,8},{8,12},{12,16},{16,20},{20,24},{24,28},{28,32},{32,36}... | collective-permute-start | bytes 786440 | tf_op jit(solution)/shard_map/ppermute | solution.py:18
  12.5 12.6 %collective-permute-start.2 = (bf16[1,256,512]{1,2,0:T(8,128)(2,1)S(1)}, bf16[1,256,512]{1,2,0:T(8,128)(2,1)}, u32[]{:S(2)}, u32[]{:S(2)}) collective-permute-start(bf16[1,256,512]{1,2,0:T(8,128)(2,1)S(1)} %copy.169), channel_id=1, source_target_pairs={{0,4},{4,8},{8,12},{12,16},{16,20},{20,24},{24,28},{28,32},{32,36}... | collective-permute-start | bytes 786440 | tf_op jit(solution)/shard_map/ppermute | solution.py:18
  30.4 11.4 %collective-permute-start.4 = (bf16[1,256,512]{2,1,0:T(8,128)(2,1)}, bf16[1,256,512]{2,1,0:T(8,128)(2,1)S(1)}, u32[]{:S(2)}, u32[]{:S(2)}) collective-permute-start(bf16[1,256,512]{2,1,0:T(8,128)(2,1)} %copy-done.14), channel_id=1, source_target_pairs={{0,4},{4,8},{8,12},{12,16},{16,20},{20,24},{24,28},{28,32},{32,36}... | collective-permute-start | bytes 786440 | tf_op jit(solution)/shard_map/ppermute | solution.py:18
  45.6 11.2 %collective-permute-start.7 = (bf16[1,256,512]{1,2,0:T(8,128)(2,1)}, bf16[1,256,512]{1,2,0:T(8,128)(2,1)}, u32[]{:S(2)}, u32[]{:S(2)}) collective-permute-start(bf16[1,256,512]{1,2,0:T(8,128)(2,1)} %collective-permute-done.6), channel_id=1, source_target_pairs={{0,4},{4,8},{8,12},{12,16},{16,20},{20,24},{24,28},{28,32},{32,36}... | collective-permute-start | bytes 786440 | tf_op jit(solution)/shard_map/ppermute | solution.py:18
  52.2 11.4 %collective-permute-start.8 = (bf16[1,256,512]{2,1,0:T(8,128)(2,1)}, bf16[1,256,512]{2,1,0:T(8,128)(2,1)S(1)}, u32[]{:S(2)}, u32[]{:S(2)}) collective-permute-start(bf16[1,256,512]{2,1,0:T(8,128)(2,1)} %copy-done.9), channel_id=1, source_target_pairs={{0,4},{4,8},{8,12},{12,16},{16,20},{20,24},{24,28},{28,32},{32,36}... | collective-permute-start | bytes 786440 | tf_op jit(solution)/shard_map/ppermute | solution.py:18
  57.9 10.4 %collective-permute-start.10 = (bf16[1,256,512]{1,2,0:T(8,128)(2,1)}, bf16[1,256,512]{1,2,0:T(8,128)(2,1)}, u32[]{:S(2)}, u32[]{:S(2)}) collective-permute-start(bf16[1,256,512]{1,2,0:T(8,128)(2,1)} %collective-permute-done.7), channel_id=1, source_target_pairs={{0,4},{4,8},{8,12},{12,16},{16,20},{20,24},{24,28},{28,32},{32,36}... | collective-permute-start | bytes 786440 | tf_op jit(solution)/shard_map/ppermute | solution.py:18
  68.3 11.3 %collective-permute-start.11 = (bf16[1,256,512]{1,2,0:T(8,128)(2,1)}, bf16[1,256,512]{1,2,0:T(8,128)(2,1)}, u32[]{:S(2)}, u32[]{:S(2)}) collective-permute-start(bf16[1,256,512]{1,2,0:T(8,128)(2,1)} %collective-permute-done.10), channel_id=1, source_target_pairs={{0,4},{4,8},{8,12},{12,16},{16,20},{20,24},{24,28},{28,32},{32,36}... | collective-permute-start | bytes 786440 | tf_op jit(solution)/shard_map/ppermute | solution.py:18
  74.9 11.5 %collective-permute-start.12 = (bf16[1,256,512]{2,1,0:T(8,128)(2,1)}, bf16[1,256,512]{2,1,0:T(8,128)(2,1)S(1)}, u32[]{:S(2)}, u32[]{:S(2)}) collective-permute-start(bf16[1,256,512]{2,1,0:T(8,128)(2,1)} %copy-done.10), channel_id=1, source_target_pairs={{0,4},{4,8},{8,12},{12,16},{16,20},{20,24},{24,28},{28,32},{32,36}... | collective-permute-start | bytes 786440 | tf_op jit(solution)/shard_map/ppermute | solution.py:18
  86.4 10.8 %collective-permute-start.13 = (bf16[1,256,512]{2,1,0:T(8,128)(2,1)S(1)}, bf16[1,256,512]{2,1,0:T(8,128)(2,1)S(1)}, u32[]{:S(2)}, u32[]{:S(2)}) collective-permute-start(bf16[1,256,512]{2,1,0:T(8,128)(2,1)S(1)} %collective-permute-done.12), channel_id=1, source_target_pairs={{0,4},{4,8},{8,12},{12,16},{16,20},{20,24},{24,28},{28,32},{32,36}... | collective-permute-start | bytes 786440 | tf_op jit(solution)/shard_map/ppermute | solution.py:18
  90.8 12.3 %collective-permute-start.15 = (bf16[1,256,512]{1,2,0:T(8,128)(2,1)}, bf16[1,256,512]{1,2,0:T(8,128)(2,1)}, u32[]{:S(2)}, u32[]{:S(2)}) collective-permute-start(bf16[1,256,512]{1,2,0:T(8,128)(2,1)} %collective-permute-done.14), channel_id=1, source_target_pairs={{0,4},{4,8},{8,12},{12,16},{16,20},{20,24},{24,28},{28,32},{32,36}... | collective-permute-start | bytes 786440 | tf_op jit(solution)/shard_map/ppermute | solution.py:18
  98.1 13.0 %collective-permute-start.16 = (bf16[1,256,512]{2,1,0:T(8,128)(2,1)}, bf16[1,256,512]{2,1,0:T(8,128)(2,1)S(1)}, u32[]{:S(2)}, u32[]{:S(2)}) collective-permute-start(bf16[1,256,512]{2,1,0:T(8,128)(2,1)} %copy-done.11), channel_id=1, source_target_pairs={{0,4},{4,8},{8,12},{12,16},{16,20},{20,24},{24,28},{28,32},{32,36}... | collective-permute-start | bytes 786440 | tf_op jit(solution)/shard_map/ppermute | solution.py:18
  104.2 12.3 %collective-permute-start.18 = (bf16[1,256,512]{1,2,0:T(8,128)(2,1)}, bf16[1,256,512]{1,2,0:T(8,128)(2,1)}, u32[]{:S(2)}, u32[]{:S(2)}) collective-permute-start(bf16[1,256,512]{1,2,0:T(8,128)(2,1)} %collective-permute-done.15), channel_id=1, source_target_pairs={{0,4},{4,8},{8,12},{12,16},{16,20},{20,24},{24,28},{28,32},{32,36}... | collective-permute-start | bytes 786440 | tf_op jit(solution)/shard_map/ppermute | solution.py:18
  111.1 11.5 %collective-permute-start.17 = (bf16[1,256,512]{2,1,0:T(8,128)(2,1)S(1)}, bf16[1,256,512]{2,1,0:T(8,128)(2,1)S(1)}, u32[]{:S(2)}, u32[]{:S(2)}) collective-permute-start(bf16[1,256,512]{2,1,0:T(8,128)(2,1)S(1)} %collective-permute-done.16), channel_id=1, source_target_pairs={{0,4},{4,8},{8,12},{12,16},{16,20},{20,24},{24,28},{28,32},{32,36}... | collective-permute-start | bytes 786440 | tf_op jit(solution)/shard_map/ppermute | solution.py:18
  123.6 11.7 %collective-permute-start.20 = (bf16[1,256,512]{2,1,0:T(8,128)(2,1)}, bf16[1,256,512]{2,1,0:T(8,128)(2,1)S(1)}, u32[]{:S(2)}, u32[]{:S(2)}) collective-permute-start(bf16[1,256,512]{2,1,0:T(8,128)(2,1)} %copy-done.12), channel_id=1, source_target_pairs={{0,4},{4,8},{8,12},{12,16},{16,20},{20,24},{24,28},{28,32},{32,36}... | collective-permute-start | bytes 786440 | tf_op jit(solution)/shard_map/ppermute | solution.py:18
  128.1 10.8 %collective-permute-start.22 = (bf16[1,256,512]{1,2,0:T(8,128)(2,1)}, bf16[1,256,512]{1,2,0:T(8,128)(2,1)}, u32[]{:S(2)}, u32[]{:S(2)}) collective-permute-start(bf16[1,256,512]{1,2,0:T(8,128)(2,1)} %collective-permute-done.19), channel_id=1, source_target_pairs={{0,4},{4,8},{8,12},{12,16},{16,20},{20,24},{24,28},{28,32},{32,36}... | collective-permute-start | bytes 786440 | tf_op jit(solution)/shard_map/ppermute | solution.py:18
  138.9 12.5 %collective-permute-start.23 = (bf16[1,256,512]{1,2,0:T(8,128)(2,1)}, bf16[1,256,512]{1,2,0:T(8,128)(2,1)}, u32[]{:S(2)}, u32[]{:S(2)}) collective-permute-start(bf16[1,256,512]{1,2,0:T(8,128)(2,1)} %collective-permute-done.22), channel_id=1, source_target_pairs={{0,4},{4,8},{8,12},{12,16},{16,20},{20,24},{24,28},{28,32},{32,36}... | collective-permute-start | bytes 786440 | tf_op jit(solution)/shard_map/ppermute | solution.py:18
  146.0 13.8 %collective-permute-start.24 = (bf16[1,256,512]{2,1,0:T(8,128)(2,1)}, bf16[1,256,512]{2,1,0:T(8,128)(2,1)S(1)}, u32[]{:S(2)}, u32[]{:S(2)}) collective-permute-start(bf16[1,256,512]{2,1,0:T(8,128)(2,1)} %copy-done.13), channel_id=1, source_target_pairs={{0,4},{4,8},{8,12},{12,16},{16,20},{20,24},{24,28},{28,32},{32,36}... | collective-permute-start | bytes 786440 | tf_op jit(solution)/shard_map/ppermute | solution.py:18
  152.5 11.5 %collective-permute-start.26 = (bf16[1,256,512]{1,2,0:T(8,128)(2,1)}, bf16[1,256,512]{1,2,0:T(8,128)(2,1)S(1)}, u32[]{:S(2)}, u32[]{:S(2)}) collective-permute-start(bf16[1,256,512]{1,2,0:T(8,128)(2,1)} %collective-permute-done.23), channel_id=1, source_target_pairs={{0,4},{4,8},{8,12},{12,16},{16,20},{20,24},{24,28},{28,32},{32,36}... | collective-permute-start | bytes 786440 | tf_op jit(solution)/shard_map/ppermute | solution.py:18
  159.8 10.7 %collective-permute-start.25 = (bf16[1,256,512]{2,1,0:T(8,128)(2,1)S(1)}, bf16[1,256,512]{2,1,0:T(8,128)(2,1)S(1)}, u32[]{:S(2)}, u32[]{:S(2)}) collective-permute-start(bf16[1,256,512]{2,1,0:T(8,128)(2,1)S(1)} %collective-permute-done.24), channel_id=1, source_target_pairs={{0,4},{4,8},{8,12},{12,16},{16,20},{20,24},{24,28},{28,32},{32,36}... | collective-permute-start | bytes 786440 | tf_op jit(solution)/shard_map/ppermute | solution.py:18
  164.0 13.0 %collective-permute-start.27 = (bf16[1,256,512]{1,2,0:T(8,128)(2,1)S(1)}, bf16[1,256,512]{1,2,0:T(8,128)(2,1)S(1)}, u32[]{:S(2)}, u32[]{:S(2)}) collective-permute-start(bf16[1,256,512]{1,2,0:T(8,128)(2,1)S(1)} %collective-permute-done.26), channel_id=1, source_target_pairs={{0,4},{4,8},{8,12},{12,16},{16,20},{20,24},{24,28},{28,32},{32,36}... | collective-permute-start | bytes 786440 | tf_op jit(solution)/shard_map/ppermute | solution.py:18
  171.5 12.5 %collective-permute-start.28 = (bf16[1,256,512]{2,1,0:T(8,128)(2,1)S(1)}, bf16[1,256,512]{2,1,0:T(8,128)(2,1)S(1)}, u32[]{:S(2)}, u32[]{:S(2)}) collective-permute-start(bf16[1,256,512]{2,1,0:T(8,128)(2,1)S(1)} %collective-permute-done.25), channel_id=1, source_target_pairs={{0,4},{4,8},{8,12},{12,16},{16,20},{20,24},{24,28},{28,32},{32,36}... | collective-permute-start | bytes 786440 | tf_op jit(solution)/shard_map/ppermute | solution.py:18
  177.1 11.3 %collective-permute-start.30 = (bf16[1,256,512]{1,2,0:T(8,128)(2,1)S(1)}, bf16[1,256,512]{1,2,0:T(8,128)(2,1)}, u32[]{:S(2)}, u32[]{:S(2)}) collective-permute-start(bf16[1,256,512]{1,2,0:T(8,128)(2,1)S(1)} %collective-permute-done.27), channel_id=1, source_target_pairs={{0,4},{4,8},{8,12},{12,16},{16,20},{20,24},{24,28},{28,32},{32,36}... | collective-permute-start | bytes 786440 | tf_op jit(solution)/shard_map/ppermute | solution.py:18
  220.2 74.2 %all-to-all-start.1 = ((bf16[2,64,4,512]{3,2,0,1:T(4,128)(2,1)}), bf16[2,64,4,512]{3,2,0,1:T(4,128)(2,1)S(1)}, u32[]{:S(2)}, u32[]{:S(2)}) async-start(bf16[2,64,4,512]{3,2,0,1:T(4,128)(2,1)} %copy.202), calls=%async_computation.1 | async-start | bytes 1048576 | tf_op jit(solution)/shard_map/all_to_all | solution.py:34
  (41 other events, 476.6 us)
Sparse Core Ops, SparseCore 0:
  216.6 96.4 reduce-scatter.3
where the time goes:
time: 333 us; the launch traced here: 332 us
  starting transfers between devices  209 us (63%)
  waiting for transfers between devices  39.4 us (12%)
  local copies, waits for them, and re-layouts  32 us (10%)
  matrix products  22 us (7%)
  between operations  15.8 us (5%)
  other arithmetic  13.8 us (4%)
    ppermute x32, starting transfers between devices, shifted(): return lax.ppermute(x, axis, pairs)  145 us
    all_to_all x1, starting transfers between devices, in_one_piece(): lax.all_to_all(both, axis, split_axis=split_dim, concat_axis=concat_dim,...  60.3 us
    unnamed x65, local copies, waits for them, and re-layouts  21.2 us
    unnamed x2, waiting for transfers between devices  18.3 us
    all_to_all x1, waiting for transfers between devices, in_one_piece(): lax.all_to_all(both, axis, split_axis=split_dim, concat_axis=concat_dim,...  14 us
    dot_general x9, matrix products, attend_block(): jnp.einsum('sqhgd,skhd->shgqk', grouped, keyed_rows, preferred_element_ty...  12.6 us
    concatenate x8, other arithmetic, local(): block_keys = jnp.concatenate([member[1][0] for member in ordered], axis=1)  7.47 us
  transfers between devices with their start and end apart: 35, of which 12 were waited for; matrix products, arithmetic and copies ran while one was open for 12% of the time, Pallas kernels for 0%

commit v1 on v0

v1 whole, which is shorter than its diff:
```python
import jax
import jax.numpy as jnp
from jax import lax
from jax.sharding import PartitionSpec as P

D = 3584
HD = 256
WINDOW = 4096
LINE = 4

soft_cap = 50.0
norm_eps = 1e-06


def lines(axis):
    count = lax.axis_size(axis)
    return [list(range(at, at + LINE)) for at in range(0, count, LINE)]


def across_line(x):
    return lax.all_to_all(x, "seq", 0, 0, axis_index_groups=lines("seq"), tiled=True)


def swap_core(x):
    peers = lax.axis_size("tp")
    return lax.ppermute(x, "tp", [(i, i ^ 1) for i in range(peers)])


def swap_chip(x):
    peers = lax.axis_size("tp")
    return lax.ppermute(x, "tp", [(i, i ^ 2) for i in range(peers)])


def along(x, by):
    peers = lax.axis_size("seq")
    return lax.ppermute(x, "seq", [(i, i + by) for i in range(peers - by)])


def heads_first(x, heads):
    return jnp.transpose(x.reshape(x.shape[0], heads, HD), (1, 0, 2))


def ordered(is_first, mine, theirs):
    low = jnp.where(is_first, mine, theirs)
    high = jnp.where(is_first, theirs, mine)
    return jnp.concatenate([low, high], axis=0)


def attend_plane(q, k, v, mask, valid):
    scores = jnp.dot(q, k.T, preferred_element_type=jnp.float32) * HD ** (-0.5)
    capped = soft_cap * jnp.tanh(scores / soft_cap)
    weights = jnp.exp(capped)
    if mask is not None:
        weights = jnp.where(mask, weights, 0.0)
    total = jnp.sum(weights, axis=-1)
    mixture = jnp.dot(weights.astype(jnp.bfloat16), v, preferred_element_type=jnp.float32)
    if valid is not None:
        total = jnp.where(valid, total, 0.0)
    return mixture, total


def cache_rows(key_rows, value_rows, lengths, owners, position):
    rows = key_rows.shape[0]
    width = key_rows.shape[1]
    seq_devices = lax.axis_size("seq")
    spans = WINDOW // rows
    block_rows = rows // seq_devices
    row_pos = position * rows + jnp.arange(rows, dtype=jnp.int32)
    live = (row_pos < lengths[0])[:, None]
    both = jnp.concatenate([key_rows, value_rows], axis=1)
    kept = jnp.where(live, both, jnp.zeros_like(both))
    devices = jnp.arange(seq_devices, dtype=jnp.int32)
    inverse = jnp.sum(jnp.where(owners[0][:, None] == devices[None, :], devices[:, None], 0), axis=0)
    outgoing = kept.reshape(seq_devices, block_rows, 2 * width)[inverse]
    outgoing = outgoing.reshape(seq_devices, block_rows * 2 * width)
    group = position // spans
    held = jnp.where(group == 0, outgoing[:spans], jnp.zeros_like(outgoing[:spans]))
    for part in range(1, seq_devices // spans):
        sent = lax.ppermute(
            outgoing[part * spans : (part + 1) * spans],
            "seq",
            [(i, i + part * spans) for i in range(spans)],
        )
        held = jnp.where(group == part, sent, held)
    groups = [list(range(at, at + spans)) for at in range(0, seq_devices, spans)]
    got = lax.all_to_all(held, "seq", 0, 0, axis_index_groups=groups, tiled=True)
    got = got.reshape(spans * block_rows, 2 * width)
    return got[:, :width], got[:, width:]


def local(queries, key_rows, value_rows, residual, out_weight, post_scale, lengths, owners):
    rows = queries.shape[1]
    q, k, v = queries[0], key_rows[0], value_rows[0]
    position = lax.axis_index("seq")
    is_first = lax.axis_index("tp") % 2 == 0
    plane_rows = LINE * rows
    plane = position // LINE
    steps = WINDOW // plane_rows

    theirs = swap_core(jnp.where(is_first, v, k))
    mine = jnp.where(is_first, k, v)
    current = across_line(ordered(is_first, heads_first(mine, 2), heads_first(theirs, 2)))
    halves = [current[: LINE // 2].reshape(-1, HD), current[LINE // 2 :].reshape(-1, HD)]
    planes = [halves]
    for step in range(steps):
        halves = [along(half, LINE) for half in halves]
        planes.append(halves)

    pairs = q.reshape(rows, 2, 2, HD)
    even, odd = pairs[:, :, 0], pairs[:, :, 1]
    keep = jnp.transpose(jnp.where(is_first, even, odd), (1, 0, 2))
    give = jnp.transpose(jnp.where(is_first, odd, even), (1, 0, 2))
    lined = across_line(ordered(is_first, keep, swap_core(give))).reshape(plane_rows, HD)

    at = jnp.arange(plane_rows, dtype=jnp.int32)
    half_rows = plane_rows // 2
    numerator = jnp.zeros((plane_rows, HD), jnp.float32)
    denominator = jnp.zeros((plane_rows,), jnp.float32)
    for step in range(steps + 1):
        for side in range(2):
            own = planes[step][side]
            other = swap_core(own)
            keys = jnp.where(is_first, own, other)
            values = jnp.where(is_first, other, own)
            there = side * half_rows + jnp.arange(half_rows, dtype=jnp.int32)
            mask = None
            if step == 0:
                mask = at[:, None] >= there[None, :]
            if step == steps:
                mask = at[:, None] < there[None, :]
            valid = None if step == 0 else plane >= step
            mixture, total = attend_plane(lined, keys, values, mask, valid)
            numerator = numerator + mixture
            denominator = denominator + total
    attended = (numerator / denominator[:, None]).astype(jnp.bfloat16)

    back = across_line(attended.reshape(LINE, rows, HD))
    low, high = back[: LINE // 2], back[LINE // 2 :]
    theirs = swap_core(jnp.where(is_first, high, low))
    mine = jnp.where(is_first, low, high)
    head_even = jnp.where(is_first, mine, theirs)
    head_odd = jnp.where(is_first, theirs, mine)
    mixed = jnp.concatenate([head_even[0], head_odd[0], head_even[1], head_odd[1]], axis=1)

    width = out_weight.shape[1] // lax.axis_size("tp")
    partial = [
        jnp.dot(
            mixed, out_weight[:, t * width : (t + 1) * width], preferred_element_type=jnp.float32
        )
        for t in range(lax.axis_size("tp"))
    ]
    keep_0 = jnp.where(is_first, partial[0], partial[1])
    keep_1 = jnp.where(is_first, partial[2], partial[3])
    give_0 = jnp.where(is_first, partial[1], partial[0]).astype(jnp.bfloat16)
    give_1 = jnp.where(is_first, partial[3], partial[2]).astype(jnp.bfloat16)
    half_0 = keep_0 + swap_core(give_0).astype(jnp.float32)
    half_1 = keep_1 + swap_core(give_1).astype(jnp.float32)
    low_chip = lax.axis_index("tp") < 2
    kept = jnp.where(low_chip, half_0, half_1)
    given = jnp.where(low_chip, half_1, half_0).astype(jnp.bfloat16)
    branch = kept + swap_chip(given).astype(jnp.float32)
    squares = jnp.sum(branch * branch, axis=-1)
    squares = squares + swap_core(squares)
    squares = squares + swap_chip(squares)
    normed = branch * lax.rsqrt(squares / D + norm_eps)[:, None] * post_scale
    hidden_out = (residual[0].astype(jnp.float32) + normed).astype(jnp.bfloat16)

    cache_keys, cache_values = cache_rows(k, v, lengths, owners, position)
    return (hidden_out[None], cache_keys[None], cache_values[None])


def solution(mesh):
    placed = (
        P(None, "seq", "tp"),
        P(None, "seq", "tp"),
        P(None, "seq", "tp"),
        P(None, "seq", "tp"),
        P("tp", None),
        P("tp"),
        P(),
        P(),
    )
    return jax.shard_map(
        local,
        mesh=mesh,
        in_specs=placed,
        out_specs=(P(None, "seq", "tp"), P(None, "seq", "tp"), P(None, "seq", "tp")),
        check_vma=False,
    )
```

time: 333 us -> 154 us (0.46)
  starting transfers between devices: 209 us -> 82.5 us
  local copies, waits for them, and re-layouts: 32 us -> 8.7 us
  waiting for transfers between devices: 39.4 us -> 23.7 us
  between operations: 15.8 us -> 1.95 us
    ppermute x32 -> x29, starting transfers between devices: 145 us -> 67.2 us  [the longest x8 29.8 us: along(): return lax.ppermute(x, 'seq', [(i, i + by) for i in range(peers - by)])]
    all_to_all x2 -> x4, starting transfers between devices: 63.8 us -> 15.3 us  [the longest x3 11.8 us: across_line(): lax.all_to_all(x, 'seq', 0, 0, axis_index_groups=lines('seq'), tiled=True)]
    unnamed x2 -> x0, waiting for transfers between devices: 18.3 us -> none
    unnamed x65 -> x24, local copies, waits for them, and re-layouts: 21.2 us -> 3.27 us
    concatenate x25 -> x2, other arithmetic: 8.98 us -> 1.7 us  [ordered(): return jnp.concatenate([low, high], axis=0)]
    concatenate x9 -> x2, local copies, waits for them, and re-layouts: 5.29 us -> 0.83 us  [cache_rows(): both = jnp.concatenate([key_rows, value_rows], axis=1)]
    ppermute x32 -> x29, waiting for transfers between devices: 5.61 us -> 8.18 us  [the longest x2 6.14 us: swap_chip(): return lax.ppermute(x, 'tp', [(i, i ^ 2) for i in range(peers)])]
    dot_general x21 -> x24, matrix products: 22 us -> 24.1 us  [the longest x4 10.8 us: local(): jnp.dot(mixed, out_weight[:, t * width:(t + 1) * width], preferred_elemen...]
  transfers between devices with their start and end apart: 35 -> 33, of which waited for: 12 -> 6; matrix products, arithmetic and copies ran while one was open for 12% -> 20% of each run, Pallas kernels for 0% -> 0%
where the time goes in v1:
time: 154 us; the launch traced here: 152 us
  starting transfers between devices  82.5 us (54%)
  matrix products  24.1 us (16%)
  waiting for transfers between devices  23.7 us (15%)
  other arithmetic  11 us (7%)
  local copies, waits for them, and re-layouts  8.7 us (6%)
  between operations  1.95 us (1%)
    ppermute x8, starting transfers between devices, along(): return lax.ppermute(x, 'seq', [(i, i + by) for i in range(peers - by)])  29.8 us
    ppermute x3, starting transfers between devices, cache_rows(): lax.ppermute(outgoing[part * spans:(part + 1) * spans], 'seq', [(i, i + p...  17.9 us
    ppermute x16, starting transfers between devices, swap_core(): return lax.ppermute(x, 'tp', [(i, i ^ 1) for i in range(peers)])  17 us
    all_to_all x3, waiting for transfers between devices, across_line(): lax.all_to_all(x, 'seq', 0, 0, axis_index_groups=lines('seq'), tiled=True)  15.5 us
    all_to_all x3, starting transfers between devices, across_line(): lax.all_to_all(x, 'seq', 0, 0, axis_index_groups=lines('seq'), tiled=True)  11.8 us
    dot_general x4, matrix products, local(): jnp.dot(mixed, out_weight[:, t * width:(t + 1) * width], preferred_elemen...  10.8 us
    dot_general x10, matrix products, attend_plane(): scores = jnp.dot(q, k.T, preferred_element_type=jnp.float32) * HD ** (-0.5)  7.58 us
    ppermute x2, waiting for transfers between devices, swap_chip(): return lax.ppermute(x, 'tp', [(i, i ^ 2) for i in range(peers)])  6.14 us
  transfers between devices with their start and end apart: 33, of which 6 were waited for; matrix products, arithmetic and copies ran while one was open for 20% of the time, Pallas kernels for 0%

profile of v1, /device:TPU:1, one launch (start us, length us, event | category | flops | bytes accessed | tf_op | source)
XLA Modules:
  0.0 151.9 jit_solution(14228686704755368949)
XLA Ops:
  2.9 3.3 %collective-permute-start.1 = (bf16[256,512]{0,1:T(8,128)(2,1)S(1)}, bf16[256,512]{0,1:T(8,128)(2,1)S(1)}, u32[]{:S(2)}, u32[]{:S(2)}) collective-permute-start(bf16[256,512]{0,1:T(8,128)(2,1)S(1)} %get-tuple-element.18), channel_id=1, source_target_pairs={{0,1},{1,0},{2,3},{3,2},{4,5},{5,4},{6,7},{7,6},{8,9},{9,8},{10,11... | collective-permute-start | bytes 786440 | tf_op jit(solution)/shard_map/ppermute | solution.py:26
  8.4 3.5 %all-to-all-start.1 = ((bf16[4,256,256]{1,2,0:T(8,128)(2,1)}), bf16[4,256,256]{1,2,0:T(8,128)(2,1)S(1)}, u32[]{:S(2)}, u32[]{:S(2)}) async-start(bf16[4,256,256]{1,2,0:T(8,128)(2,1)} %pad_maximum_fusion.1), calls=%async_computation.1 | async-start | bytes 1048576 | tf_op jit(solution)/shard_map/all_to_all | solution.py:21
  12.9 8.1 %all-to-all-done.1 = bf16[4,256,256]{1,2,0:T(8,128)(2,1)S(1)} async-done(((bf16[4,256,256]{1,2,0:T(8,128)(2,1)}), bf16[4,256,256]{1,2,0:T(8,128)(2,1)S(1)}, u32[]{:S(2)}, u32[]{:S(2)}) %all-to-all-start.1) | async-done | bytes 524320 | tf_op jit(solution)/shard_map/all_to_all | solution.py:21
  21.0 3.5 %all-to-all-start = ((bf16[4,256,256]{2,1,0:T(8,128)(2,1)}), bf16[4,256,256]{2,1,0:T(8,128)(2,1)S(1)}, u32[]{:S(2)}, u32[]{:S(2)}) async-start(bf16[4,256,256]{2,1,0:T(8,128)(2,1)} %pad_maximum_fusion), calls=%async_computation | async-start | bytes 1048576 | tf_op jit(solution)/shard_map/all_to_all | solution.py:21
  24.6 2.3 %collective-permute-start.6 = (bf16[512,256]{1,0:T(8,128)(2,1)S(1)}, bf16[512,256]{1,0:T(8,128)(2,1)S(1)}, u32[]{:S(2)}, u32[]{:S(2)}) collective-permute-start(bf16[512,256]{1,0:T(8,128)(2,1)S(1)} %bitcast.80), channel_id=1, source_target_pairs={{0,16},{4,20},{8,24},{12,28},{16,32},{20,36},{24,40},{28,44},{32,4... | collective-permute-start | bytes 786440 | tf_op jit(solution)/shard_map/ppermute | solution.py:36
  27.1 3.5 %collective-permute-start.4 = (bf16[512,256]{1,0:T(8,128)(2,1)S(1)}, bf16[512,256]{1,0:T(8,128)(2,1)S(1)}, u32[]{:S(2)}, u32[]{:S(2)}) collective-permute-start(bf16[512,256]{1,0:T(8,128)(2,1)S(1)} %bitcast.76), channel_id=1, source_target_pairs={{0,16},{4,20},{8,24},{12,28},{16,32},{20,36},{24,40},{28,44},{32,4... | collective-permute-start | bytes 786440 | tf_op jit(solution)/shard_map/ppermute | solution.py:36
  30.6 2.3 %collective-permute-start.3 = (bf16[512,256]{1,0:T(8,128)(2,1)S(1)}, bf16[512,256]{1,0:T(8,128)(2,1)S(1)}, u32[]{:S(2)}, u32[]{:S(2)}) collective-permute-start(bf16[512,256]{1,0:T(8,128)(2,1)S(1)} %bitcast.81), channel_id=1, source_target_pairs={{0,1},{1,0},{2,3},{3,2},{4,5},{5,4},{6,7},{7,6},{8,9},{9,8},{10,11... | collective-permute-start | bytes 786440 | tf_op jit(solution)/shard_map/ppermute | solution.py:26
  33.0 3.5 %collective-permute-start.10 = (bf16[512,256]{1,0:T(8,128)(2,1)S(1)}, bf16[512,256]{1,0:T(8,128)(2,1)S(1)}, u32[]{:S(2)}, u32[]{:S(2)}) collective-permute-start(bf16[512,256]{1,0:T(8,128)(2,1)S(1)} %collective-permute-done.6), channel_id=1, source_target_pairs={{0,16},{4,20},{8,24},{12,28},{16,32},{20,36},{24,40},{28,44},{32,4... | collective-permute-start | bytes 786440 | tf_op jit(solution)/shard_map/ppermute | solution.py:36
  36.6 3.2 %collective-permute-start.7 = (bf16[512,256]{1,0:T(8,128)(2,1)S(1)}, bf16[512,256]{1,0:T(8,128)(2,1)S(1)}, u32[]{:S(2)}, u32[]{:S(2)}) collective-permute-start(bf16[512,256]{1,0:T(8,128)(2,1)S(1)} %collective-permute-done.6), channel_id=1, source_target_pairs={{0,1},{1,0},{2,3},{3,2},{4,5},{5,4},{6,7},{7,6},{8,9},{9,8},{10,11... | collective-permute-start | bytes 786440 | tf_op jit(solution)/shard_map/ppermute | solution.py:26
  40.6 4.1 %collective-permute-start.8 = (bf16[512,256]{1,0:T(8,128)(2,1)S(1)}, bf16[512,256]{1,0:T(8,128)(2,1)S(1)}, u32[]{:S(2)}, u32[]{:S(2)}) collective-permute-start(bf16[512,256]{1,0:T(8,128)(2,1)S(1)} %collective-permute-done.4), channel_id=1, source_target_pairs={{0,16},{4,20},{8,24},{12,28},{16,32},{20,36},{24,40},{28,44},{32,4... | collective-permute-start | bytes 786440 | tf_op jit(solution)/shard_map/ppermute | solution.py:36
  47.4 3.1 %collective-permute-start.14 = (bf16[512,256]{1,0:T(8,128)(2,1)S(1)}, bf16[512,256]{1,0:T(8,128)(2,1)S(1)}, u32[]{:S(2)}, u32[]{:S(2)}) collective-permute-start(bf16[512,256]{1,0:T(8,128)(2,1)S(1)} %collective-permute-done.10), channel_id=1, source_target_pairs={{0,16},{4,20},{8,24},{12,28},{16,32},{20,36},{24,40},{28,44},{32,4... | collective-permute-start | bytes 786440 | tf_op jit(solution)/shard_map/ppermute | solution.py:36
  51.6 5.5 %collective-permute-start.12 = (bf16[512,256]{1,0:T(8,128)(2,1)S(1)}, bf16[512,256]{1,0:T(8,128)(2,1)S(1)}, u32[]{:S(2)}, u32[]{:S(2)}) collective-permute-start(bf16[512,256]{1,0:T(8,128)(2,1)S(1)} %collective-permute-done.8), channel_id=1, source_target_pairs={{0,16},{4,20},{8,24},{12,28},{16,32},{20,36},{24,40},{28,44},{32,4... | collective-permute-start | bytes 786440 | tf_op jit(solution)/shard_map/ppermute | solution.py:36
  59.7 4.6 %collective-permute-start.18 = (bf16[512,256]{1,0:T(8,128)(2,1)S(1)}, bf16[512,256]{1,0:T(8,128)(2,1)S(1)}, u32[]{:S(2)}, u32[]{:S(2)}) collective-permute-start(bf16[512,256]{1,0:T(8,128)(2,1)S(1)} %collective-permute-done.14), channel_id=1, source_target_pairs={{0,16},{4,20},{8,24},{12,28},{16,32},{20,36},{24,40},{28,44},{32,4... | collective-permute-start | bytes 786440 | tf_op jit(solution)/shard_map/ppermute | solution.py:36
  65.5 3.2 %collective-permute-start.16 = (bf16[512,256]{1,0:T(8,128)(2,1)S(1)}, bf16[512,256]{1,0:T(8,128)(2,1)S(1)}, u32[]{:S(2)}, u32[]{:S(2)}) collective-permute-start(bf16[512,256]{1,0:T(8,128)(2,1)S(1)} %collective-permute-done.12), channel_id=1, source_target_pairs={{0,16},{4,20},{8,24},{12,28},{16,32},{20,36},{24,40},{28,44},{32,4... | collective-permute-start | bytes 786440 | tf_op jit(solution)/shard_map/ppermute | solution.py:36
  80.2 4.8 %all-to-all-start.2 = ((bf16[4,256,256]{2,1,0:T(8,128)(2,1)}), bf16[4,256,256]{2,1,0:T(8,128)(2,1)S(1)}, u32[]{:S(2)}, u32[]{:S(2)}) async-start(bf16[4,256,256]{2,1,0:T(8,128)(2,1)} %bitcast.14), calls=%async_computation.2 | async-start | bytes 1048576 | tf_op jit(solution)/shard_map/all_to_all | solution.py:21
  86.8 7.4 %all-to-all-done.2 = bf16[4,256,256]{2,1,0:T(8,128)(2,1)S(1)} async-done(((bf16[4,256,256]{2,1,0:T(8,128)(2,1)}), bf16[4,256,256]{2,1,0:T(8,128)(2,1)S(1)}, u32[]{:S(2)}, u32[]{:S(2)}) %all-to-all-start.2) | async-done | bytes 524320 | tf_op jit(solution)/shard_map/all_to_all | solution.py:21
  99.1 2.2 %fusion.2 = f32[256,896]{1,0:T(8,128)S(1)} fusion(bf16[1024,3584]{1,0:T(8,128)(2,1)} %param.12, bf16[256,256]{1,0:T(8,128)(2,1)S(1)} %get-tuple-element.24, bf16[256,256]{1,0:T(8,128)(2,1)S(1)} %get-tuple-element.51, bf16[256,256]{1,0:T(8,128)(2,1)S(1)} %get-tuple-element.23, bf16[256,256]{1,0:T(8,128)(2,1)S(1)} %get-tuple-element.52), kind=kOutput, calls=%fused_computation.17 | convolution fusion | flops 471859200 | bytes 3276800 | tf_op jit(solution)/shard_map/dot_general | solution.py:147
  101.3 3.0 %select_convert_fusion.2 = (bf16[256,896]{1,0:T(8,128)(2,1)}, f32[256,896]{1,0:T(8,128)S(1)}) fusion(f32[256,896]{1,0:T(8,128)S(1)} %fusion.6, pred[]{:T(512)S(6)} %eq.32, bf16[1024,3584]{1,0:T(8,128)(2,1)} %param.12, bf16[256,256]{1,0:T(8,128)(2,1)S(1)} %get-tuple-element.24, bf16[256,256]{1,0:T(8,128)(2,1)S(1)} %get-tuple-element.51, ...), kind=kOutput, calls=%fused_computation.57 | convolution fusion | flops 472088576 | bytes 4653057 | tf_op jit(solution)/shard_map/dot_general | solution.py:147
  104.6 3.3 %select_convert_fusion.1 = (bf16[256,896]{1,0:T(8,128)(2,1)}, f32[256,896]{1,0:T(8,128)}) fusion(f32[256,896]{1,0:T(8,128)S(1)} %fusion.2, pred[]{:T(512)S(6)} %eq.32, bf16[1024,3584]{1,0:T(8,128)(2,1)} %param.12, bf16[256,256]{1,0:T(8,128)(2,1)S(1)} %get-tuple-element.24, bf16[256,256]{1,0:T(8,128)(2,1)S(1)} %get-tuple-element.51, ...), kind=kOutput, calls=%fused_computation.55 | convolution fusion | flops 472088576 | bytes 4653057 | tf_op jit(solution)/shard_map/dot_general | solution.py:147
  111.8 14.0 %collective-permute-start.26 = (bf16[16,4096]{1,0:T(8,128)(2,1)S(1)}, bf16[16,4096]{1,0:T(8,128)(2,1)S(1)}, u32[]{:S(2)}, u32[]{:S(2)}) collective-permute-start(bf16[16,4096]{1,0:T(8,128)(2,1)S(1)} %bitcast.100), channel_id=1, source_target_pairs={{0,192},{4,196},{8,200},{12,204},{16,208},{20,212},{24,216},{28,22... | collective-permute-start | bytes 393224 | tf_op jit(solution)/shard_map/ppermute | solution.py:79
  129.9 2.5 %select_convert_fusion = bf16[256,896]{1,0:T(8,128)(2,1)} fusion(pred[]{:T(512)S(6)} %lt.50, bf16[256,896]{1,0:T(8,128)(2,1)} %collective-permute-done.21, f32[256,896]{1,0:T(8,128)S(1)} %fusion.6, f32[256,896]{1,0:T(8,128)S(1)} %get-tuple-element.48, pred[]{:T(512)S(6)} %eq.32, bf16[256,896]{1,0:T(8,128)(2,1)} %collective-permute-done.22, ...), kind=kLoop, calls=%fused_computation.53 | loop fusion | flops 1835008 | bytes 5046274 | tf_op jit(solution)/shard_map/convert_element_type | solution.py:160
  135.5 3.5 %all-to-all-start.3 = ((bf16[16,2,2048]{2,1,0:T(2,128)(2,1)}), bf16[16,2,2048]{2,1,0:T(2,128)(2,1)S(1)}, u32[]{:S(2)}, u32[]{:S(2)}) async-start(bf16[16,2,2048]{2,1,0:T(2,128)(2,1)} %reshape.136), calls=%async_computation.3 | async-start | bytes 262144 | tf_op jit(solution)/shard_map/all_to_all | solution.py:86
  139.1 5.6 %collective-permute-done.23 = bf16[256,896]{1,0:T(8,128)(2,1)} collective-permute-done((bf16[256,896]{1,0:T(8,128)(2,1)}, bf16[256,896]{1,0:T(8,128)(2,1)}, u32[]{:S(2)}, u32[]{:S(2)}) %collective-permute-start.23) | collective-permute-done | bytes 458784 | tf_op jit(solution)/shard_map/ppermute | solution.py:31
  144.6 2.3 %multiply_reduce_fusion = (f32[256]{0:T(256)S(1)}, f32[256,896]{1,0:T(8,128)S(1)}) fusion(bf16[256,896]{1,0:T(8,128)(2,1)} %collective-permute-done.23, bf16[256,896]{1,0:T(8,128)(2,1)} %collective-permute-done.22, f32[256,896]{1,0:T(8,128)S(1)} %fusion.2, f32[256,896]{1,0:T(8,128)} %get-tuple-element.50, bf16[256,896]{1,0:T(8,128)(2,1)} %collective-permute-done.21, ...), kind=kLoop, calls=%fused_computation.51 | loop fusion | flops 2522880 | bytes 5964802 | tf_op jit(solution)/shard_map/reduce_sum | solution.py:162
  (128 shorter events, 47.7 us)
Async XLA Ops:
  8.4 12.5 %all-to-all-start.1 = ((bf16[4,256,256]{1,2,0:T(8,128)(2,1)}), bf16[4,256,256]{1,2,0:T(8,128)(2,1)S(1)}, u32[]{:S(2)}, u32[]{:S(2)}) async-start(bf16[4,256,256]{1,2,0:T(8,128)(2,1)} %pad_maximum_fusion.1), calls=%async_computation.1 | async-start | bytes 1048576 | tf_op jit(solution)/shard_map/all_to_all | solution.py:21
  21.0 23.8 %all-to-all-start = ((bf16[4,256,256]{2,1,0:T(8,128)(2,1)}), bf16[4,256,256]{2,1,0:T(8,128)(2,1)S(1)}, u32[]{:S(2)}, u32[]{:S(2)}) async-start(bf16[4,256,256]{2,1,0:T(8,128)(2,1)} %pad_maximum_fusion), calls=%async_computation | async-start | bytes 1048576 | tf_op jit(solution)/shard_map/all_to_all | solution.py:21
  24.6 8.4 %collective-permute-start.6 = (bf16[512,256]{1,0:T(8,128)(2,1)S(1)}, bf16[512,256]{1,0:T(8,128)(2,1)S(1)}, u32[]{:S(2)}, u32[]{:S(2)}) collective-permute-start(bf16[512,256]{1,0:T(8,128)(2,1)S(1)} %bitcast.80), channel_id=1, source_target_pairs={{0,16},{4,20},{8,24},{12,28},{16,32},{20,36},{24,40},{28,44},{32,4... | collective-permute-start | bytes 786440 | tf_op jit(solution)/shard_map/ppermute | solution.py:36
  27.1 12.8 %collective-permute-start.4 = (bf16[512,256]{1,0:T(8,128)(2,1)S(1)}, bf16[512,256]{1,0:T(8,128)(2,1)S(1)}, u32[]{:S(2)}, u32[]{:S(2)}) collective-permute-start(bf16[512,256]{1,0:T(8,128)(2,1)S(1)} %bitcast.76), channel_id=1, source_target_pairs={{0,16},{4,20},{8,24},{12,28},{16,32},{20,36},{24,40},{28,44},{32,4... | collective-permute-start | bytes 786440 | tf_op jit(solution)/shard_map/ppermute | solution.py:36
  30.6 10.0 %collective-permute-start.3 = (bf16[512,256]{1,0:T(8,128)(2,1)S(1)}, bf16[512,256]{1,0:T(8,128)(2,1)S(1)}, u32[]{:S(2)}, u32[]{:S(2)}) collective-permute-start(bf16[512,256]{1,0:T(8,128)(2,1)S(1)} %bitcast.81), channel_id=1, source_target_pairs={{0,1},{1,0},{2,3},{3,2},{4,5},{5,4},{6,7},{7,6},{8,9},{9,8},{10,11... | collective-permute-start | bytes 786440 | tf_op jit(solution)/shard_map/ppermute | solution.py:26
  32.9 13.2 %collective-permute-start.2 = (bf16[512,256]{1,0:T(8,128)(2,1)S(1)}, bf16[512,256]{1,0:T(8,128)(2,1)S(1)}, u32[]{:S(2)}, u32[]{:S(2)}) collective-permute-start(bf16[512,256]{1,0:T(8,128)(2,1)S(1)} %bitcast.77), channel_id=1, source_target_pairs={{0,1},{1,0},{2,3},{3,2},{4,5},{5,4},{6,7},{7,6},{8,9},{9,8},{10,11... | collective-permute-start | bytes 786440 | tf_op jit(solution)/shard_map/ppermute | solution.py:26
  33.0 14.3 %collective-permute-start.10 = (bf16[512,256]{1,0:T(8,128)(2,1)S(1)}, bf16[512,256]{1,0:T(8,128)(2,1)S(1)}, u32[]{:S(2)}, u32[]{:S(2)}) collective-permute-start(bf16[512,256]{1,0:T(8,128)(2,1)S(1)} %collective-permute-done.6), channel_id=1, source_target_pairs={{0,16},{4,20},{8,24},{12,28},{16,32},{20,36},{24,40},{28,44},{32,4... | collective-permute-start | bytes 786440 | tf_op jit(solution)/shard_map/ppermute | solution.py:36
  36.6 15.0 %collective-permute-start.7 = (bf16[512,256]{1,0:T(8,128)(2,1)S(1)}, bf16[512,256]{1,0:T(8,128)(2,1)S(1)}, u32[]{:S(2)}, u32[]{:S(2)}) collective-permute-start(bf16[512,256]{1,0:T(8,128)(2,1)S(1)} %collective-permute-done.6), channel_id=1, source_target_pairs={{0,1},{1,0},{2,3},{3,2},{4,5},{5,4},{6,7},{7,6},{8,9},{9,8},{10,11... | collective-permute-start | bytes 786440 | tf_op jit(solution)/shard_map/ppermute | solution.py:26
  39.8 18.6 %collective-permute-start.5 = (bf16[512,256]{1,0:T(8,128)(2,1)S(1)}, bf16[512,256]{1,0:T(8,128)(2,1)S(1)}, u32[]{:S(2)}, u32[]{:S(2)}) collective-permute-start(bf16[512,256]{1,0:T(8,128)(2,1)S(1)} %collective-permute-done.4), channel_id=1, source_target_pairs={{0,1},{1,0},{2,3},{3,2},{4,5},{5,4},{6,7},{7,6},{8,9},{9,8},{10,11... | collective-permute-start | bytes 786440 | tf_op jit(solution)/shard_map/ppermute | solution.py:26
  40.6 10.9 %collective-permute-start.8 = (bf16[512,256]{1,0:T(8,128)(2,1)S(1)}, bf16[512,256]{1,0:T(8,128)(2,1)S(1)}, u32[]{:S(2)}, u32[]{:S(2)}) collective-permute-start(bf16[512,256]{1,0:T(8,128)(2,1)S(1)} %collective-permute-done.4), channel_id=1, source_target_pairs={{0,16},{4,20},{8,24},{12,28},{16,32},{20,36},{24,40},{28,44},{32,4... | collective-permute-start | bytes 786440 | tf_op jit(solution)/shard_map/ppermute | solution.py:36
  47.4 12.3 %collective-permute-start.14 = (bf16[512,256]{1,0:T(8,128)(2,1)S(1)}, bf16[512,256]{1,0:T(8,128)(2,1)S(1)}, u32[]{:S(2)}, u32[]{:S(2)}) collective-permute-start(bf16[512,256]{1,0:T(8,128)(2,1)S(1)} %collective-permute-done.10), channel_id=1, source_target_pairs={{0,16},{4,20},{8,24},{12,28},{16,32},{20,36},{24,40},{28,44},{32,4... | collective-permute-start | bytes 786440 | tf_op jit(solution)/shard_map/ppermute | solution.py:36
  50.5 15.0 %collective-permute-start.11 = (bf16[512,256]{1,0:T(8,128)(2,1)S(1)}, bf16[512,256]{1,0:T(8,128)(2,1)S(1)}, u32[]{:S(2)}, u32[]{:S(2)}) collective-permute-start(bf16[512,256]{1,0:T(8,128)(2,1)S(1)} %collective-permute-done.10), channel_id=1, source_target_pairs={{0,1},{1,0},{2,3},{3,2},{4,5},{5,4},{6,7},{7,6},{8,9},{9,8},{10,11... | collective-permute-start | bytes 786440 | tf_op jit(solution)/shard_map/ppermute | solution.py:26
  51.5 18.4 %collective-permute-start.9 = (bf16[512,256]{1,0:T(8,128)(2,1)S(1)}, bf16[512,256]{1,0:T(8,128)(2,1)S(1)}, u32[]{:S(2)}, u32[]{:S(2)}) collective-permute-start(bf16[512,256]{1,0:T(8,128)(2,1)S(1)} %collective-permute-done.8), channel_id=1, source_target_pairs={{0,1},{1,0},{2,3},{3,2},{4,5},{5,4},{6,7},{7,6},{8,9},{9,8},{10,11... | collective-permute-start | bytes 786440 | tf_op jit(solution)/shard_map/ppermute | solution.py:26
  51.6 13.7 %collective-permute-start.12 = (bf16[512,256]{1,0:T(8,128)(2,1)S(1)}, bf16[512,256]{1,0:T(8,128)(2,1)S(1)}, u32[]{:S(2)}, u32[]{:S(2)}) collective-permute-start(bf16[512,256]{1,0:T(8,128)(2,1)S(1)} %collective-permute-done.8), channel_id=1, source_target_pairs={{0,16},{4,20},{8,24},{12,28},{16,32},{20,36},{24,40},{28,44},{32,4... | collective-permute-start | bytes 786440 | tf_op jit(solution)/shard_map/ppermute | solution.py:36
  59.7 11.5 %collective-permute-start.18 = (bf16[512,256]{1,0:T(8,128)(2,1)S(1)}, bf16[512,256]{1,0:T(8,128)(2,1)S(1)}, u32[]{:S(2)}, u32[]{:S(2)}) collective-permute-start(bf16[512,256]{1,0:T(8,128)(2,1)S(1)} %collective-permute-done.14), channel_id=1, source_target_pairs={{0,16},{4,20},{8,24},{12,28},{16,32},{20,36},{24,40},{28,44},{32,4... | collective-permute-start | bytes 786440 | tf_op jit(solution)/shard_map/ppermute | solution.py:36
  64.3 7.7 %collective-permute-start.15 = (bf16[512,256]{1,0:T(8,128)(2,1)S(1)}, bf16[512,256]{1,0:T(8,128)(2,1)S(1)}, u32[]{:S(2)}, u32[]{:S(2)}) collective-permute-start(bf16[512,256]{1,0:T(8,128)(2,1)S(1)} %collective-permute-done.14), channel_id=1, source_target_pairs={{0,1},{1,0},{2,3},{3,2},{4,5},{5,4},{6,7},{7,6},{8,9},{9,8},{10,11... | collective-permute-start | bytes 786440 | tf_op jit(solution)/shard_map/ppermute | solution.py:26
  65.3 7.9 %collective-permute-start.13 = (bf16[512,256]{1,0:T(8,128)(2,1)S(1)}, bf16[512,256]{1,0:T(8,128)(2,1)S(1)}, u32[]{:S(2)}, u32[]{:S(2)}) collective-permute-start(bf16[512,256]{1,0:T(8,128)(2,1)S(1)} %collective-permute-done.12), channel_id=1, source_target_pairs={{0,1},{1,0},{2,3},{3,2},{4,5},{5,4},{6,7},{7,6},{8,9},{9,8},{10,11... | collective-permute-start | bytes 786440 | tf_op jit(solution)/shard_map/ppermute | solution.py:26
  65.5 9.4 %collective-permute-start.16 = (bf16[512,256]{1,0:T(8,128)(2,1)S(1)}, bf16[512,256]{1,0:T(8,128)(2,1)S(1)}, u32[]{:S(2)}, u32[]{:S(2)}) collective-permute-start(bf16[512,256]{1,0:T(8,128)(2,1)S(1)} %collective-permute-done.12), channel_id=1, source_target_pairs={{0,16},{4,20},{8,24},{12,28},{16,32},{20,36},{24,40},{28,44},{32,4... | collective-permute-start | bytes 786440 | tf_op jit(solution)/shard_map/ppermute | solution.py:36
  80.2 14.0 %all-to-all-start.2 = ((bf16[4,256,256]{2,1,0:T(8,128)(2,1)}), bf16[4,256,256]{2,1,0:T(8,128)(2,1)S(1)}, u32[]{:S(2)}, u32[]{:S(2)}) async-start(bf16[4,256,256]{2,1,0:T(8,128)(2,1)} %bitcast.14), calls=%async_computation.2 | async-start | bytes 1048576 | tf_op jit(solution)/shard_map/all_to_all | solution.py:21
  104.3 25.6 %collective-permute-start.21 = (bf16[256,896]{1,0:T(8,128)(2,1)}, bf16[256,896]{1,0:T(8,128)(2,1)}, u32[]{:S(2)}, u32[]{:S(2)}) collective-permute-start(bf16[256,896]{1,0:T(8,128)(2,1)} %get-tuple-element.47), channel_id=1, source_target_pairs={{0,1},{1,0},{2,3},{3,2},{4,5},{5,4},{6,7},{7,6},{8,9},{9,8},{10,11... | collective-permute-start | bytes 1376264 | tf_op jit(solution)/shard_map/ppermute | solution.py:26
  108.0 21.9 %collective-permute-start.22 = (bf16[256,896]{1,0:T(8,128)(2,1)}, bf16[256,896]{1,0:T(8,128)(2,1)}, u32[]{:S(2)}, u32[]{:S(2)}) collective-permute-start(bf16[256,896]{1,0:T(8,128)(2,1)} %get-tuple-element.49), channel_id=1, source_target_pairs={{0,1},{1,0},{2,3},{3,2},{4,5},{5,4},{6,7},{7,6},{8,9},{9,8},{10,11... | collective-permute-start | bytes 1376264 | tf_op jit(solution)/shard_map/ppermute | solution.py:26
  111.8 21.7 %collective-permute-start.26 = (bf16[16,4096]{1,0:T(8,128)(2,1)S(1)}, bf16[16,4096]{1,0:T(8,128)(2,1)S(1)}, u32[]{:S(2)}, u32[]{:S(2)}) collective-permute-start(bf16[16,4096]{1,0:T(8,128)(2,1)S(1)} %bitcast.100), channel_id=1, source_target_pairs={{0,192},{4,196},{8,200},{12,204},{16,208},{20,212},{24,216},{28,22... | collective-permute-start | bytes 393224 | tf_op jit(solution)/shard_map/ppermute | solution.py:79
  132.3 12.3 %collective-permute-start.23 = (bf16[256,896]{1,0:T(8,128)(2,1)}, bf16[256,896]{1,0:T(8,128)(2,1)}, u32[]{:S(2)}, u32[]{:S(2)}) collective-permute-start(bf16[256,896]{1,0:T(8,128)(2,1)} %select_convert_fusion), channel_id=1, source_target_pairs={{0,2},{1,3},{2,0},{3,1},{4,6},{5,7},{6,4},{7,5},{8,10},{9,11},{10,... | collective-permute-start | bytes 1376264 | tf_op jit(solution)/shard_map/ppermute | solution.py:31
  135.5 11.9 %all-to-all-start.3 = ((bf16[16,2,2048]{2,1,0:T(2,128)(2,1)}), bf16[16,2,2048]{2,1,0:T(2,128)(2,1)S(1)}, u32[]{:S(2)}, u32[]{:S(2)}) async-start(bf16[16,2,2048]{2,1,0:T(2,128)(2,1)} %reshape.136), calls=%async_computation.3 | async-start | bytes 262144 | tf_op jit(solution)/shard_map/all_to_all | solution.py:86
  (17 other events, 115.5 us)

commit v2 on v1

v2 whole, which is shorter than its diff:
```python
import jax
import jax.numpy as jnp
from jax import lax
from jax.sharding import PartitionSpec as P

D = 3584
HD = 256
WINDOW = 4096
LINE = 4

soft_cap = 50.0
norm_eps = 1e-06


def after(x, *others):
    return lax.optimization_barrier((x, others))[0]


def swap_core(x):
    peers = lax.axis_size("tp")
    return lax.ppermute(x, "tp", [(i, i ^ 1) for i in range(peers)])


def swap_chip(x):
    peers = lax.axis_size("tp")
    return lax.ppermute(x, "tp", [(i, i ^ 2) for i in range(peers)])


def along(x, by):
    peers = lax.axis_size("seq")
    return lax.ppermute(x, "seq", [(i, i + by) for i in range(peers - by)])


def pairs_in_line(target):
    pairs = []
    for s in range(lax.axis_size("seq")):
        for t in range(lax.axis_size("tp")):
            y, core = target(s % LINE, t % 2)
            pairs.append((s * 4 + t, (s - s % LINE + y) * 4 + (t - t % 2 + core)))
    return pairs


def block_pairs(m):
    return pairs_in_line(lambda y, core: (2 * core + (m ^ (y & 1)), y >> 1))


def head_pairs(a, b):
    return pairs_in_line(lambda y, core: (2 * core + (a ^ (y & 1)), b ^ (y >> 1)))


def move(x, pairs):
    return lax.ppermute(x, ("seq", "tp"), pairs)


def head_of(x, head):
    return lax.dynamic_slice_in_dim(x, head * HD, HD, axis=1)


def regroup(x, low_bit):
    return jnp.concatenate(
        [move(head_of(x, m ^ low_bit), block_pairs(m)) for m in range(2)], axis=0
    )


def weigh(q, k, mask, valid):
    scores = lax.dot_general(
        q, k, (((1,), (1,)), ((), ())), preferred_element_type=jnp.float32
    ) * HD ** (-0.5)
    weights = jnp.exp(soft_cap * jnp.tanh(scores / soft_cap))
    if mask is not None:
        weights = jnp.where(mask, weights, 0.0)
    total = jnp.sum(weights, axis=-1)
    if valid is not None:
        total = jnp.where(valid, total, 0.0)
    return weights.astype(jnp.bfloat16), total


def pick(select, rows):
    return jnp.dot(
        select.astype(jnp.bfloat16), rows, preferred_element_type=jnp.float32
    ).astype(jnp.bfloat16)


def cache_outgoing(key_rows, value_rows, lengths, owners, position):
    rows, width = key_rows.shape
    live = (position * rows + jnp.arange(rows, dtype=jnp.int32) < lengths[0])[:, None]
    both = jnp.concatenate([key_rows, value_rows], axis=1)
    both = jnp.where(live, both, jnp.zeros_like(both))
    y, u = position % LINE, (position // LINE) % 4
    row = jnp.arange(rows, dtype=jnp.int32)
    to_y = y ^ ((row >> 6) & 3)
    to_x = (row >> 5) & 1
    far = (row >> 4) & 1
    to_z = u ^ ((row >> 2) & 3) ^ (3 * far)
    to = to_x * 32 + (far * 4 + to_z) * LINE + to_y
    block = row // (rows // owners.shape[1])
    fits = (owners[0][None, :] == to[:, None])
    number = jnp.arange(owners.shape[1], dtype=jnp.int32)
    wanted = jnp.sum(jnp.where(fits, number[None, :], 0), axis=1)
    return pick((wanted[:, None] == block[None, :]) & ((row & 3)[:, None] == (row & 3)[None, :]), both)


def cut(parts):
    at = parts[0].shape[0] // 2
    return [p[:at] for p in parts], jnp.concatenate([p[at:] for p in parts], axis=0)


def apart(x, count):
    each = x.shape[0] // count
    return [x[n * each : (n + 1) * each] for n in range(count)]


def first_planes(e):
    return [(i, i ^ e) for i in range(16)]


def cache_y1(outgoing):
    kept, given = cut([outgoing])
    return kept + [lax.ppermute(given, "seq", first_planes(2))]


def cache_y0(held):
    kept, given = cut(held)
    return kept + apart(lax.ppermute(given, "seq", first_planes(1)), 2)


def cache_x(held, position):
    kept, given = cut(held)
    got = lax.ppermute(given, "seq", [(i, i + 32) for i in range(16)])
    return jnp.where(position < 32, jnp.concatenate(kept, axis=0), got)


def cache_far(held, position):
    kept, given = cut(apart(held, 4))
    pairs = [
        (x * 32 + z * LINE + y, x * 32 + (7 - z) * LINE + y)
        for x in range(2)
        for z in range(4)
        for y in range(LINE)
    ]
    got = lax.ppermute(given, "seq", pairs)
    return jnp.where((position // LINE) % 8 < 4, jnp.concatenate(kept, axis=0), got)


def cache_w(held, e):
    kept, given = cut(held)
    got = lax.ppermute(given, "seq", [(i, i ^ (e * LINE)) for i in range(64)])
    return kept + apart(got, len(held))


def cache_turn(held):
    row = jnp.arange(64, dtype=jnp.int32)
    take = ((row >> 2) & 3) * 16 + (row >> 4) * 4 + (row & 3)
    return pick(take[:, None] == row[None, :], held)


def cache_sorted(held, position):
    z, y = (position // LINE) % 8, position % LINE
    u = jnp.where(z < 4, z, 7 - z)
    row = jnp.arange(64, dtype=jnp.int32)
    z_from = u ^ (((row >> 5) & 1) | (((row >> 4) & 1) << 1))
    y_from = y ^ (((row >> 3) & 1) | (((row >> 2) & 1) << 1))
    final = (z_from * LINE + y_from) * 4 + (row & 3)
    return pick(row[:, None] == final[None, :], held)


def local(queries, key_rows, value_rows, residual, out_weight, post_scale, lengths, owners):
    rows = queries.shape[1]
    q, k, v = queries[0], key_rows[0], value_rows[0]
    position = lax.axis_index("seq")
    tp = lax.axis_index("tp")
    core = tp % 2
    y = position % LINE
    y0, y1 = y & 1, y >> 1
    plane = position // LINE
    steps = WINDOW // (LINE * rows)

    k_raw = along(k, LINE)
    v_raw = along(v, LINE)
    messages = [(a, b) for a in range(2) for b in range(2)]
    lined = jnp.concatenate(
        [move(head_of(q, 2 * (a ^ y0) + (b ^ y1)), head_pairs(a, b)) for a, b in messages], axis=0
    )
    k_one = regroup(k_raw, y0)
    v_one = regroup(v_raw, y0)
    k_zero = regroup(after(k, k_one), y0)
    v_zero = regroup(after(v, v_one), y0)
    keys, values = [k_zero, k_one], [v_zero, v_one]
    for step in range(2, steps + 1):
        keys.append(along(keys[-1], LINE))
        values.append(along(values[-1], LINE))

    width = out_weight.shape[1] // lax.axis_size("tp")
    weight = after(out_weight, keys[2])
    weights = [
        lax.dynamic_slice_in_dim(weight, t * width, width, axis=1)
        for t in (tp ^ 3, tp ^ 2, tp ^ 1, tp)
    ]
    outgoing = cache_outgoing(k, v, lengths, owners, position)
    with jax.named_scope("cache_y1"):
        held_y1 = cache_y1(after(outgoing, keys[2]))
    with jax.named_scope("cache_y0"):
        held_y0 = cache_y0(held_y1)
    with jax.named_scope("cache_x"):
        held_x = cache_x(held_y0, position)

    offsets = jnp.arange(rows, dtype=jnp.int32)
    q_at = jnp.concatenate([(2 * (b ^ core) + (a ^ y0)) * rows + offsets for a, b in messages])
    k_at = [
        jnp.concatenate([(2 * c + (m ^ y0)) * rows + offsets for m in range(2)])
        for c in (core, 1 - core)
    ]
    numerator = jnp.zeros((LINE * rows, HD), jnp.float32)
    denominator = jnp.zeros((LINE * rows,), jnp.float32)
    for step in range(steps + 1):
        key_sides = (keys[step], swap_core(keys[step]))
        value_sides = (values[step], swap_core(values[step]))
        asked = lined
        if step == 3:
            asked, weights, held_y0 = lax.optimization_barrier((lined, weights, held_y0))
        if step == 4:
            asked = after(lined, held_x)
        for side in range(2):
            mask = None
            if step == 0:
                mask = q_at[:, None] >= k_at[side][None, :]
            if step == steps:
                mask = q_at[:, None] < k_at[side][None, :]
            rounded, total = weigh(
                asked, key_sides[side], mask, None if step == 0 else plane >= step
            )
            numerator = numerator + jnp.dot(
                rounded, value_sides[side], preferred_element_type=jnp.float32
            )
            denominator = denominator + total
    attended = (numerator / denominator[:, None]).astype(jnp.bfloat16)

    returned = {}
    for n, (a, b) in enumerate(messages):
        with jax.named_scope(f"back_{n}"):
            returned[a, b] = move(
                attended[n * rows : (n + 1) * rows],
                [(there, here) for here, there in head_pairs(a, b)],
            )
    with jax.named_scope("cache_far"):
        held_far = cache_far(after(held_x, attended), position)
    by_head = []
    for j in range(2):
        flipped = [jnp.where(y0 == 0, returned[j, b], returned[1 - j, b]) for b in range(2)]
        for b in range(2):
            by_head.append(jnp.where(y1 == 0, flipped[b], flipped[1 - b]))
    mixed = jnp.concatenate(by_head, axis=1)

    def project(w):
        return jnp.dot(mixed, w, preferred_element_type=jnp.float32)

    give_away = swap_core(project(weights[0]).astype(jnp.bfloat16))
    keep_away = project(weights[1])
    give_own = swap_core(project(weights[2]).astype(jnp.bfloat16))
    keep_own = project(weights[3])
    away = (keep_away + give_away.astype(jnp.float32)).astype(jnp.bfloat16)
    with jax.named_scope("across"):
        across = swap_chip(away)
    turned = cache_turn(after(held_far, away))
    with jax.named_scope("cache_w1"):
        held_w1 = cache_w([turned], 2)
    with jax.named_scope("cache_w0"):
        held_w0 = cache_w(held_w1, 1)
    cache = cache_sorted(jnp.concatenate(held_w0, axis=0), position)
    cache_keys, cache_values = cache[:, : k.shape[1]], cache[:, k.shape[1] :]
    branch = (keep_own + give_own.astype(jnp.float32)) + across.astype(jnp.float32)
    squares = jnp.sum(branch * branch, axis=-1)
    squares = squares + swap_core(squares)
    squares = squares + swap_chip(squares)
    normed = branch * lax.rsqrt(squares / D + norm_eps)[:, None] * post_scale
    hidden_out = (residual[0].astype(jnp.float32) + normed).astype(jnp.bfloat16)
    return (hidden_out[None], cache_keys[None], cache_values[None])


def solution(mesh):
    placed = (
        P(None, "seq", "tp"),
        P(None, "seq", "tp"),
        P(None, "seq", "tp"),
        P(None, "seq", "tp"),
        P("tp", None),
        P("tp"),
        P(),
        P(),
    )
    return jax.shard_map(
        local,
        mesh=mesh,
        in_specs=placed,
        out_specs=(P(None, "seq", "tp"), P(None, "seq", "tp"), P(None, "seq", "tp")),
        check_vma=False,
    )
```

time: 154 us -> 145 us (0.942)
  waiting for transfers between devices: 23.7 us -> 39.2 us
  other arithmetic: 11 us -> 2.04 us
  matrix products: 24.1 us -> 17.4 us
  local copies, waits for them, and re-layouts: 8.7 us -> 3.18 us
  starting transfers between devices: 82.5 us -> 78.9 us
    ppermute x3 -> x22, waiting for transfers between devices: 0.01 us -> 28.4 us  [the longest x16 18.2 us: move(): return lax.ppermute(x, ('seq', 'tp'), pairs)]
    ppermute x3 -> x22, starting transfers between devices: 17.9 us -> 43.6 us  [the longest x16 32.5 us: move(): return lax.ppermute(x, ('seq', 'tp'), pairs)]
    all_to_all x4 -> x0, waiting for transfers between devices: 15.5 us -> none  [the longest x3 15.5 us: across_line(): lax.all_to_all(x, 'seq', 0, 0, axis_index_groups=lines('seq'), tiled=True)]
    all_to_all x4 -> x0, starting transfers between devices: 15.3 us -> none  [the longest x3 11.8 us: across_line(): lax.all_to_all(x, 'seq', 0, 0, axis_index_groups=lines('seq'), tiled=True)]
    ppermute x16 -> x13, starting transfers between devices: 17 us -> 7.44 us  [swap_core(): return lax.ppermute(x, 'tp', [(i, i ^ 1) for i in range(peers)])]
    dot_general x24 -> x27, matrix products: 24.1 us -> 17.4 us  [the longest x10 7.83 us: weigh(): lax.dot_general(q, k, (((1,), (1,)), ((), ())), preferred_element_type=jn...]
    unnamed x24 -> x21, local copies, waits for them, and re-layouts: 3.27 us -> 0.11 us
    ppermute x8, starting transfers between devices: 29.8 us -> 27.2 us  [along(): return lax.ppermute(x, 'seq', [(i, i + by) for i in range(peers - by)])]
  transfers between devices with their start and end apart: 33 -> 45, of which waited for: 6 -> 16; matrix products, arithmetic and copies ran while one was open for 20% -> 14% of each run, Pallas kernels for 0% -> 0%
where the time goes in v2:
time: 145 us; the launch traced here: 143 us
  starting transfers between devices  78.9 us (54%)
  waiting for transfers between devices  39.2 us (27%)
  matrix products  17.4 us (12%)
  local copies, waits for them, and re-layouts  3.18 us (2%)
  between operations  2.46 us (2%)
  other arithmetic  2.04 us (1%)
    ppermute x16, starting transfers between devices, move(): return lax.ppermute(x, ('seq', 'tp'), pairs)  32.5 us
    ppermute x8, starting transfers between devices, along(): return lax.ppermute(x, 'seq', [(i, i + by) for i in range(peers - by)])  27.2 us
    ppermute x16, waiting for transfers between devices, move(): return lax.ppermute(x, ('seq', 'tp'), pairs)  18.2 us
    ppermute x2, waiting for transfers between devices, swap_chip(): return lax.ppermute(x, 'tp', [(i, i ^ 2) for i in range(peers)])  8.58 us
    dot_general x10, matrix products, weigh(): lax.dot_general(q, k, (((1,), (1,)), ((), ())), preferred_element_type=jn...  7.83 us
    ppermute x13, starting transfers between devices, swap_core(): return lax.ppermute(x, 'tp', [(i, i ^ 1) for i in range(peers)])  7.44 us
    ppermute x1, waiting for transfers between devices, cache_x(): got = lax.ppermute(given, 'seq', [(i, i + 32) for i in range(16)])  6.28 us
    dot_general x10, matrix products, local(): jnp.dot(rounded, value_sides[side], preferred_element_type=jnp.float32)  4.77 us
  transfers between devices with their start and end apart: 45, of which 16 were waited for; matrix products, arithmetic and copies ran while one was open for 14% of the time, Pallas kernels for 0%

profile of v2, /device:TPU:1, one launch (start us, length us, event | category | flops | bytes accessed | tf_op | source)
XLA Modules:
  0.0 143.3 jit_solution(16648081862889651320)
XLA Ops:
  0.6 4.4 %collective-permute-start.4 = (bf16[256,512]{1,0:T(8,128)(2,1)}, bf16[256,512]{1,0:T(8,128)(2,1)S(1)}, u32[]{:S(2)}, u32[]{:S(2)}) collective-permute-start(bf16[256,512]{1,0:T(8,128)(2,1)} %bitcast.69), channel_id=1, source_target_pairs={{0,16},{4,20},{8,24},{12,28},{16,32},{20,36},{24,40},{28,44},{32,4... | collective-permute-start | bytes 786440 | tf_op jit(solution)/shard_map/ppermute | solution.py:31
  5.0 3.5 %collective-permute-start.9 = (bf16[256,512]{1,0:T(8,128)(2,1)}, bf16[256,512]{1,0:T(8,128)(2,1)S(1)}, u32[]{:S(2)}, u32[]{:S(2)}) collective-permute-start(bf16[256,512]{1,0:T(8,128)(2,1)} %bitcast.72), channel_id=1, source_target_pairs={{0,16},{4,20},{8,24},{12,28},{16,32},{20,36},{24,40},{28,44},{32,4... | collective-permute-start | bytes 786440 | tf_op jit(solution)/shard_map/ppermute | solution.py:31
  9.8 2.8 %collective-permute-start.3 = (bf16[256,256]{1,0:T(8,128)(2,1)S(1)}, bf16[256,256]{1,0:T(8,128)(2,1)S(1)}, u32[]{:S(2)}, u32[]{:S(2)}) collective-permute-start(bf16[256,256]{1,0:T(8,128)(2,1)S(1)} %get-tuple-element.41), channel_id=1, source_target_pairs={{0,5},{1,13},{2,7},{3,15},{4,1},{5,9},{6,3},{7,11},{8,4},{9,12},{1... | collective-permute-start | bytes 393224 | tf_op jit(solution)/shard_map/ppermute | solution.py:52
  12.6 2.3 %collective-permute-start.1 = (bf16[256,256]{1,0:T(8,128)(2,1)S(1)}, bf16[256,256]{1,0:T(8,128)(2,1)S(1)}, u32[]{:S(2)}, u32[]{:S(2)}) collective-permute-start(bf16[256,256]{1,0:T(8,128)(2,1)S(1)} %get-tuple-element.42), channel_id=1, source_target_pairs={{0,1},{1,9},{2,3},{3,11},{4,5},{5,13},{6,7},{7,15},{8,0},{9,8},{10... | collective-permute-start | bytes 393224 | tf_op jit(solution)/shard_map/ppermute | solution.py:52
  20.0 3.1 %collective-permute-done = bf16[256,256]{1,0:T(8,128)(2,1)S(1)} collective-permute-done((bf16[256,256]{1,0:T(8,128)(2,1)S(1)}, bf16[256,256]{1,0:T(8,128)(2,1)S(1)}, u32[]{:S(2)}, u32[]{:S(2)}) %collective-permute-start) | collective-permute-done | bytes 131104 | tf_op jit(solution)/shard_map/ppermute | solution.py:52
  23.1 5.6 %collective-permute-done.2 = bf16[256,256]{1,0:T(8,128)(2,1)S(1)} collective-permute-done((bf16[256,256]{1,0:T(8,128)(2,1)S(1)}, bf16[256,256]{1,0:T(8,128)(2,1)S(1)}, u32[]{:S(2)}, u32[]{:S(2)}) %collective-permute-start.2) | collective-permute-done | bytes 131104 | tf_op jit(solution)/shard_map/ppermute | solution.py:52
  33.9 3.9 %collective-permute-start.10 = (bf16[256,256]{1,0:T(8,128)(2,1)S(1)}, bf16[256,256]{1,0:T(8,128)(2,1)S(1)}, u32[]{:S(2)}, u32[]{:S(2)}) collective-permute-start(bf16[256,256]{1,0:T(8,128)(2,1)S(1)} %get-tuple-element.64), channel_id=1, source_target_pairs={{0,0},{1,8},{2,2},{3,10},{4,4},{5,12},{6,6},{7,14},{8,1},{9,9},{10... | collective-permute-start | bytes 393224 | tf_op jit(solution)/shard_map/ppermute | solution.py:52
  37.8 3.5 %collective-permute-start.18 = (bf16[512,256]{1,0:T(8,128)(2,1)S(1)}, bf16[512,256]{1,0:T(8,128)(2,1)S(1)}, u32[]{:S(2)}, u32[]{:S(2)}) collective-permute-start(bf16[512,256]{1,0:T(8,128)(2,1)S(1)} %constant_dynamic-update-slice_fusion.4), channel_id=1, source_target_pairs={{0,16},{4,20},{8,24},{12,28},{16,32},{20,36},{24,40},{28,44},{32,4... | collective-permute-start | bytes 786440 | tf_op jit(solution)/shard_map/ppermute | solution.py:31
  41.7 4.9 %collective-permute-start.19 = (bf16[512,256]{1,0:T(8,128)(2,1)S(1)}, bf16[512,256]{1,0:T(8,128)(2,1)S(1)}, u32[]{:S(2)}, u32[]{:S(2)}) collective-permute-start(bf16[512,256]{1,0:T(8,128)(2,1)S(1)} %constant_dynamic-update-slice_fusion.8), channel_id=1, source_target_pairs={{0,16},{4,20},{8,24},{12,28},{16,32},{20,36},{24,40},{28,44},{32,4... | collective-permute-start | bytes 786440 | tf_op jit(solution)/shard_map/ppermute | solution.py:31
  46.6 3.7 %collective-permute-start.7 = (bf16[256,256]{1,0:T(8,128)(2,1)S(1)}, bf16[256,256]{1,0:T(8,128)(2,1)S(1)}, u32[]{:S(2)}, u32[]{:S(2)}) collective-permute-start(bf16[256,256]{1,0:T(8,128)(2,1)S(1)} %get-tuple-element.54), channel_id=1, source_target_pairs={{0,0},{1,8},{2,2},{3,10},{4,4},{5,12},{6,6},{7,14},{8,1},{9,9},{10... | collective-permute-start | bytes 393224 | tf_op jit(solution)/shard_map/ppermute | solution.py:52
  50.4 3.4 %collective-permute-start.12 = (bf16[256,256]{1,0:T(8,128)(2,1)S(1)}, bf16[256,256]{1,0:T(8,128)(2,1)S(1)}, u32[]{:S(2)}, u32[]{:S(2)}) collective-permute-start(bf16[256,256]{1,0:T(8,128)(2,1)S(1)} %get-tuple-element.56), channel_id=1, source_target_pairs={{0,0},{1,8},{2,2},{3,10},{4,4},{5,12},{6,6},{7,14},{8,1},{9,9},{10... | collective-permute-start | bytes 393224 | tf_op jit(solution)/shard_map/ppermute | solution.py:52
  61.5 2.4 %collective-permute-done.13 = bf16[256,256]{1,0:T(8,128)(2,1)S(1)} collective-permute-done((bf16[256,256]{1,0:T(8,128)(2,1)S(1)}, bf16[256,256]{1,0:T(8,128)(2,1)S(1)}, u32[]{:S(2)}, u32[]{:S(2)}) %collective-permute-start.13) | collective-permute-done | bytes 131104 | tf_op jit(solution)/shard_map/ppermute | solution.py:52
  66.7 2.8 %collective-permute-start.26 = (bf16[128,1024]{1,0:T(8,128)(2,1)S(1)}, bf16[128,1024]{1,0:T(8,128)(2,1)S(1)}, u32[]{:S(2)}, u32[]{:S(2)}) collective-permute-start(bf16[128,1024]{1,0:T(8,128)(2,1)S(1)} %slice.124), channel_id=1, source_target_pairs={{0,8},{4,12},{8,0},{12,4},{16,24},{20,28},{24,16},{28,20},{32,40},... | collective-permute-start | bytes 786440 | tf_op jit(solution)/shard_map/cache_y1/ppermute | solution.py:119
  70.0 3.6 %collective-permute-start.22 = (bf16[512,256]{1,0:T(8,128)(2,1)S(1)}, bf16[512,256]{1,0:T(8,128)(2,1)S(1)}, u32[]{:S(2)}, u32[]{:S(2)}) collective-permute-start(bf16[512,256]{1,0:T(8,128)(2,1)S(1)} %collective-permute-done.18), channel_id=1, source_target_pairs={{0,16},{4,20},{8,24},{12,28},{16,32},{20,36},{24,40},{28,44},{32,4... | collective-permute-start | bytes 786440 | tf_op jit(solution)/shard_map/ppermute | solution.py:31
  76.0 2.6 %collective-permute-start.23 = (bf16[512,256]{1,0:T(8,128)(2,1)S(1)}, bf16[512,256]{1,0:T(8,128)(2,1)S(1)}, u32[]{:S(2)}, u32[]{:S(2)}) collective-permute-start(bf16[512,256]{1,0:T(8,128)(2,1)S(1)} %collective-permute-done.19), channel_id=1, source_target_pairs={{0,16},{4,20},{8,24},{12,28},{16,32},{20,36},{24,40},{28,44},{32,4... | collective-permute-start | bytes 786440 | tf_op jit(solution)/shard_map/ppermute | solution.py:31
  81.3 3.9 %collective-permute-start.27 = (bf16[128,1024]{1,0:T(8,128)(2,1)S(1)}, bf16[128,1024]{1,0:T(8,128)(2,1)S(1)}, u32[]{:S(2)}, u32[]{:S(2)}) collective-permute-start(bf16[128,1024]{1,0:T(8,128)(2,1)S(1)} %pad_maximum_fusion.1), channel_id=1, source_target_pairs={{0,4},{4,0},{8,12},{12,8},{16,20},{20,16},{24,28},{28,24},{32,36},... | collective-permute-start | bytes 786440 | tf_op jit(solution)/shard_map/cache_y0/ppermute | solution.py:124
  85.2 2.6 %collective-permute-start.29 = (bf16[512,256]{1,0:T(8,128)(2,1)S(1)}, bf16[512,256]{1,0:T(8,128)(2,1)S(1)}, u32[]{:S(2)}, u32[]{:S(2)}) collective-permute-start(bf16[512,256]{1,0:T(8,128)(2,1)S(1)} %collective-permute-done.22), channel_id=1, source_target_pairs={{0,16},{4,20},{8,24},{12,28},{16,32},{20,36},{24,40},{28,44},{32,4... | collective-permute-start | bytes 786440 | tf_op jit(solution)/shard_map/ppermute | solution.py:31
  93.6 3.0 %collective-permute-start.28 = (bf16[128,1024]{1,0:T(8,128)(2,1)S(1)}, bf16[128,1024]{1,0:T(8,128)(2,1)S(1)}, u32[]{:S(2)}, u32[]{:S(2)}) collective-permute-start(bf16[128,1024]{1,0:T(8,128)(2,1)S(1)} %pad_maximum_fusion.2), channel_id=1, source_target_pairs={{0,128},{4,132},{8,136},{12,140},{16,144},{20,148},{24,152},{28,15... | collective-permute-start | bytes 786440 | tf_op jit(solution)/shard_map/cache_x/ppermute | solution.py:129
  100.7 6.3 %collective-permute-done.28 = bf16[128,1024]{1,0:T(8,128)(2,1)S(1)} collective-permute-done((bf16[128,1024]{1,0:T(8,128)(2,1)S(1)}, bf16[128,1024]{1,0:T(8,128)(2,1)S(1)}, u32[]{:S(2)}, u32[]{:S(2)}) %collective-permute-start.28) | collective-permute-done | bytes 262176 | tf_op jit(solution)/shard_map/cache_x/ppermute | solution.py:129
  110.8 2.7 %collective-permute-start.36 = (bf16[256,256]{1,0:T(8,128)(2,1)S(1)}, bf16[256,256]{1,0:T(8,128)(2,1)S(1)}, u32[]{:S(2)}, u32[]{:S(2)}) collective-permute-start(bf16[256,256]{1,0:T(8,128)(2,1)S(1)} %get-tuple-element.36), channel_id=1, source_target_pairs={{5,0},{13,1},{7,2},{15,3},{1,4},{9,5},{3,6},{11,7},{4,8},{12,9},{6... | collective-permute-start | bytes 393224 | tf_op jit(solution)/shard_map/back_3/ppermute | solution.py:52
  113.9 3.1 %collective-permute-start.33 = (bf16[256,256]{1,0:T(8,128)(2,1)S(1)}, bf16[256,256]{1,0:T(8,128)(2,1)S(1)}, u32[]{:S(2)}, u32[]{:S(2)}) collective-permute-start(bf16[256,256]{1,0:T(8,128)(2,1)S(1)} %get-tuple-element.38), channel_id=1, source_target_pairs={{0,0},{8,1},{2,2},{10,3},{4,4},{12,5},{6,6},{14,7},{1,8},{9,9},{3,... | collective-permute-start | bytes 393224 | tf_op jit(solution)/shard_map/back_0/ppermute | solution.py:52
  119.2 2.5 %collective-permute-done.33 = bf16[256,256]{1,0:T(8,128)(2,1)S(1)} collective-permute-done((bf16[256,256]{1,0:T(8,128)(2,1)S(1)}, bf16[256,256]{1,0:T(8,128)(2,1)S(1)}, u32[]{:S(2)}, u32[]{:S(2)}) %collective-permute-start.33) | collective-permute-done | bytes 131104 | tf_op jit(solution)/shard_map/back_0/ppermute | solution.py:52
  125.8 4.0 %collective-permute-done.43 = bf16[32,1024]{1,0:T(8,128)(2,1)S(1)} collective-permute-done((bf16[32,1024]{1,0:T(8,128)(2,1)S(1)}, bf16[32,1024]{1,0:T(8,128)(2,1)S(1)}, u32[]{:S(2)}, u32[]{:S(2)}) %collective-permute-start.43) | collective-permute-done | bytes 65568 | tf_op jit(solution)/shard_map/cache_w1/ppermute | solution.py:147
  130.0 7.1 %collective-permute-done.39 = bf16[256,896]{1,0:T(8,128)(2,1)S(1)} collective-permute-done((bf16[256,896]{1,0:T(8,128)(2,1)S(1)}, bf16[256,896]{1,0:T(8,128)(2,1)S(1)}, u32[]{:S(2)}, u32[]{:S(2)}) %collective-permute-start.39) | collective-permute-done | bytes 458784 | tf_op jit(solution)/shard_map/across/ppermute | solution.py:26
  (162 shorter events, 53.0 us)
Async XLA Ops:
  0.6 28.1 %collective-permute-start.4 = (bf16[256,512]{1,0:T(8,128)(2,1)}, bf16[256,512]{1,0:T(8,128)(2,1)S(1)}, u32[]{:S(2)}, u32[]{:S(2)}) collective-permute-start(bf16[256,512]{1,0:T(8,128)(2,1)} %bitcast.69), channel_id=1, source_target_pairs={{0,16},{4,20},{8,24},{12,28},{16,32},{20,36},{24,40},{28,44},{32,4... | collective-permute-start | bytes 786440 | tf_op jit(solution)/shard_map/ppermute | solution.py:31
  5.0 27.9 %collective-permute-start.9 = (bf16[256,512]{1,0:T(8,128)(2,1)}, bf16[256,512]{1,0:T(8,128)(2,1)S(1)}, u32[]{:S(2)}, u32[]{:S(2)}) collective-permute-start(bf16[256,512]{1,0:T(8,128)(2,1)} %bitcast.72), channel_id=1, source_target_pairs={{0,16},{4,20},{8,24},{12,28},{16,32},{20,36},{24,40},{28,44},{32,4... | collective-permute-start | bytes 786440 | tf_op jit(solution)/shard_map/ppermute | solution.py:31
  9.8 20.9 %collective-permute-start.3 = (bf16[256,256]{1,0:T(8,128)(2,1)S(1)}, bf16[256,256]{1,0:T(8,128)(2,1)S(1)}, u32[]{:S(2)}, u32[]{:S(2)}) collective-permute-start(bf16[256,256]{1,0:T(8,128)(2,1)S(1)} %get-tuple-element.41), channel_id=1, source_target_pairs={{0,5},{1,13},{2,7},{3,15},{4,1},{5,9},{6,3},{7,11},{8,4},{9,12},{1... | collective-permute-start | bytes 393224 | tf_op jit(solution)/shard_map/ppermute | solution.py:52
  12.6 10.5 %collective-permute-start.1 = (bf16[256,256]{1,0:T(8,128)(2,1)S(1)}, bf16[256,256]{1,0:T(8,128)(2,1)S(1)}, u32[]{:S(2)}, u32[]{:S(2)}) collective-permute-start(bf16[256,256]{1,0:T(8,128)(2,1)S(1)} %get-tuple-element.42), channel_id=1, source_target_pairs={{0,1},{1,9},{2,3},{3,11},{4,5},{5,13},{6,7},{7,15},{8,0},{9,8},{10... | collective-permute-start | bytes 393224 | tf_op jit(solution)/shard_map/ppermute | solution.py:52
  37.8 26.8 %collective-permute-start.18 = (bf16[512,256]{1,0:T(8,128)(2,1)S(1)}, bf16[512,256]{1,0:T(8,128)(2,1)S(1)}, u32[]{:S(2)}, u32[]{:S(2)}) collective-permute-start(bf16[512,256]{1,0:T(8,128)(2,1)S(1)} %constant_dynamic-update-slice_fusion.4), channel_id=1, source_target_pairs={{0,16},{4,20},{8,24},{12,28},{16,32},{20,36},{24,40},{28,44},{32,4... | collective-permute-start | bytes 786440 | tf_op jit(solution)/shard_map/ppermute | solution.py:31
  41.4 28.6 %collective-permute-start.16 = (bf16[512,256]{1,0:T(8,128)(2,1)S(1)}, bf16[512,256]{1,0:T(8,128)(2,1)S(1)}, u32[]{:S(2)}, u32[]{:S(2)}) collective-permute-start(bf16[512,256]{1,0:T(8,128)(2,1)S(1)} %constant_dynamic-update-slice_fusion.4), channel_id=1, source_target_pairs={{0,1},{1,0},{2,3},{3,2},{4,5},{5,4},{6,7},{7,6},{8,9},{9,8},{10,11... | collective-permute-start | bytes 786440 | tf_op jit(solution)/shard_map/ppermute | solution.py:21
  41.7 25.0 %collective-permute-start.19 = (bf16[512,256]{1,0:T(8,128)(2,1)S(1)}, bf16[512,256]{1,0:T(8,128)(2,1)S(1)}, u32[]{:S(2)}, u32[]{:S(2)}) collective-permute-start(bf16[512,256]{1,0:T(8,128)(2,1)S(1)} %constant_dynamic-update-slice_fusion.8), channel_id=1, source_target_pairs={{0,16},{4,20},{8,24},{12,28},{16,32},{20,36},{24,40},{28,44},{32,4... | collective-permute-start | bytes 786440 | tf_op jit(solution)/shard_map/ppermute | solution.py:31
  46.6 9.2 %collective-permute-start.7 = (bf16[256,256]{1,0:T(8,128)(2,1)S(1)}, bf16[256,256]{1,0:T(8,128)(2,1)S(1)}, u32[]{:S(2)}, u32[]{:S(2)}) collective-permute-start(bf16[256,256]{1,0:T(8,128)(2,1)S(1)} %get-tuple-element.54), channel_id=1, source_target_pairs={{0,0},{1,8},{2,2},{3,10},{4,4},{5,12},{6,6},{7,14},{8,1},{9,9},{10... | collective-permute-start | bytes 393224 | tf_op jit(solution)/shard_map/ppermute | solution.py:52
  61.4 12.9 %collective-permute-start.17 = (bf16[512,256]{1,0:T(8,128)(2,1)S(1)}, bf16[512,256]{1,0:T(8,128)(2,1)S(1)}, u32[]{:S(2)}, u32[]{:S(2)}) collective-permute-start(bf16[512,256]{1,0:T(8,128)(2,1)S(1)} %constant_dynamic-update-slice_fusion.8), channel_id=1, source_target_pairs={{0,1},{1,0},{2,3},{3,2},{4,5},{5,4},{6,7},{7,6},{8,9},{9,8},{10,11... | collective-permute-start | bytes 786440 | tf_op jit(solution)/shard_map/ppermute | solution.py:21
  63.8 12.2 %collective-permute-start.14 = (bf16[512,256]{1,0:T(8,128)(2,1)S(1)}, bf16[512,256]{1,0:T(8,128)(2,1)S(1)}, u32[]{:S(2)}, u32[]{:S(2)}) collective-permute-start(bf16[512,256]{1,0:T(8,128)(2,1)S(1)} %constant_dynamic-update-slice_fusion.6), channel_id=1, source_target_pairs={{0,1},{1,0},{2,3},{3,2},{4,5},{5,4},{6,7},{7,6},{8,9},{9,8},{10,11... | collective-permute-start | bytes 786440 | tf_op jit(solution)/shard_map/ppermute | solution.py:21
  64.7 14.8 %collective-permute-start.15 = (bf16[512,256]{1,0:T(8,128)(2,1)S(1)}, bf16[512,256]{1,0:T(8,128)(2,1)S(1)}, u32[]{:S(2)}, u32[]{:S(2)}) collective-permute-start(bf16[512,256]{1,0:T(8,128)(2,1)S(1)} %constant_dynamic-update-slice_fusion.10), channel_id=1, source_target_pairs={{0,1},{1,0},{2,3},{3,2},{4,5},{5,4},{6,7},{7,6},{8,9},{9,8},{10,11... | collective-permute-start | bytes 786440 | tf_op jit(solution)/shard_map/ppermute | solution.py:21
  66.7 14.1 %collective-permute-start.26 = (bf16[128,1024]{1,0:T(8,128)(2,1)S(1)}, bf16[128,1024]{1,0:T(8,128)(2,1)S(1)}, u32[]{:S(2)}, u32[]{:S(2)}) collective-permute-start(bf16[128,1024]{1,0:T(8,128)(2,1)S(1)} %slice.124), channel_id=1, source_target_pairs={{0,8},{4,12},{8,0},{12,4},{16,24},{20,28},{24,16},{28,20},{32,40},... | collective-permute-start | bytes 786440 | tf_op jit(solution)/shard_map/cache_y1/ppermute | solution.py:119
  70.0 15.2 %collective-permute-start.22 = (bf16[512,256]{1,0:T(8,128)(2,1)S(1)}, bf16[512,256]{1,0:T(8,128)(2,1)S(1)}, u32[]{:S(2)}, u32[]{:S(2)}) collective-permute-start(bf16[512,256]{1,0:T(8,128)(2,1)S(1)} %collective-permute-done.18), channel_id=1, source_target_pairs={{0,16},{4,20},{8,24},{12,28},{16,32},{20,36},{24,40},{28,44},{32,4... | collective-permute-start | bytes 786440 | tf_op jit(solution)/shard_map/ppermute | solution.py:31
  74.4 15.6 %collective-permute-start.20 = (bf16[512,256]{1,0:T(8,128)(2,1)S(1)}, bf16[512,256]{1,0:T(8,128)(2,1)S(1)}, u32[]{:S(2)}, u32[]{:S(2)}) collective-permute-start(bf16[512,256]{1,0:T(8,128)(2,1)S(1)} %collective-permute-done.18), channel_id=1, source_target_pairs={{0,1},{1,0},{2,3},{3,2},{4,5},{5,4},{6,7},{7,6},{8,9},{9,8},{10,11... | collective-permute-start | bytes 786440 | tf_op jit(solution)/shard_map/ppermute | solution.py:21
  76.0 12.6 %collective-permute-start.23 = (bf16[512,256]{1,0:T(8,128)(2,1)S(1)}, bf16[512,256]{1,0:T(8,128)(2,1)S(1)}, u32[]{:S(2)}, u32[]{:S(2)}) collective-permute-start(bf16[512,256]{1,0:T(8,128)(2,1)S(1)} %collective-permute-done.19), channel_id=1, source_target_pairs={{0,16},{4,20},{8,24},{12,28},{16,32},{20,36},{24,40},{28,44},{32,4... | collective-permute-start | bytes 786440 | tf_op jit(solution)/shard_map/ppermute | solution.py:31
  79.5 13.2 %collective-permute-start.21 = (bf16[512,256]{1,0:T(8,128)(2,1)S(1)}, bf16[512,256]{1,0:T(8,128)(2,1)S(1)}, u32[]{:S(2)}, u32[]{:S(2)}) collective-permute-start(bf16[512,256]{1,0:T(8,128)(2,1)S(1)} %collective-permute-done.19), channel_id=1, source_target_pairs={{0,1},{1,0},{2,3},{3,2},{4,5},{5,4},{6,7},{7,6},{8,9},{9,8},{10,11... | collective-permute-start | bytes 786440 | tf_op jit(solution)/shard_map/ppermute | solution.py:21
  81.3 12.3 %collective-permute-start.27 = (bf16[128,1024]{1,0:T(8,128)(2,1)S(1)}, bf16[128,1024]{1,0:T(8,128)(2,1)S(1)}, u32[]{:S(2)}, u32[]{:S(2)}) collective-permute-start(bf16[128,1024]{1,0:T(8,128)(2,1)S(1)} %pad_maximum_fusion.1), channel_id=1, source_target_pairs={{0,4},{4,0},{8,12},{12,8},{16,20},{20,16},{24,28},{28,24},{32,36},... | collective-permute-start | bytes 786440 | tf_op jit(solution)/shard_map/cache_y0/ppermute | solution.py:124
  85.2 11.5 %collective-permute-start.29 = (bf16[512,256]{1,0:T(8,128)(2,1)S(1)}, bf16[512,256]{1,0:T(8,128)(2,1)S(1)}, u32[]{:S(2)}, u32[]{:S(2)}) collective-permute-start(bf16[512,256]{1,0:T(8,128)(2,1)S(1)} %collective-permute-done.22), channel_id=1, source_target_pairs={{0,16},{4,20},{8,24},{12,28},{16,32},{20,36},{24,40},{28,44},{32,4... | collective-permute-start | bytes 786440 | tf_op jit(solution)/shard_map/ppermute | solution.py:31
  88.6 11.3 %collective-permute-start.24 = (bf16[512,256]{1,0:T(8,128)(2,1)S(1)}, bf16[512,256]{1,0:T(8,128)(2,1)S(1)}, u32[]{:S(2)}, u32[]{:S(2)}) collective-permute-start(bf16[512,256]{1,0:T(8,128)(2,1)S(1)} %collective-permute-done.22), channel_id=1, source_target_pairs={{0,1},{1,0},{2,3},{3,2},{4,5},{5,4},{6,7},{7,6},{8,9},{9,8},{10,11... | collective-permute-start | bytes 786440 | tf_op jit(solution)/shard_map/ppermute | solution.py:21
  92.7 15.7 %collective-permute-start.25 = (bf16[512,256]{1,0:T(8,128)(2,1)S(1)}, bf16[512,256]{1,0:T(8,128)(2,1)S(1)}, u32[]{:S(2)}, u32[]{:S(2)}) collective-permute-start(bf16[512,256]{1,0:T(8,128)(2,1)S(1)} %collective-permute-done.23), channel_id=1, source_target_pairs={{0,1},{1,0},{2,3},{3,2},{4,5},{5,4},{6,7},{7,6},{8,9},{9,8},{10,11... | collective-permute-start | bytes 786440 | tf_op jit(solution)/shard_map/ppermute | solution.py:21
  93.6 13.4 %collective-permute-start.28 = (bf16[128,1024]{1,0:T(8,128)(2,1)S(1)}, bf16[128,1024]{1,0:T(8,128)(2,1)S(1)}, u32[]{:S(2)}, u32[]{:S(2)}) collective-permute-start(bf16[128,1024]{1,0:T(8,128)(2,1)S(1)} %pad_maximum_fusion.2), channel_id=1, source_target_pairs={{0,128},{4,132},{8,136},{12,140},{16,144},{20,148},{24,152},{28,15... | collective-permute-start | bytes 786440 | tf_op jit(solution)/shard_map/cache_x/ppermute | solution.py:129
  96.7 12.2 %collective-permute-start.31 = (bf16[512,256]{1,0:T(8,128)(2,1)S(1)}, bf16[512,256]{1,0:T(8,128)(2,1)S(1)}, u32[]{:S(2)}, u32[]{:S(2)}) collective-permute-start(bf16[512,256]{1,0:T(8,128)(2,1)S(1)} %collective-permute-done.29), channel_id=1, source_target_pairs={{0,1},{1,0},{2,3},{3,2},{4,5},{5,4},{6,7},{7,6},{8,9},{9,8},{10,11... | collective-permute-start | bytes 786440 | tf_op jit(solution)/shard_map/ppermute | solution.py:21
  98.6 11.1 %collective-permute-start.32 = (bf16[512,256]{1,0:T(8,128)(2,1)S(1)}, bf16[512,256]{1,0:T(8,128)(2,1)S(1)}, u32[]{:S(2)}, u32[]{:S(2)}) collective-permute-start(bf16[512,256]{1,0:T(8,128)(2,1)S(1)} %collective-permute-done.30), channel_id=1, source_target_pairs={{0,1},{1,0},{2,3},{3,2},{4,5},{5,4},{6,7},{7,6},{8,9},{9,8},{10,11... | collective-permute-start | bytes 786440 | tf_op jit(solution)/shard_map/ppermute | solution.py:21
  125.1 12.0 %collective-permute-start.39 = (bf16[256,896]{1,0:T(8,128)(2,1)S(1)}, bf16[256,896]{1,0:T(8,128)(2,1)S(1)}, u32[]{:S(2)}, u32[]{:S(2)}) collective-permute-start(bf16[256,896]{1,0:T(8,128)(2,1)S(1)} %fusion.8), channel_id=1, source_target_pairs={{0,2},{1,3},{2,0},{3,1},{4,6},{5,7},{6,4},{7,5},{8,10},{9,11},{10,... | collective-permute-start | bytes 1376264 | tf_op jit(solution)/shard_map/across/ppermute | solution.py:26
  (29 other events, 300.5 us)

commit v3 on v2

--- a/solution.py
+++ b/solution.py
@@ -2,6 +2,7 @@
 import jax.numpy as jnp
 from jax import lax
 from jax.sharding import PartitionSpec as P
+
 
 D = 3584
 HD = 256
@@ -57,9 +58,7 @@
 
 
 def regroup(x, low_bit):
-    return jnp.concatenate(
-        [move(head_of(x, m ^ low_bit), block_pairs(m)) for m in range(2)], axis=0
-    )
+    return [move(head_of(x, m ^ low_bit), block_pairs(m)) for m in range(2)]
 
 
 def weigh(q, k, mask, valid):
@@ -82,14 +81,14 @@
 
 
 def cache_outgoing(key_rows, value_rows, lengths, owners, position):
-    rows, width = key_rows.shape
+    rows, _ = key_rows.shape
     live = (position * rows + jnp.arange(rows, dtype=jnp.int32) < lengths[0])[:, None]
     both = jnp.concatenate([key_rows, value_rows], axis=1)
     both = jnp.where(live, both, jnp.zeros_like(both))
     y, u = position % LINE, (position // LINE) % 4
     row = jnp.arange(rows, dtype=jnp.int32)
-    to_y = y ^ ((row >> 6) & 3)
-    to_x = (row >> 5) & 1
+    to_x = (row >> 7) & 1
+    to_y = y ^ ((row >> 5) & 3)
     far = (row >> 4) & 1
     to_z = u ^ ((row >> 2) & 3) ^ (3 * far)
     to = to_x * 32 + (far * 4 + to_z) * LINE + to_y
@@ -111,11 +110,17 @@
 
 
 def first_planes(e):
-    return [(i, i ^ e) for i in range(16)]
-
-
-def cache_y1(outgoing):
+    return [(x + i, x + (i ^ e)) for x in (0, 32) for i in range(16)]
+
+
+def cache_x(outgoing, position):
     kept, given = cut([outgoing])
+    got = lax.ppermute(given, "seq", [(i, i + 32) for i in range(16)])
+    return jnp.where(position < 32, kept[0], got)
+
+
+def cache_y1(held):
+    kept, given = cut([held])
     return kept + [lax.ppermute(given, "seq", first_planes(2))]
 
 
@@ -124,14 +129,8 @@
     return kept + apart(lax.ppermute(given, "seq", first_planes(1)), 2)
 
 
-def cache_x(held, position):
+def cache_far(held, position):
     kept, given = cut(held)
-    got = lax.ppermute(given, "seq", [(i, i + 32) for i in range(16)])
-    return jnp.where(position < 32, jnp.concatenate(kept, axis=0), got)
-
-
-def cache_far(held, position):
-    kept, given = cut(apart(held, 4))
     pairs = [
         (x * 32 + z * LINE + y, x * 32 + (7 - z) * LINE + y)
         for x in range(2)
@@ -164,7 +163,7 @@
     return pick(row[:, None] == final[None, :], held)
 
 
-def local(queries, key_rows, value_rows, residual, out_weight, post_scale, lengths, owners):
+def layer(queries, key_rows, value_rows, residual, out_weight, post_scale, lengths, owners):
     rows = queries.shape[1]
     q, k, v = queries[0], key_rows[0], value_rows[0]
     position = lax.axis_index("seq")
@@ -177,32 +176,34 @@
 
     k_raw = along(k, LINE)
     v_raw = along(v, LINE)
-    messages = [(a, b) for a in range(2) for b in range(2)]
-    lined = jnp.concatenate(
-        [move(head_of(q, 2 * (a ^ y0) + (b ^ y1)), head_pairs(a, b)) for a, b in messages], axis=0
+    messages = [(a, b) for b in range(2) for a in range(2)]
+    asked_for = [head_of(q, 2 * (a ^ y0) + (b ^ y1)) for a, b in messages]
+    stored = regroup(k_raw, y0) + regroup(v_raw, y0)
+    chunks = [None, jnp.concatenate(stored, axis=0)]
+    for _ in range(2, steps + 1):
+        chunks.append(along(chunks[-1], LINE))
+    lined = []
+    for n, (a, b) in enumerate(messages):
+        columns = [asked_for[n]]
+        if b == 0:
+            columns += [head_of(k, a ^ y0), head_of(v, a ^ y0)]
+        got = move(jnp.concatenate(columns, axis=1), head_pairs(a, b))
+        lined.append(got)
+    chunks[0] = jnp.concatenate(
+        [got[:, at : at + HD] for at in (HD, 2 * HD) for got in lined[:2]], axis=0
     )
-    k_one = regroup(k_raw, y0)
-    v_one = regroup(v_raw, y0)
-    k_zero = regroup(after(k, k_one), y0)
-    v_zero = regroup(after(v, v_one), y0)
-    keys, values = [k_zero, k_one], [v_zero, v_one]
-    for step in range(2, steps + 1):
-        keys.append(along(keys[-1], LINE))
-        values.append(along(values[-1], LINE))
+    lined = jnp.concatenate([got[:, :HD] for got in lined], axis=0)
 
     width = out_weight.shape[1] // lax.axis_size("tp")
-    weight = after(out_weight, keys[2])
+    weight = after(out_weight, chunks[3])
     weights = [
         lax.dynamic_slice_in_dim(weight, t * width, width, axis=1)
         for t in (tp ^ 3, tp ^ 2, tp ^ 1, tp)
     ]
     outgoing = cache_outgoing(k, v, lengths, owners, position)
-    with jax.named_scope("cache_y1"):
-        held_y1 = cache_y1(after(outgoing, keys[2]))
-    with jax.named_scope("cache_y0"):
-        held_y0 = cache_y0(held_y1)
-    with jax.named_scope("cache_x"):
-        held_x = cache_x(held_y0, position)
+    held_x = cache_x(outgoing, position)
+    held_y1 = cache_y1(held_x)
+    held_y0 = cache_y0(held_y1)
 
     offsets = jnp.arange(rows, dtype=jnp.int32)
     q_at = jnp.concatenate([(2 * (b ^ core) + (a ^ y0)) * rows + offsets for a, b in messages])
@@ -213,37 +214,33 @@
     numerator = jnp.zeros((LINE * rows, HD), jnp.float32)
     denominator = jnp.zeros((LINE * rows,), jnp.float32)
     for step in range(steps + 1):
-        key_sides = (keys[step], swap_core(keys[step]))
-        value_sides = (values[step], swap_core(values[step]))
+        sides = [chunks[step], swap_core(chunks[step])]
         asked = lined
-        if step == 3:
-            asked, weights, held_y0 = lax.optimization_barrier((lined, weights, held_y0))
-        if step == 4:
-            asked = after(lined, held_x)
-        for side in range(2):
+        if step == steps:
+            asked, weights = lax.optimization_barrier((lined, weights))
+            numerator = lax.optimization_barrier(numerator)
+        for side, chunk in enumerate(sides):
             mask = None
             if step == 0:
                 mask = q_at[:, None] >= k_at[side][None, :]
             if step == steps:
                 mask = q_at[:, None] < k_at[side][None, :]
             rounded, total = weigh(
-                asked, key_sides[side], mask, None if step == 0 else plane >= step
+                asked, chunk[: 2 * rows], mask, None if step == 0 else plane >= step
             )
             numerator = numerator + jnp.dot(
-                rounded, value_sides[side], preferred_element_type=jnp.float32
+                rounded, chunk[2 * rows :], preferred_element_type=jnp.float32
             )
             denominator = denominator + total
     attended = (numerator / denominator[:, None]).astype(jnp.bfloat16)
 
     returned = {}
     for n, (a, b) in enumerate(messages):
-        with jax.named_scope(f"back_{n}"):
-            returned[a, b] = move(
-                attended[n * rows : (n + 1) * rows],
-                [(there, here) for here, there in head_pairs(a, b)],
-            )
-    with jax.named_scope("cache_far"):
-        held_far = cache_far(after(held_x, attended), position)
+        returned[a, b] = move(
+            attended[n * rows : (n + 1) * rows],
+            [(there, here) for here, there in head_pairs(a, b)],
+        )
+    held_far = cache_far(after(held_y0, attended), position)
     by_head = []
     for j in range(2):
         flipped = [jnp.where(y0 == 0, returned[j, b], returned[1 - j, b]) for b in range(2)]
@@ -259,13 +256,10 @@
     give_own = swap_core(project(weights[2]).astype(jnp.bfloat16))
     keep_own = project(weights[3])
     away = (keep_away + give_away.astype(jnp.float32)).astype(jnp.bfloat16)
-    with jax.named_scope("across"):
-        across = swap_chip(away)
+    across = swap_chip(away)
     turned = cache_turn(after(held_far, away))
-    with jax.named_scope("cache_w1"):
-        held_w1 = cache_w([turned], 2)
-    with jax.named_scope("cache_w0"):
-        held_w0 = cache_w(held_w1, 1)
+    held_w1 = cache_w([turned], 2)
+    held_w0 = cache_w(held_w1, 1)
     cache = cache_sorted(jnp.concatenate(held_w0, axis=0), position)
     cache_keys, cache_values = cache[:, : k.shape[1]], cache[:, k.shape[1] :]
     branch = (keep_own + give_own.astype(jnp.float32)) + across.astype(jnp.float32)
@@ -289,7 +283,7 @@
         P(),
     )
     return jax.shard_map(
-        local,
+        layer,
         mesh=mesh,
         in_specs=placed,
         out_specs=(P(None, "seq", "tp"), P(None, "seq", "tp"), P(None, "seq", "tp")),

time: 145 us -> 146 us (level)
  the two profiles are of different devices: /device:TPU:1 before, /device:TPU:6 now
where the time goes in v3:
time: 146 us
  waiting for transfers between devices  70.7 us (48%)
  starting transfers between devices  50.7 us (35%)
  matrix products  17.5 us (12%)
  local copies, waits for them, and re-layouts  2.38 us (2%)
  between operations  2.33 us (2%)
  other arithmetic  2.11 us (1%)
    ppermute x5, waiting for transfers between devices, along(): return lax.ppermute(x, 'seq', [(i, i + by) for i in range(peers - by)])  34.7 us
    ppermute x5, starting transfers between devices, along(): return lax.ppermute(x, 'seq', [(i, i + by) for i in range(peers - by)])  13.5 us
    ppermute x1, starting transfers between devices, cache_y1(): return kept + [lax.ppermute(given, 'seq', first_planes(2))]  13.5 us
    ppermute x12, starting transfers between devices, move(): return lax.ppermute(x, ('seq', 'tp'), pairs)  10.7 us
    ppermute x2, waiting for transfers between devices, swap_chip(): return lax.ppermute(x, 'tp', [(i, i ^ 2) for i in range(peers)])  9.67 us
    ppermute x1, waiting for transfers between devices, cache_x(): got = lax.ppermute(given, 'seq', [(i, i + 32) for i in range(16)])  8.78 us
    dot_general x10, matrix products, weigh(): lax.dot_general(q, k, (((1,), (1,)), ((), ())), preferred_element_type=jn...  7.85 us
    ppermute x8, starting transfers between devices, swap_core(): return lax.ppermute(x, 'tp', [(i, i ^ 1) for i in range(peers)])  7.33 us
  transfers between devices with their start and end apart: 33, of which 17 were waited for; matrix products, arithmetic and copies ran while one was open for 13% of the time, Pallas kernels for 0%

profile of v3, /device:TPU:6, one launch (start us, length us, event | category | flops | bytes accessed | tf_op | source)
XLA Modules:
  0.0 145.7 jit_solution(3263619839168048557)
XLA Ops:
  0.7 4.0 %collective-permute-start.5 = (bf16[256,512]{1,0:T(8,128)(2,1)}, bf16[256,512]{1,0:T(8,128)(2,1)S(1)}, u32[]{:S(2)}, u32[]{:S(2)}) collective-permute-start(bf16[256,512]{1,0:T(8,128)(2,1)} %bitcast.49), channel_id=1, source_target_pairs={{0,16},{4,20},{8,24},{12,28},{16,32},{20,36},{24,40},{28,44},{32,4... | collective-permute-start | bytes 786440 | tf_op jit(solution)/shard_map/ppermute | solution.py:32
  4.6 3.8 %collective-permute-start.8 = (bf16[256,512]{1,0:T(8,128)(2,1)}, bf16[256,512]{1,0:T(8,128)(2,1)S(1)}, u32[]{:S(2)}, u32[]{:S(2)}) collective-permute-start(bf16[256,512]{1,0:T(8,128)(2,1)} %bitcast.51), channel_id=1, source_target_pairs={{0,16},{4,20},{8,24},{12,28},{16,32},{20,36},{24,40},{28,44},{32,4... | collective-permute-start | bytes 786440 | tf_op jit(solution)/shard_map/ppermute | solution.py:32
  10.0 1.4 convolution_convert_fusion
  14.0 1.6 %collective-permute-start.2 = (bf16[256,256]{1,0:T(8,128)(2,1)}, bf16[256,256]{1,0:T(8,128)(2,1)S(1)}, u32[]{:S(2)}, u32[]{:S(2)}) collective-permute-start(bf16[256,256]{1,0:T(8,128)(2,1)} %get-tuple-element.40), channel_id=1, source_target_pairs={{0,1},{1,9},{2,3},{3,11},{4,5},{5,13},{6,7},{7,15},{8,0},{9,8},{10... | collective-permute-start | bytes 393224 | tf_op jit(solution)/shard_map/ppermute | solution.py:53
  16.8 1.6 %collective-permute-start.1 = (bf16[256,768]{1,0:T(8,128)(2,1)S(1)}, bf16[256,768]{1,0:T(8,128)(2,1)S(1)}, u32[]{:S(2)}, u32[]{:S(2)}) collective-permute-start(bf16[256,768]{1,0:T(8,128)(2,1)S(1)} %pad_maximum_fusion.4), channel_id=1, source_target_pairs={{0,4},{1,12},{2,6},{3,14},{4,0},{5,8},{6,2},{7,10},{8,5},{9,13},{1... | collective-permute-start | bytes 1179656 | tf_op jit(solution)/shard_map/ppermute | solution.py:53
  18.4 8.8 %collective-permute-done.27 = bf16[128,1024]{1,0:T(8,128)(2,1)S(1)} collective-permute-done((bf16[128,1024]{1,0:T(8,128)(2,1)S(1)}, bf16[128,1024]{1,0:T(8,128)(2,1)S(1)}, u32[]{:S(2)}, u32[]{:S(2)}) %collective-permute-start.27) | collective-permute-done | bytes 262176 | tf_op jit(solution)/shard_map/ppermute | solution.py:118
  27.9 1.7 %collective-permute-start.7 = (bf16[256,256]{1,0:T(8,128)(2,1)S(1)}, bf16[256,256]{1,0:T(8,128)(2,1)S(1)}, u32[]{:S(2)}, u32[]{:S(2)}) collective-permute-start(bf16[256,256]{1,0:T(8,128)(2,1)S(1)} %get-tuple-element.51), channel_id=1, source_target_pairs={{0,4},{1,12},{2,6},{3,14},{4,0},{5,8},{6,2},{7,10},{8,5},{9,13},{1... | collective-permute-start | bytes 393224 | tf_op jit(solution)/shard_map/ppermute | solution.py:53
  30.3 2.6 %collective-permute-done.7 = bf16[256,256]{1,0:T(8,128)(2,1)S(1)} collective-permute-done((bf16[256,256]{1,0:T(8,128)(2,1)S(1)}, bf16[256,256]{1,0:T(8,128)(2,1)S(1)}, u32[]{:S(2)}, u32[]{:S(2)}) %collective-permute-start.7) | collective-permute-done | bytes 131104 | tf_op jit(solution)/shard_map/ppermute | solution.py:53
  32.9 1.6 %collective-permute-start.10 = (bf16[256,256]{1,0:T(8,128)(2,1)S(1)}, bf16[256,256]{1,0:T(8,128)(2,1)S(1)}, u32[]{:S(2)}, u32[]{:S(2)}) collective-permute-start(bf16[256,256]{1,0:T(8,128)(2,1)S(1)} %get-tuple-element.49), channel_id=1, source_target_pairs={{0,4},{1,12},{2,6},{3,14},{4,0},{5,8},{6,2},{7,10},{8,5},{9,13},{1... | collective-permute-start | bytes 393224 | tf_op jit(solution)/shard_map/ppermute | solution.py:53
  34.5 13.5 %collective-permute-start.28 = (bf16[64,1024]{1,0:T(8,128)(2,1)S(1)}, bf16[64,1024]{1,0:T(8,128)(2,1)S(1)}, u32[]{:S(2)}, u32[]{:S(2)}) collective-permute-start(bf16[64,1024]{1,0:T(8,128)(2,1)S(1)} %slice.246), channel_id=1, source_target_pairs={{0,8},{4,12},{8,0},{12,4},{16,24},{20,28},{24,16},{28,20},{32,40},... | collective-permute-start | bytes 393224 | tf_op jit(solution)/shard_map/ppermute | solution.py:124
  48.8 3.5 %collective-permute-done.28 = bf16[64,1024]{1,0:T(8,128)(2,1)S(1)} collective-permute-done((bf16[64,1024]{1,0:T(8,128)(2,1)S(1)}, bf16[64,1024]{1,0:T(8,128)(2,1)S(1)}, u32[]{:S(2)}, u32[]{:S(2)}) %collective-permute-start.28) | collective-permute-done | bytes 131104 | tf_op jit(solution)/shard_map/ppermute | solution.py:124
  52.2 1.9 %collective-permute-start.12 = (bf16[1024,256]{1,0:T(8,128)(2,1)S(1)}, bf16[1024,256]{1,0:T(8,128)(2,1)S(1)}, u32[]{:S(2)}, u32[]{:S(2)}) collective-permute-start(bf16[1024,256]{1,0:T(8,128)(2,1)S(1)} %constant_dynamic-update-slice_fusion), channel_id=1, source_target_pairs={{0,16},{4,20},{8,24},{12,28},{16,32},{20,36},{24,40},{28,44},{32,4... | collective-permute-start | bytes 1572872 | tf_op jit(solution)/shard_map/ppermute | solution.py:32
  54.3 2.6 %collective-permute-start.29 = (bf16[64,1024]{1,0:T(8,128)(2,1)S(1)}, bf16[64,1024]{1,0:T(8,128)(2,1)S(1)}, u32[]{:S(2)}, u32[]{:S(2)}) collective-permute-start(bf16[64,1024]{1,0:T(8,128)(2,1)S(1)} %pad_maximum_fusion.5), channel_id=1, source_target_pairs={{0,4},{4,0},{8,12},{12,8},{16,20},{20,16},{24,28},{28,24},{32,36},... | collective-permute-start | bytes 393224 | tf_op jit(solution)/shard_map/ppermute | solution.py:129
  57.0 1.8 %collective-permute-start.4 = (bf16[1024,256]{1,0:T(8,128)(2,1)S(1)}, bf16[1024,256]{1,0:T(8,128)(2,1)S(1)}, u32[]{:S(2)}, u32[]{:S(2)}) collective-permute-start(bf16[1024,256]{1,0:T(8,128)(2,1)S(1)} %pad_maximum_fusion.1), channel_id=1, source_target_pairs={{0,1},{1,0},{2,3},{3,2},{4,5},{5,4},{6,7},{7,6},{8,9},{9,8},{10,11... | collective-permute-start | bytes 1572872 | tf_op jit(solution)/shard_map/ppermute | solution.py:22
  61.4 10.2 %collective-permute-done.12 = bf16[1024,256]{1,0:T(8,128)(2,1)S(1)} collective-permute-done((bf16[1024,256]{1,0:T(8,128)(2,1)S(1)}, bf16[1024,256]{1,0:T(8,128)(2,1)S(1)}, u32[]{:S(2)}, u32[]{:S(2)}) %collective-permute-start.12) | collective-permute-done | bytes 524320 | tf_op jit(solution)/shard_map/ppermute | solution.py:32
  71.5 1.9 %collective-permute-start.14 = (bf16[1024,256]{1,0:T(8,128)(2,1)S(1)}, bf16[1024,256]{1,0:T(8,128)(2,1)S(1)}, u32[]{:S(2)}, u32[]{:S(2)}) collective-permute-start(bf16[1024,256]{1,0:T(8,128)(2,1)S(1)} %collective-permute-done.12), channel_id=1, source_target_pairs={{0,16},{4,20},{8,24},{12,28},{16,32},{20,36},{24,40},{28,44},{32,4... | collective-permute-start | bytes 1572872 | tf_op jit(solution)/shard_map/ppermute | solution.py:32
  78.1 11.9 %collective-permute-done.14 = bf16[1024,256]{1,0:T(8,128)(2,1)S(1)} collective-permute-done((bf16[1024,256]{1,0:T(8,128)(2,1)S(1)}, bf16[1024,256]{1,0:T(8,128)(2,1)S(1)}, u32[]{:S(2)}, u32[]{:S(2)}) %collective-permute-start.14) | collective-permute-done | bytes 524320 | tf_op jit(solution)/shard_map/ppermute | solution.py:32
  90.6 1.9 %collective-permute-start.16 = (bf16[1024,256]{1,0:T(8,128)(2,1)S(1)}, bf16[1024,256]{1,0:T(8,128)(2,1)S(1)}, u32[]{:S(2)}, u32[]{:S(2)}) collective-permute-start(bf16[1024,256]{1,0:T(8,128)(2,1)S(1)} %collective-permute-done.14), channel_id=1, source_target_pairs={{0,16},{4,20},{8,24},{12,28},{16,32},{20,36},{24,40},{28,44},{32,4... | collective-permute-start | bytes 1572872 | tf_op jit(solution)/shard_map/ppermute | solution.py:32
  96.5 11.8 %collective-permute-done.16 = bf16[1024,256]{1,0:T(8,128)(2,1)S(1)} collective-permute-done((bf16[1024,256]{1,0:T(8,128)(2,1)S(1)}, bf16[1024,256]{1,0:T(8,128)(2,1)S(1)}, u32[]{:S(2)}, u32[]{:S(2)}) %collective-permute-start.16) | collective-permute-done | bytes 524320 | tf_op jit(solution)/shard_map/ppermute | solution.py:32
  115.2 2.4 %collective-permute-done.21 = bf16[256,256]{1,0:T(8,128)(2,1)S(1)} collective-permute-done((bf16[256,256]{1,0:T(8,128)(2,1)S(1)}, bf16[256,256]{1,0:T(8,128)(2,1)S(1)}, u32[]{:S(2)}, u32[]{:S(2)}) %collective-permute-start.21) | collective-permute-done | bytes 131104 | tf_op jit(solution)/shard_map/ppermute | solution.py:53
  119.1 4.9 %collective-permute-start.23 = (bf16[256,896]{1,0:T(8,128)(2,1)S(1)}, bf16[256,896]{1,0:T(8,128)(2,1)S(1)}, u32[]{:S(2)}, u32[]{:S(2)}) collective-permute-start(bf16[256,896]{1,0:T(8,128)(2,1)S(1)} %convolution_convert_fusion.1), channel_id=1, source_target_pairs={{0,1},{1,0},{2,3},{3,2},{4,5},{5,4},{6,7},{7,6},{8,9},{9,8},{10,11... | collective-permute-start | bytes 1376264 | tf_op jit(solution)/shard_map/ppermute | solution.py:22
  126.6 5.2 %collective-permute-done.31 = bf16[32,1024]{1,0:T(8,128)(2,1)S(1)} collective-permute-done((bf16[32,1024]{1,0:T(8,128)(2,1)S(1)}, bf16[32,1024]{1,0:T(8,128)(2,1)S(1)}, u32[]{:S(2)}, u32[]{:S(2)}) %collective-permute-start.31) | collective-permute-done | bytes 65568 | tf_op jit(solution)/shard_map/ppermute | solution.py:146
  132.0 7.0 %collective-permute-done.24 = bf16[256,896]{1,0:T(8,128)(2,1)S(1)} collective-permute-done((bf16[256,896]{1,0:T(8,128)(2,1)S(1)}, bf16[256,896]{1,0:T(8,128)(2,1)S(1)}, u32[]{:S(2)}, u32[]{:S(2)}) %collective-permute-start.24) | collective-permute-done | bytes 458784 | tf_op jit(solution)/shard_map/ppermute | solution.py:27
  142.1 2.6 %collective-permute-done.26 = f32[256]{0:T(256)S(1)} collective-permute-done((f32[256]{0:T(256)S(1)}, f32[256]{0:T(256)S(1)}, u32[]{:S(2)}, u32[]{:S(2)}) %collective-permute-start.26) | collective-permute-done | bytes 1056 | tf_op jit(solution)/shard_map/ppermute | solution.py:27
  (136 shorter events, 33.3 us)
Async XLA Ops:
  0.7 16.1 %collective-permute-start.5 = (bf16[256,512]{1,0:T(8,128)(2,1)}, bf16[256,512]{1,0:T(8,128)(2,1)S(1)}, u32[]{:S(2)}, u32[]{:S(2)}) collective-permute-start(bf16[256,512]{1,0:T(8,128)(2,1)} %bitcast.49), channel_id=1, source_target_pairs={{0,16},{4,20},{8,24},{12,28},{16,32},{20,36},{24,40},{28,44},{32,4... | collective-permute-start | bytes 786440 | tf_op jit(solution)/shard_map/ppermute | solution.py:32
  4.6 23.2 %collective-permute-start.8 = (bf16[256,512]{1,0:T(8,128)(2,1)}, bf16[256,512]{1,0:T(8,128)(2,1)S(1)}, u32[]{:S(2)}, u32[]{:S(2)}) collective-permute-start(bf16[256,512]{1,0:T(8,128)(2,1)} %bitcast.51), channel_id=1, source_target_pairs={{0,16},{4,20},{8,24},{12,28},{16,32},{20,36},{24,40},{28,44},{32,4... | collective-permute-start | bytes 786440 | tf_op jit(solution)/shard_map/ppermute | solution.py:32
  11.4 15.7 %collective-permute-start.27 = (bf16[128,1024]{1,0:T(8,128)(2,1)S(1)}, bf16[128,1024]{1,0:T(8,128)(2,1)S(1)}, u32[]{:S(2)}, u32[]{:S(2)}) collective-permute-start(bf16[128,1024]{1,0:T(8,128)(2,1)S(1)} %slice.244), channel_id=1, source_target_pairs={{0,128},{4,132},{8,136},{12,140},{16,144},{20,148},{24,152},{28,15... | collective-permute-start | bytes 786440 | tf_op jit(solution)/shard_map/ppermute | solution.py:118
  13.5 43.5 %collective-permute-start.3 = (bf16[256,256]{1,0:T(8,128)(2,1)}, bf16[256,256]{1,0:T(8,128)(2,1)S(1)}, u32[]{:S(2)}, u32[]{:S(2)}) collective-permute-start(bf16[256,256]{1,0:T(8,128)(2,1)} %get-tuple-element.39), channel_id=1, source_target_pairs={{0,5},{1,13},{2,7},{3,15},{4,1},{5,9},{6,3},{7,11},{8,4},{9,12},{1... | collective-permute-start | bytes 393224 | tf_op jit(solution)/shard_map/ppermute | solution.py:53
  14.0 44.8 %collective-permute-start.2 = (bf16[256,256]{1,0:T(8,128)(2,1)}, bf16[256,256]{1,0:T(8,128)(2,1)S(1)}, u32[]{:S(2)}, u32[]{:S(2)}) collective-permute-start(bf16[256,256]{1,0:T(8,128)(2,1)} %get-tuple-element.40), channel_id=1, source_target_pairs={{0,1},{1,9},{2,3},{3,11},{4,5},{5,13},{6,7},{7,15},{8,0},{9,8},{10... | collective-permute-start | bytes 393224 | tf_op jit(solution)/shard_map/ppermute | solution.py:53
  16.8 37.4 %collective-permute-start.1 = (bf16[256,768]{1,0:T(8,128)(2,1)S(1)}, bf16[256,768]{1,0:T(8,128)(2,1)S(1)}, u32[]{:S(2)}, u32[]{:S(2)}) collective-permute-start(bf16[256,768]{1,0:T(8,128)(2,1)S(1)} %pad_maximum_fusion.4), channel_id=1, source_target_pairs={{0,4},{1,12},{2,6},{3,14},{4,0},{5,8},{6,2},{7,10},{8,5},{9,13},{1... | collective-permute-start | bytes 1179656 | tf_op jit(solution)/shard_map/ppermute | solution.py:53
  32.9 15.1 %collective-permute-start.10 = (bf16[256,256]{1,0:T(8,128)(2,1)S(1)}, bf16[256,256]{1,0:T(8,128)(2,1)S(1)}, u32[]{:S(2)}, u32[]{:S(2)}) collective-permute-start(bf16[256,256]{1,0:T(8,128)(2,1)S(1)} %get-tuple-element.49), channel_id=1, source_target_pairs={{0,4},{1,12},{2,6},{3,14},{4,0},{5,8},{6,2},{7,10},{8,5},{9,13},{1... | collective-permute-start | bytes 393224 | tf_op jit(solution)/shard_map/ppermute | solution.py:53
  34.5 17.7 %collective-permute-start.28 = (bf16[64,1024]{1,0:T(8,128)(2,1)S(1)}, bf16[64,1024]{1,0:T(8,128)(2,1)S(1)}, u32[]{:S(2)}, u32[]{:S(2)}) collective-permute-start(bf16[64,1024]{1,0:T(8,128)(2,1)S(1)} %slice.246), channel_id=1, source_target_pairs={{0,8},{4,12},{8,0},{12,4},{16,24},{20,28},{24,16},{28,20},{32,40},... | collective-permute-start | bytes 393224 | tf_op jit(solution)/shard_map/ppermute | solution.py:124
  48.0 6.3 %collective-permute-start = (bf16[256,768]{1,0:T(8,128)(2,1)S(1)}, bf16[256,768]{1,0:T(8,128)(2,1)S(1)}, u32[]{:S(2)}, u32[]{:S(2)}) collective-permute-start(bf16[256,768]{1,0:T(8,128)(2,1)S(1)} %pad_maximum_fusion.3), channel_id=1, source_target_pairs={{0,0},{1,8},{2,2},{3,10},{4,4},{5,12},{6,6},{7,14},{8,1},{9,9},{10... | collective-permute-start | bytes 1179656 | tf_op jit(solution)/shard_map/ppermute | solution.py:53
  52.2 19.3 %collective-permute-start.12 = (bf16[1024,256]{1,0:T(8,128)(2,1)S(1)}, bf16[1024,256]{1,0:T(8,128)(2,1)S(1)}, u32[]{:S(2)}, u32[]{:S(2)}) collective-permute-start(bf16[1024,256]{1,0:T(8,128)(2,1)S(1)} %constant_dynamic-update-slice_fusion), channel_id=1, source_target_pairs={{0,16},{4,20},{8,24},{12,28},{16,32},{20,36},{24,40},{28,44},{32,4... | collective-permute-start | bytes 1572872 | tf_op jit(solution)/shard_map/ppermute | solution.py:32
  54.2 21.6 %collective-permute-start.11 = (bf16[1024,256]{1,0:T(8,128)(2,1)S(1)}, bf16[1024,256]{1,0:T(8,128)(2,1)S(1)}, u32[]{:S(2)}, u32[]{:S(2)}) collective-permute-start(bf16[1024,256]{1,0:T(8,128)(2,1)S(1)} %constant_dynamic-update-slice_fusion), channel_id=1, source_target_pairs={{0,1},{1,0},{2,3},{3,2},{4,5},{5,4},{6,7},{7,6},{8,9},{9,8},{10,11... | collective-permute-start | bytes 1572872 | tf_op jit(solution)/shard_map/ppermute | solution.py:22
  54.3 7.0 %collective-permute-start.29 = (bf16[64,1024]{1,0:T(8,128)(2,1)S(1)}, bf16[64,1024]{1,0:T(8,128)(2,1)S(1)}, u32[]{:S(2)}, u32[]{:S(2)}) collective-permute-start(bf16[64,1024]{1,0:T(8,128)(2,1)S(1)} %pad_maximum_fusion.5), channel_id=1, source_target_pairs={{0,4},{4,0},{8,12},{12,8},{16,20},{20,16},{24,28},{28,24},{32,36},... | collective-permute-start | bytes 393224 | tf_op jit(solution)/shard_map/ppermute | solution.py:129
  57.0 16.8 %collective-permute-start.4 = (bf16[1024,256]{1,0:T(8,128)(2,1)S(1)}, bf16[1024,256]{1,0:T(8,128)(2,1)S(1)}, u32[]{:S(2)}, u32[]{:S(2)}) collective-permute-start(bf16[1024,256]{1,0:T(8,128)(2,1)S(1)} %pad_maximum_fusion.1), channel_id=1, source_target_pairs={{0,1},{1,0},{2,3},{3,2},{4,5},{5,4},{6,7},{7,6},{8,9},{9,8},{10,11... | collective-permute-start | bytes 1572872 | tf_op jit(solution)/shard_map/ppermute | solution.py:22
  71.5 18.5 %collective-permute-start.14 = (bf16[1024,256]{1,0:T(8,128)(2,1)S(1)}, bf16[1024,256]{1,0:T(8,128)(2,1)S(1)}, u32[]{:S(2)}, u32[]{:S(2)}) collective-permute-start(bf16[1024,256]{1,0:T(8,128)(2,1)S(1)} %collective-permute-done.12), channel_id=1, source_target_pairs={{0,16},{4,20},{8,24},{12,28},{16,32},{20,36},{24,40},{28,44},{32,4... | collective-permute-start | bytes 1572872 | tf_op jit(solution)/shard_map/ppermute | solution.py:32
  73.5 20.4 %collective-permute-start.13 = (bf16[1024,256]{1,0:T(8,128)(2,1)S(1)}, bf16[1024,256]{1,0:T(8,128)(2,1)S(1)}, u32[]{:S(2)}, u32[]{:S(2)}) collective-permute-start(bf16[1024,256]{1,0:T(8,128)(2,1)S(1)} %collective-permute-done.12), channel_id=1, source_target_pairs={{0,1},{1,0},{2,3},{3,2},{4,5},{5,4},{6,7},{7,6},{8,9},{9,8},{10,11... | collective-permute-start | bytes 1572872 | tf_op jit(solution)/shard_map/ppermute | solution.py:22
  90.6 17.6 %collective-permute-start.16 = (bf16[1024,256]{1,0:T(8,128)(2,1)S(1)}, bf16[1024,256]{1,0:T(8,128)(2,1)S(1)}, u32[]{:S(2)}, u32[]{:S(2)}) collective-permute-start(bf16[1024,256]{1,0:T(8,128)(2,1)S(1)} %collective-permute-done.14), channel_id=1, source_target_pairs={{0,16},{4,20},{8,24},{12,28},{16,32},{20,36},{24,40},{28,44},{32,4... | collective-permute-start | bytes 1572872 | tf_op jit(solution)/shard_map/ppermute | solution.py:32
  111.7 5.9 %collective-permute-start.21 = (bf16[256,256]{1,0:T(8,128)(2,1)S(1)}, bf16[256,256]{1,0:T(8,128)(2,1)S(1)}, u32[]{:S(2)}, u32[]{:S(2)}) collective-permute-start(bf16[256,256]{1,0:T(8,128)(2,1)S(1)} %get-tuple-element.34), channel_id=1, source_target_pairs={{5,0},{13,1},{7,2},{15,3},{1,4},{9,5},{3,6},{11,7},{4,8},{12,9},{6... | collective-permute-start | bytes 393224 | tf_op jit(solution)/shard_map/ppermute | solution.py:53
  111.8 6.5 %collective-permute-start.19 = (bf16[256,256]{1,0:T(8,128)(2,1)S(1)}, bf16[256,256]{1,0:T(8,128)(2,1)S(1)}, u32[]{:S(2)}, u32[]{:S(2)}) collective-permute-start(bf16[256,256]{1,0:T(8,128)(2,1)S(1)} %get-tuple-element.35), channel_id=1, source_target_pairs={{4,0},{12,1},{6,2},{14,3},{0,4},{8,5},{2,6},{10,7},{5,8},{13,9},{7... | collective-permute-start | bytes 393224 | tf_op jit(solution)/shard_map/ppermute | solution.py:53
  112.8 5.6 %collective-permute-start.18 = (bf16[256,256]{1,0:T(8,128)(2,1)S(1)}, bf16[256,256]{1,0:T(8,128)(2,1)S(1)}, u32[]{:S(2)}, u32[]{:S(2)}) collective-permute-start(bf16[256,256]{1,0:T(8,128)(2,1)S(1)} %get-tuple-element.36), channel_id=1, source_target_pairs={{0,0},{8,1},{2,2},{10,3},{4,4},{12,5},{6,6},{14,7},{1,8},{9,9},{3,... | collective-permute-start | bytes 393224 | tf_op jit(solution)/shard_map/ppermute | solution.py:53
  113.5 11.3 %collective-permute-start.30 = (bf16[64,1024]{1,0:T(8,128)(2,1)S(1)}, bf16[64,1024]{1,0:T(8,128)(2,1)S(1)}, u32[]{:S(2)}, u32[]{:S(2)}) collective-permute-start(bf16[64,1024]{1,0:T(8,128)(2,1)S(1)} %pad_maximum_fusion.6), channel_id=1, source_target_pairs={{0,112},{4,116},{8,120},{12,124},{16,96},{20,100},{24,104},{28,108... | collective-permute-start | bytes 393224 | tf_op jit(solution)/shard_map/ppermute | solution.py:140
  119.1 6.3 %collective-permute-start.23 = (bf16[256,896]{1,0:T(8,128)(2,1)S(1)}, bf16[256,896]{1,0:T(8,128)(2,1)S(1)}, u32[]{:S(2)}, u32[]{:S(2)}) collective-permute-start(bf16[256,896]{1,0:T(8,128)(2,1)S(1)} %convolution_convert_fusion.1), channel_id=1, source_target_pairs={{0,1},{1,0},{2,3},{3,2},{4,5},{5,4},{6,7},{7,6},{8,9},{9,8},{10,11... | collective-permute-start | bytes 1376264 | tf_op jit(solution)/shard_map/ppermute | solution.py:22
  124.7 7.3 %collective-permute-start.22 = (bf16[256,896]{1,0:T(8,128)(2,1)S(1)}, bf16[256,896]{1,0:T(8,128)(2,1)S(1)}, u32[]{:S(2)}, u32[]{:S(2)}) collective-permute-start(bf16[256,896]{1,0:T(8,128)(2,1)S(1)} %convolution_convert_fusion.2), channel_id=1, source_target_pairs={{0,1},{1,0},{2,3},{3,2},{4,5},{5,4},{6,7},{7,6},{8,9},{9,8},{10,11... | collective-permute-start | bytes 1376264 | tf_op jit(solution)/shard_map/ppermute | solution.py:22
  126.2 12.9 %collective-permute-start.24 = (bf16[256,896]{1,0:T(8,128)(2,1)S(1)}, bf16[256,896]{1,0:T(8,128)(2,1)S(1)}, u32[]{:S(2)}, u32[]{:S(2)}) collective-permute-start(bf16[256,896]{1,0:T(8,128)(2,1)S(1)} %fusion.7), channel_id=1, source_target_pairs={{0,2},{1,3},{2,0},{3,1},{4,6},{5,7},{6,4},{7,5},{8,10},{9,11},{10,... | collective-permute-start | bytes 1376264 | tf_op jit(solution)/shard_map/ppermute | solution.py:27
  131.9 8.1 %collective-permute-start.32 = (bf16[32,1024]{1,0:T(8,128)(2,1)S(1)}, bf16[32,1024]{1,0:T(8,128)(2,1)S(1)}, u32[]{:S(2)}, u32[]{:S(2)}) collective-permute-start(bf16[32,1024]{1,0:T(8,128)(2,1)S(1)} %pad_maximum_fusion.7), channel_id=1, source_target_pairs={{0,16},{4,20},{8,24},{12,28},{16,0},{20,4},{24,8},{28,12},{32,48},... | collective-permute-start | bytes 196616 | tf_op jit(solution)/shard_map/ppermute | solution.py:146
  (16 other events, 125.5 us)

commit v4 on v3

--- a/solution.py
+++ b/solution.py
@@ -195,11 +195,6 @@
     lined = jnp.concatenate([got[:, :HD] for got in lined], axis=0)
 
     width = out_weight.shape[1] // lax.axis_size("tp")
-    weight = after(out_weight, chunks[3])
-    weights = [
-        lax.dynamic_slice_in_dim(weight, t * width, width, axis=1)
-        for t in (tp ^ 3, tp ^ 2, tp ^ 1, tp)
-    ]
     outgoing = cache_outgoing(k, v, lengths, owners, position)
     held_x = cache_x(outgoing, position)
     held_y1 = cache_y1(held_x)
@@ -213,11 +208,10 @@
     ]
     numerator = jnp.zeros((LINE * rows, HD), jnp.float32)
     denominator = jnp.zeros((LINE * rows,), jnp.float32)
-    for step in range(steps + 1):
+    for step in (1, 0, 2, 3, 4):
         sides = [chunks[step], swap_core(chunks[step])]
         asked = lined
-        if step == steps:
-            asked, weights = lax.optimization_barrier((lined, weights))
+        if step != 1:
             numerator = lax.optimization_barrier(numerator)
         for side, chunk in enumerate(sides):
             mask = None
@@ -248,14 +242,16 @@
             by_head.append(jnp.where(y1 == 0, flipped[b], flipped[1 - b]))
     mixed = jnp.concatenate(by_head, axis=1)
 
-    def project(w):
-        return jnp.dot(mixed, w, preferred_element_type=jnp.float32)
-
-    give_away = swap_core(project(weights[0]).astype(jnp.bfloat16))
-    keep_away = project(weights[1])
-    give_own = swap_core(project(weights[2]).astype(jnp.bfloat16))
-    keep_own = project(weights[3])
-    away = (keep_away + give_away.astype(jnp.float32)).astype(jnp.bfloat16)
+    partial = jnp.dot(mixed, out_weight, preferred_element_type=jnp.float32)
+    partial = partial.astype(jnp.bfloat16)
+
+    def part(t):
+        return lax.dynamic_slice_in_dim(partial, t * width, width, axis=1)
+
+    give_away = swap_core(part(tp ^ 3))
+    give_own = swap_core(part(tp ^ 1))
+    away = (part(tp ^ 2).astype(jnp.float32) + give_away.astype(jnp.float32)).astype(jnp.bfloat16)
+    keep_own = part(tp).astype(jnp.float32)
     across = swap_chip(away)
     turned = cache_turn(after(held_far, away))
     held_w1 = cache_w([turned], 2)

time: 146 us -> 150 us (1.027)
  the two profiles are of different devices: /device:TPU:6 before, /device:TPU:1 now
where the time goes in v4:
time: 150 us; the launch traced here: 148 us
  starting transfers between devices  78.6 us (52%)
  waiting for transfers between devices  43.9 us (29%)
  matrix products  16.5 us (11%)
  local copies, waits for them, and re-layouts  3.48 us (2%)
  other arithmetic  3.37 us (2%)
  between operations  2.22 us (1%)
    ppermute x12, starting transfers between devices, move(): return lax.ppermute(x, ('seq', 'tp'), pairs)  27.4 us
    ppermute x5, starting transfers between devices, along(): return lax.ppermute(x, 'seq', [(i, i + by) for i in range(peers - by)])  20.7 us
    ppermute x5, waiting for transfers between devices, along(): return lax.ppermute(x, 'seq', [(i, i + by) for i in range(peers - by)])  13.1 us
    ppermute x1, starting transfers between devices, cache_far(): got = lax.ppermute(given, 'seq', pairs)  11.5 us
    ppermute x12, waiting for transfers between devices, move(): return lax.ppermute(x, ('seq', 'tp'), pairs)  9.51 us
    ppermute x8, starting transfers between devices, swap_core(): return lax.ppermute(x, 'tp', [(i, i ^ 1) for i in range(peers)])  7.92 us
    dot_general x10, matrix products, weigh(): lax.dot_general(q, k, (((1,), (1,)), ((), ())), preferred_element_type=jn...  7.83 us
    ppermute x2, waiting for transfers between devices, swap_chip(): return lax.ppermute(x, 'tp', [(i, i ^ 2) for i in range(peers)])  5.79 us
  transfers between devices with their start and end apart: 33, of which 20 were waited for; matrix products, arithmetic and copies ran while one was open for 13% of the time, Pallas kernels for 0%

profile of v4, /device:TPU:1, one launch (start us, length us, event | category | flops | bytes accessed | tf_op | source)
XLA Modules:
  0.0 148.1 jit_solution(6439558803953724126)
XLA Ops:
  0.7 4.5 %collective-permute-start.4 = (bf16[256,512]{1,0:T(8,128)(2,1)}, bf16[256,512]{1,0:T(8,128)(2,1)S(1)}, u32[]{:S(2)}, u32[]{:S(2)}) collective-permute-start(bf16[256,512]{1,0:T(8,128)(2,1)} %bitcast.42), channel_id=1, source_target_pairs={{0,16},{4,20},{8,24},{12,28},{16,32},{20,36},{24,40},{28,44},{32,4... | collective-permute-start | bytes 786440 | tf_op jit(solution)/shard_map/ppermute | solution.py:32
  5.2 3.5 %collective-permute-start.7 = (bf16[256,512]{1,0:T(8,128)(2,1)}, bf16[256,512]{1,0:T(8,128)(2,1)S(1)}, u32[]{:S(2)}, u32[]{:S(2)}) collective-permute-start(bf16[256,512]{1,0:T(8,128)(2,1)} %bitcast.44), channel_id=1, source_target_pairs={{0,16},{4,20},{8,24},{12,28},{16,32},{20,36},{24,40},{28,44},{32,4... | collective-permute-start | bytes 786440 | tf_op jit(solution)/shard_map/ppermute | solution.py:32
  9.9 2.8 %collective-permute-start.3 = (bf16[256,256]{1,0:T(8,128)(2,1)S(1)}, bf16[256,256]{1,0:T(8,128)(2,1)S(1)}, u32[]{:S(2)}, u32[]{:S(2)}) collective-permute-start(bf16[256,256]{1,0:T(8,128)(2,1)S(1)} %get-tuple-element.25), channel_id=1, source_target_pairs={{0,5},{1,13},{2,7},{3,15},{4,1},{5,9},{6,3},{7,11},{8,4},{9,12},{1... | collective-permute-start | bytes 393224 | tf_op jit(solution)/shard_map/ppermute | solution.py:53
  12.7 2.3 %collective-permute-start.2 = (bf16[256,256]{1,0:T(8,128)(2,1)S(1)}, bf16[256,256]{1,0:T(8,128)(2,1)S(1)}, u32[]{:S(2)}, u32[]{:S(2)}) collective-permute-start(bf16[256,256]{1,0:T(8,128)(2,1)S(1)} %get-tuple-element.26), channel_id=1, source_target_pairs={{0,1},{1,9},{2,3},{3,11},{4,5},{5,13},{6,7},{7,15},{8,0},{9,8},{10... | collective-permute-start | bytes 393224 | tf_op jit(solution)/shard_map/ppermute | solution.py:53
  17.9 4.7 %collective-permute-start.27 = (bf16[128,1024]{1,0:T(8,128)(2,1)S(1)}, bf16[128,1024]{1,0:T(8,128)(2,1)S(1)}, u32[]{:S(2)}, u32[]{:S(2)}) collective-permute-start(bf16[128,1024]{1,0:T(8,128)(2,1)S(1)} %slice.244), channel_id=1, source_target_pairs={{0,128},{4,132},{8,136},{12,140},{16,144},{20,148},{24,152},{28,15... | collective-permute-start | bytes 786440 | tf_op jit(solution)/shard_map/ppermute | solution.py:118
  23.5 3.9 %collective-permute-done.27 = bf16[128,1024]{1,0:T(8,128)(2,1)S(1)} collective-permute-done((bf16[128,1024]{1,0:T(8,128)(2,1)S(1)}, bf16[128,1024]{1,0:T(8,128)(2,1)S(1)}, u32[]{:S(2)}, u32[]{:S(2)}) %collective-permute-start.27) | collective-permute-done | bytes 262176 | tf_op jit(solution)/shard_map/ppermute | solution.py:118
  27.4 4.1 %collective-permute-start.5 = (bf16[256,256]{1,0:T(8,128)(2,1)S(1)}, bf16[256,256]{1,0:T(8,128)(2,1)S(1)}, u32[]{:S(2)}, u32[]{:S(2)}) collective-permute-start(bf16[256,256]{1,0:T(8,128)(2,1)S(1)} %get-tuple-element.42), channel_id=1, source_target_pairs={{0,0},{1,8},{2,2},{3,10},{4,4},{5,12},{6,6},{7,14},{8,1},{9,9},{10... | collective-permute-start | bytes 393224 | tf_op jit(solution)/shard_map/ppermute | solution.py:53
  32.4 2.7 %collective-permute-done.5 = bf16[256,256]{1,0:T(8,128)(2,1)S(1)} collective-permute-done((bf16[256,256]{1,0:T(8,128)(2,1)S(1)}, bf16[256,256]{1,0:T(8,128)(2,1)S(1)}, u32[]{:S(2)}, u32[]{:S(2)}) %collective-permute-start.5) | collective-permute-done | bytes 131104 | tf_op jit(solution)/shard_map/ppermute | solution.py:53
  35.1 4.2 %collective-permute-start.8 = (bf16[256,256]{1,0:T(8,128)(2,1)S(1)}, bf16[256,256]{1,0:T(8,128)(2,1)S(1)}, u32[]{:S(2)}, u32[]{:S(2)}) collective-permute-start(bf16[256,256]{1,0:T(8,128)(2,1)S(1)} %get-tuple-element.40), channel_id=1, source_target_pairs={{0,0},{1,8},{2,2},{3,10},{4,4},{5,12},{6,6},{7,14},{8,1},{9,9},{10... | collective-permute-start | bytes 393224 | tf_op jit(solution)/shard_map/ppermute | solution.py:53
  40.2 2.7 %collective-permute-done.8 = bf16[256,256]{1,0:T(8,128)(2,1)S(1)} collective-permute-done((bf16[256,256]{1,0:T(8,128)(2,1)S(1)}, bf16[256,256]{1,0:T(8,128)(2,1)S(1)}, u32[]{:S(2)}, u32[]{:S(2)}) %collective-permute-start.8) | collective-permute-done | bytes 131104 | tf_op jit(solution)/shard_map/ppermute | solution.py:53
  45.1 4.1 %collective-permute-start = (bf16[256,768]{1,0:T(8,128)(2,1)S(1)}, bf16[256,768]{1,0:T(8,128)(2,1)S(1)}, u32[]{:S(2)}, u32[]{:S(2)}) collective-permute-start(bf16[256,768]{1,0:T(8,128)(2,1)S(1)} %pad_maximum_fusion.2), channel_id=1, source_target_pairs={{0,0},{1,8},{2,2},{3,10},{4,4},{5,12},{6,6},{7,14},{8,1},{9,9},{10... | collective-permute-start | bytes 1179656 | tf_op jit(solution)/shard_map/ppermute | solution.py:53
  51.4 3.6 %collective-permute-start.12 = (bf16[1024,256]{1,0:T(8,128)(2,1)S(1)}, bf16[1024,256]{1,0:T(8,128)(2,1)S(1)}, u32[]{:S(2)}, u32[]{:S(2)}) collective-permute-start(bf16[1024,256]{1,0:T(8,128)(2,1)S(1)} %constant_dynamic-update-slice_fusion), channel_id=1, source_target_pairs={{0,16},{4,20},{8,24},{12,28},{16,32},{20,36},{24,40},{28,44},{32,4... | collective-permute-start | bytes 1572872 | tf_op jit(solution)/shard_map/ppermute | solution.py:32
  60.0 2.6 %collective-permute-done.29 = bf16[64,1024]{1,0:T(8,128)(2,1)S(1)} collective-permute-done((bf16[64,1024]{1,0:T(8,128)(2,1)S(1)}, bf16[64,1024]{1,0:T(8,128)(2,1)S(1)}, u32[]{:S(2)}, u32[]{:S(2)}) %collective-permute-start.29) | collective-permute-done | bytes 131104 | tf_op jit(solution)/shard_map/ppermute | solution.py:129
  66.0 4.8 %collective-permute-start.14 = (bf16[1024,256]{1,0:T(8,128)(2,1)S(1)}, bf16[1024,256]{1,0:T(8,128)(2,1)S(1)}, u32[]{:S(2)}, u32[]{:S(2)}) collective-permute-start(bf16[1024,256]{1,0:T(8,128)(2,1)S(1)} %collective-permute-done.12), channel_id=1, source_target_pairs={{0,16},{4,20},{8,24},{12,28},{16,32},{20,36},{24,40},{28,44},{32,4... | collective-permute-start | bytes 1572872 | tf_op jit(solution)/shard_map/ppermute | solution.py:32
  74.6 7.0 %collective-permute-done.14 = bf16[1024,256]{1,0:T(8,128)(2,1)S(1)} collective-permute-done((bf16[1024,256]{1,0:T(8,128)(2,1)S(1)}, bf16[1024,256]{1,0:T(8,128)(2,1)S(1)}, u32[]{:S(2)}, u32[]{:S(2)}) %collective-permute-start.14) | collective-permute-done | bytes 524320 | tf_op jit(solution)/shard_map/ppermute | solution.py:32
  81.6 4.3 %collective-permute-start.16 = (bf16[1024,256]{1,0:T(8,128)(2,1)S(1)}, bf16[1024,256]{1,0:T(8,128)(2,1)S(1)}, u32[]{:S(2)}, u32[]{:S(2)}) collective-permute-start(bf16[1024,256]{1,0:T(8,128)(2,1)S(1)} %collective-permute-done.14), channel_id=1, source_target_pairs={{0,16},{4,20},{8,24},{12,28},{16,32},{20,36},{24,40},{28,44},{32,4... | collective-permute-start | bytes 1572872 | tf_op jit(solution)/shard_map/ppermute | solution.py:32
  90.2 5.8 %collective-permute-done.16 = bf16[1024,256]{1,0:T(8,128)(2,1)S(1)} collective-permute-done((bf16[1024,256]{1,0:T(8,128)(2,1)S(1)}, bf16[1024,256]{1,0:T(8,128)(2,1)S(1)}, u32[]{:S(2)}, u32[]{:S(2)}) %collective-permute-start.16) | collective-permute-done | bytes 524320 | tf_op jit(solution)/shard_map/ppermute | solution.py:32
  100.9 3.7 %collective-permute-start.18 = (bf16[256,256]{1,0:T(8,128)(2,1)S(1)}, bf16[256,256]{1,0:T(8,128)(2,1)S(1)}, u32[]{:S(2)}, u32[]{:S(2)}) collective-permute-start(bf16[256,256]{1,0:T(8,128)(2,1)S(1)} %get-tuple-element.22), channel_id=1, source_target_pairs={{0,0},{8,1},{2,2},{10,3},{4,4},{12,5},{6,6},{14,7},{1,8},{9,9},{3,... | collective-permute-start | bytes 393224 | tf_op jit(solution)/shard_map/ppermute | solution.py:53
  105.1 3.4 %collective-permute-start.21 = (bf16[256,256]{1,0:T(8,128)(2,1)S(1)}, bf16[256,256]{1,0:T(8,128)(2,1)S(1)}, u32[]{:S(2)}, u32[]{:S(2)}) collective-permute-start(bf16[256,256]{1,0:T(8,128)(2,1)S(1)} %get-tuple-element.20), channel_id=1, source_target_pairs={{5,0},{13,1},{7,2},{15,3},{1,4},{9,5},{3,6},{11,7},{4,8},{12,9},{6... | collective-permute-start | bytes 393224 | tf_op jit(solution)/shard_map/ppermute | solution.py:53
  109.8 3.1 %collective-permute-done.19 = bf16[256,256]{1,0:T(8,128)(2,1)S(1)} collective-permute-done((bf16[256,256]{1,0:T(8,128)(2,1)S(1)}, bf16[256,256]{1,0:T(8,128)(2,1)S(1)}, u32[]{:S(2)}, u32[]{:S(2)}) %collective-permute-start.19) | collective-permute-done | bytes 131104 | tf_op jit(solution)/shard_map/ppermute | solution.py:53
  115.5 11.5 %collective-permute-start.30 = (bf16[64,1024]{1,0:T(8,128)(2,1)S(1)}, bf16[64,1024]{1,0:T(8,128)(2,1)S(1)}, u32[]{:S(2)}, u32[]{:S(2)}) collective-permute-start(bf16[64,1024]{1,0:T(8,128)(2,1)S(1)} %pad_maximum_fusion.5), channel_id=1, source_target_pairs={{0,112},{4,116},{8,120},{12,124},{16,96},{20,100},{24,104},{28,108... | collective-permute-start | bytes 393224 | tf_op jit(solution)/shard_map/ppermute | solution.py:140
  131.9 4.0 %collective-permute-done.31 = bf16[32,1024]{1,0:T(8,128)(2,1)S(1)} collective-permute-done((bf16[32,1024]{1,0:T(8,128)(2,1)S(1)}, bf16[32,1024]{1,0:T(8,128)(2,1)S(1)}, u32[]{:S(2)}, u32[]{:S(2)}) %collective-permute-start.31) | collective-permute-done | bytes 65568 | tf_op jit(solution)/shard_map/ppermute | solution.py:146
  136.0 5.1 %collective-permute-done.24 = bf16[256,896]{1,0:T(8,128)(2,1)S(1)} collective-permute-done((bf16[256,896]{1,0:T(8,128)(2,1)S(1)}, bf16[256,896]{1,0:T(8,128)(2,1)S(1)}, u32[]{:S(2)}, u32[]{:S(2)}) %collective-permute-start.24) | collective-permute-done | bytes 458784 | tf_op jit(solution)/shard_map/ppermute | solution.py:27
  141.4 2.3 %collective-permute-start.25 = (f32[256]{0:T(256)S(1)}, f32[256]{0:T(256)S(1)}, u32[]{:S(2)}, u32[]{:S(2)}) collective-permute-start(f32[256]{0:T(256)S(1)} %multiply_reduce_fusion), channel_id=1, source_target_pairs={{0,1},{1,0},{2,3},{3,2},{4,5},{5,4},{6,7},{7,6},{8,9},{9,8},{10,11... | collective-permute-start | bytes 3080 | tf_op jit(solution)/shard_map/ppermute | solution.py:22
  (132 shorter events, 45.0 us)
Async XLA Ops:
  0.7 22.3 %collective-permute-start.4 = (bf16[256,512]{1,0:T(8,128)(2,1)}, bf16[256,512]{1,0:T(8,128)(2,1)S(1)}, u32[]{:S(2)}, u32[]{:S(2)}) collective-permute-start(bf16[256,512]{1,0:T(8,128)(2,1)} %bitcast.42), channel_id=1, source_target_pairs={{0,16},{4,20},{8,24},{12,28},{16,32},{20,36},{24,40},{28,44},{32,4... | collective-permute-start | bytes 786440 | tf_op jit(solution)/shard_map/ppermute | solution.py:32
  5.2 26.4 %collective-permute-start.7 = (bf16[256,512]{1,0:T(8,128)(2,1)}, bf16[256,512]{1,0:T(8,128)(2,1)S(1)}, u32[]{:S(2)}, u32[]{:S(2)}) collective-permute-start(bf16[256,512]{1,0:T(8,128)(2,1)} %bitcast.44), channel_id=1, source_target_pairs={{0,16},{4,20},{8,24},{12,28},{16,32},{20,36},{24,40},{28,44},{32,4... | collective-permute-start | bytes 786440 | tf_op jit(solution)/shard_map/ppermute | solution.py:32
  9.9 47.9 %collective-permute-start.3 = (bf16[256,256]{1,0:T(8,128)(2,1)S(1)}, bf16[256,256]{1,0:T(8,128)(2,1)S(1)}, u32[]{:S(2)}, u32[]{:S(2)}) collective-permute-start(bf16[256,256]{1,0:T(8,128)(2,1)S(1)} %get-tuple-element.25), channel_id=1, source_target_pairs={{0,5},{1,13},{2,7},{3,15},{4,1},{5,9},{6,3},{7,11},{8,4},{9,12},{1... | collective-permute-start | bytes 393224 | tf_op jit(solution)/shard_map/ppermute | solution.py:53
  12.7 45.2 %collective-permute-start.2 = (bf16[256,256]{1,0:T(8,128)(2,1)S(1)}, bf16[256,256]{1,0:T(8,128)(2,1)S(1)}, u32[]{:S(2)}, u32[]{:S(2)}) collective-permute-start(bf16[256,256]{1,0:T(8,128)(2,1)S(1)} %get-tuple-element.26), channel_id=1, source_target_pairs={{0,1},{1,9},{2,3},{3,11},{4,5},{5,13},{6,7},{7,15},{8,0},{9,8},{10... | collective-permute-start | bytes 393224 | tf_op jit(solution)/shard_map/ppermute | solution.py:53
  17.9 9.4 %collective-permute-start.27 = (bf16[128,1024]{1,0:T(8,128)(2,1)S(1)}, bf16[128,1024]{1,0:T(8,128)(2,1)S(1)}, u32[]{:S(2)}, u32[]{:S(2)}) collective-permute-start(bf16[128,1024]{1,0:T(8,128)(2,1)S(1)} %slice.244), channel_id=1, source_target_pairs={{0,128},{4,132},{8,136},{12,140},{16,144},{20,148},{24,152},{28,15... | collective-permute-start | bytes 786440 | tf_op jit(solution)/shard_map/ppermute | solution.py:118
  22.9 32.1 %collective-permute-start.1 = (bf16[256,768]{1,0:T(8,128)(2,1)S(1)}, bf16[256,768]{1,0:T(8,128)(2,1)S(1)}, u32[]{:S(2)}, u32[]{:S(2)}) collective-permute-start(bf16[256,768]{1,0:T(8,128)(2,1)S(1)} %pad_maximum_fusion.3), channel_id=1, source_target_pairs={{0,4},{1,12},{2,6},{3,14},{4,0},{5,8},{6,2},{7,10},{8,5},{9,13},{1... | collective-permute-start | bytes 1179656 | tf_op jit(solution)/shard_map/ppermute | solution.py:53
  27.4 7.8 %collective-permute-start.5 = (bf16[256,256]{1,0:T(8,128)(2,1)S(1)}, bf16[256,256]{1,0:T(8,128)(2,1)S(1)}, u32[]{:S(2)}, u32[]{:S(2)}) collective-permute-start(bf16[256,256]{1,0:T(8,128)(2,1)S(1)} %get-tuple-element.42), channel_id=1, source_target_pairs={{0,0},{1,8},{2,2},{3,10},{4,4},{5,12},{6,6},{7,14},{8,1},{9,9},{10... | collective-permute-start | bytes 393224 | tf_op jit(solution)/shard_map/ppermute | solution.py:53
  31.6 7.8 %collective-permute-start.6 = (bf16[256,256]{1,0:T(8,128)(2,1)S(1)}, bf16[256,256]{1,0:T(8,128)(2,1)S(1)}, u32[]{:S(2)}, u32[]{:S(2)}) collective-permute-start(bf16[256,256]{1,0:T(8,128)(2,1)S(1)} %get-tuple-element.41), channel_id=1, source_target_pairs={{0,4},{1,12},{2,6},{3,14},{4,0},{5,8},{6,2},{7,10},{8,5},{9,13},{1... | collective-permute-start | bytes 393224 | tf_op jit(solution)/shard_map/ppermute | solution.py:53
  35.1 7.8 %collective-permute-start.8 = (bf16[256,256]{1,0:T(8,128)(2,1)S(1)}, bf16[256,256]{1,0:T(8,128)(2,1)S(1)}, u32[]{:S(2)}, u32[]{:S(2)}) collective-permute-start(bf16[256,256]{1,0:T(8,128)(2,1)S(1)} %get-tuple-element.40), channel_id=1, source_target_pairs={{0,0},{1,8},{2,2},{3,10},{4,4},{5,12},{6,6},{7,14},{8,1},{9,9},{10... | collective-permute-start | bytes 393224 | tf_op jit(solution)/shard_map/ppermute | solution.py:53
  42.9 8.5 %collective-permute-start.28 = (bf16[64,1024]{1,0:T(8,128)(2,1)S(1)}, bf16[64,1024]{1,0:T(8,128)(2,1)S(1)}, u32[]{:S(2)}, u32[]{:S(2)}) collective-permute-start(bf16[64,1024]{1,0:T(8,128)(2,1)S(1)} %slice.246), channel_id=1, source_target_pairs={{0,8},{4,12},{8,0},{12,4},{16,24},{20,28},{24,16},{28,20},{32,40},... | collective-permute-start | bytes 393224 | tf_op jit(solution)/shard_map/ppermute | solution.py:124
  45.1 10.6 %collective-permute-start = (bf16[256,768]{1,0:T(8,128)(2,1)S(1)}, bf16[256,768]{1,0:T(8,128)(2,1)S(1)}, u32[]{:S(2)}, u32[]{:S(2)}) collective-permute-start(bf16[256,768]{1,0:T(8,128)(2,1)S(1)} %pad_maximum_fusion.2), channel_id=1, source_target_pairs={{0,0},{1,8},{2,2},{3,10},{4,4},{5,12},{6,6},{7,14},{8,1},{9,9},{10... | collective-permute-start | bytes 1179656 | tf_op jit(solution)/shard_map/ppermute | solution.py:53
  51.4 14.6 %collective-permute-start.12 = (bf16[1024,256]{1,0:T(8,128)(2,1)S(1)}, bf16[1024,256]{1,0:T(8,128)(2,1)S(1)}, u32[]{:S(2)}, u32[]{:S(2)}) collective-permute-start(bf16[1024,256]{1,0:T(8,128)(2,1)S(1)} %constant_dynamic-update-slice_fusion), channel_id=1, source_target_pairs={{0,16},{4,20},{8,24},{12,28},{16,32},{20,36},{24,40},{28,44},{32,4... | collective-permute-start | bytes 1572872 | tf_op jit(solution)/shard_map/ppermute | solution.py:32
  55.0 7.6 %collective-permute-start.10 = (bf16[1024,256]{1,0:T(8,128)(2,1)S(1)}, bf16[1024,256]{1,0:T(8,128)(2,1)S(1)}, u32[]{:S(2)}, u32[]{:S(2)}) collective-permute-start(bf16[1024,256]{1,0:T(8,128)(2,1)S(1)} %constant_dynamic-update-slice_fusion), channel_id=1, source_target_pairs={{0,1},{1,0},{2,3},{3,2},{4,5},{5,4},{6,7},{7,6},{8,9},{9,8},{10,11... | collective-permute-start | bytes 1572872 | tf_op jit(solution)/shard_map/ppermute | solution.py:22
  66.0 15.6 %collective-permute-start.14 = (bf16[1024,256]{1,0:T(8,128)(2,1)S(1)}, bf16[1024,256]{1,0:T(8,128)(2,1)S(1)}, u32[]{:S(2)}, u32[]{:S(2)}) collective-permute-start(bf16[1024,256]{1,0:T(8,128)(2,1)S(1)} %collective-permute-done.12), channel_id=1, source_target_pairs={{0,16},{4,20},{8,24},{12,28},{16,32},{20,36},{24,40},{28,44},{32,4... | collective-permute-start | bytes 1572872 | tf_op jit(solution)/shard_map/ppermute | solution.py:32
  81.6 14.4 %collective-permute-start.16 = (bf16[1024,256]{1,0:T(8,128)(2,1)S(1)}, bf16[1024,256]{1,0:T(8,128)(2,1)S(1)}, u32[]{:S(2)}, u32[]{:S(2)}) collective-permute-start(bf16[1024,256]{1,0:T(8,128)(2,1)S(1)} %collective-permute-done.14), channel_id=1, source_target_pairs={{0,16},{4,20},{8,24},{12,28},{16,32},{20,36},{24,40},{28,44},{32,4... | collective-permute-start | bytes 1572872 | tf_op jit(solution)/shard_map/ppermute | solution.py:32
  100.9 8.9 %collective-permute-start.18 = (bf16[256,256]{1,0:T(8,128)(2,1)S(1)}, bf16[256,256]{1,0:T(8,128)(2,1)S(1)}, u32[]{:S(2)}, u32[]{:S(2)}) collective-permute-start(bf16[256,256]{1,0:T(8,128)(2,1)S(1)} %get-tuple-element.22), channel_id=1, source_target_pairs={{0,0},{8,1},{2,2},{10,3},{4,4},{12,5},{6,6},{14,7},{1,8},{9,9},{3,... | collective-permute-start | bytes 393224 | tf_op jit(solution)/shard_map/ppermute | solution.py:53
  104.6 8.3 %collective-permute-start.19 = (bf16[256,256]{1,0:T(8,128)(2,1)S(1)}, bf16[256,256]{1,0:T(8,128)(2,1)S(1)}, u32[]{:S(2)}, u32[]{:S(2)}) collective-permute-start(bf16[256,256]{1,0:T(8,128)(2,1)S(1)} %get-tuple-element.21), channel_id=1, source_target_pairs={{4,0},{12,1},{6,2},{14,3},{0,4},{8,5},{2,6},{10,7},{5,8},{13,9},{7... | collective-permute-start | bytes 393224 | tf_op jit(solution)/shard_map/ppermute | solution.py:53
  105.1 7.9 %collective-permute-start.20 = (bf16[256,256]{1,0:T(8,128)(2,1)S(1)}, bf16[256,256]{1,0:T(8,128)(2,1)S(1)}, u32[]{:S(2)}, u32[]{:S(2)}) collective-permute-start(bf16[256,256]{1,0:T(8,128)(2,1)S(1)} %get-tuple-element.19), channel_id=1, source_target_pairs={{1,0},{9,1},{3,2},{11,3},{5,4},{13,5},{7,6},{15,7},{0,8},{8,9},{2,... | collective-permute-start | bytes 393224 | tf_op jit(solution)/shard_map/ppermute | solution.py:53
  105.1 8.0 %collective-permute-start.21 = (bf16[256,256]{1,0:T(8,128)(2,1)S(1)}, bf16[256,256]{1,0:T(8,128)(2,1)S(1)}, u32[]{:S(2)}, u32[]{:S(2)}) collective-permute-start(bf16[256,256]{1,0:T(8,128)(2,1)S(1)} %get-tuple-element.20), channel_id=1, source_target_pairs={{5,0},{13,1},{7,2},{15,3},{1,4},{9,5},{3,6},{11,7},{4,8},{12,9},{6... | collective-permute-start | bytes 393224 | tf_op jit(solution)/shard_map/ppermute | solution.py:53
  115.4 14.8 %collective-permute-start.23 = (bf16[256,896]{1,0:T(8,128)(2,1)S(1)}, bf16[256,896]{1,0:T(8,128)(2,1)S(1)}, u32[]{:S(2)}, u32[]{:S(2)}) collective-permute-start(bf16[256,896]{1,0:T(8,128)(2,1)S(1)} %get-tuple-element.14), channel_id=1, source_target_pairs={{0,1},{1,0},{2,3},{3,2},{4,5},{5,4},{6,7},{7,6},{8,9},{9,8},{10,11... | collective-permute-start | bytes 1376264 | tf_op jit(solution)/shard_map/ppermute | solution.py:22
  115.5 13.8 %collective-permute-start.30 = (bf16[64,1024]{1,0:T(8,128)(2,1)S(1)}, bf16[64,1024]{1,0:T(8,128)(2,1)S(1)}, u32[]{:S(2)}, u32[]{:S(2)}) collective-permute-start(bf16[64,1024]{1,0:T(8,128)(2,1)S(1)} %pad_maximum_fusion.5), channel_id=1, source_target_pairs={{0,112},{4,116},{8,120},{12,124},{16,96},{20,100},{24,104},{28,108... | collective-permute-start | bytes 393224 | tf_op jit(solution)/shard_map/ppermute | solution.py:140
  127.1 8.9 %collective-permute-start.22 = (bf16[256,896]{1,0:T(8,128)(2,1)S(1)}, bf16[256,896]{1,0:T(8,128)(2,1)S(1)}, u32[]{:S(2)}, u32[]{:S(2)}) collective-permute-start(bf16[256,896]{1,0:T(8,128)(2,1)S(1)} %get-tuple-element.13), channel_id=1, source_target_pairs={{0,1},{1,0},{2,3},{3,2},{4,5},{5,4},{6,7},{7,6},{8,9},{9,8},{10,11... | collective-permute-start | bytes 1376264 | tf_op jit(solution)/shard_map/ppermute | solution.py:22
  130.3 10.8 %collective-permute-start.24 = (bf16[256,896]{1,0:T(8,128)(2,1)S(1)}, bf16[256,896]{1,0:T(8,128)(2,1)S(1)}, u32[]{:S(2)}, u32[]{:S(2)}) collective-permute-start(bf16[256,896]{1,0:T(8,128)(2,1)S(1)} %add_convert_fusion), channel_id=1, source_target_pairs={{0,2},{1,3},{2,0},{3,1},{4,6},{5,7},{6,4},{7,5},{8,10},{9,11},{10,... | collective-permute-start | bytes 1376264 | tf_op jit(solution)/shard_map/ppermute | solution.py:27
  135.9 7.8 %collective-permute-start.32 = (bf16[32,1024]{1,0:T(8,128)(2,1)S(1)}, bf16[32,1024]{1,0:T(8,128)(2,1)S(1)}, u32[]{:S(2)}, u32[]{:S(2)}) collective-permute-start(bf16[32,1024]{1,0:T(8,128)(2,1)S(1)} %pad_maximum_fusion.6), channel_id=1, source_target_pairs={{0,16},{4,20},{8,24},{12,28},{16,0},{20,4},{24,8},{28,12},{32,48},... | collective-permute-start | bytes 196616 | tf_op jit(solution)/shard_map/ppermute | solution.py:146
  (15 other events, 142.1 us)

commit v5 on v4

--- a/solution.py
+++ b/solution.py
@@ -178,10 +178,11 @@
     v_raw = along(v, LINE)
     messages = [(a, b) for b in range(2) for a in range(2)]
     asked_for = [head_of(q, 2 * (a ^ y0) + (b ^ y1)) for a, b in messages]
-    stored = regroup(k_raw, y0) + regroup(v_raw, y0)
-    chunks = [None, jnp.concatenate(stored, axis=0)]
+    keys = [None, jnp.concatenate(regroup(k_raw, y0), axis=0)]
+    values = [None, jnp.concatenate(regroup(v_raw, y0), axis=0)]
     for _ in range(2, steps + 1):
-        chunks.append(along(chunks[-1], LINE))
+        keys.append(along(keys[-1], LINE))
+        values.append(along(values[-1], LINE))
     lined = []
     for n, (a, b) in enumerate(messages):
         columns = [asked_for[n]]
@@ -189,7 +190,7 @@
             columns += [head_of(k, a ^ y0), head_of(v, a ^ y0)]
         got = move(jnp.concatenate(columns, axis=1), head_pairs(a, b))
         lined.append(got)
-    chunks[0] = jnp.concatenate(
+    chunk = jnp.concatenate(
         [got[:, at : at + HD] for at in (HD, 2 * HD) for got in lined[:2]], axis=0
     )
     lined = jnp.concatenate([got[:, :HD] for got in lined], axis=0)
@@ -209,21 +210,28 @@
     numerator = jnp.zeros((LINE * rows, HD), jnp.float32)
     denominator = jnp.zeros((LINE * rows,), jnp.float32)
     for step in (1, 0, 2, 3, 4):
-        sides = [chunks[step], swap_core(chunks[step])]
+        if step == 0:
+            other = swap_core(chunk)
+            sides = [(x[: 2 * rows], x[2 * rows :]) for x in (chunk, other)]
+        else:
+            sides = [
+                (keys[step], values[step]),
+                (swap_core(keys[step]), swap_core(values[step])),
+            ]
         asked = lined
         if step != 1:
             numerator = lax.optimization_barrier(numerator)
-        for side, chunk in enumerate(sides):
+        for side, (key_side, value_side) in enumerate(sides):
             mask = None
             if step == 0:
                 mask = q_at[:, None] >= k_at[side][None, :]
             if step == steps:
                 mask = q_at[:, None] < k_at[side][None, :]
             rounded, total = weigh(
-                asked, chunk[: 2 * rows], mask, None if step == 0 else plane >= step
+                asked, key_side, mask, None if step == 0 else plane >= step
             )
             numerator = numerator + jnp.dot(
-                rounded, chunk[2 * rows :], preferred_element_type=jnp.float32
+                rounded, value_side, preferred_element_type=jnp.float32
             )
             denominator = denominator + total
     attended = (numerator / denominator[:, None]).astype(jnp.bfloat16)

time: 150 us -> 150 us (level); the launches traced: 148 us -> 150 us
  starting transfers between devices: 78.6 us -> 81.1 us
    ppermute x5 -> x8, waiting for transfers between devices: 13.1 us -> 2.92 us  [along(): return lax.ppermute(x, 'seq', [(i, i + by) for i in range(peers - by)])]
    ppermute x5 -> x8, starting transfers between devices: 20.7 us -> 27.2 us  [along(): return lax.ppermute(x, 'seq', [(i, i + by) for i in range(peers - by)])]
    ppermute x1, starting transfers between devices: 11.5 us -> 7.8 us  [cache_far(): got = lax.ppermute(given, 'seq', pairs)]
    ppermute x1, waiting for transfers between devices: 1.42 us -> 4.97 us  [cache_far(): got = lax.ppermute(given, 'seq', pairs)]
    ppermute x2, waiting for transfers between devices: 5.79 us -> 8.29 us  [swap_chip(): return lax.ppermute(x, 'tp', [(i, i ^ 2) for i in range(peers)])]
    ppermute x12, waiting for transfers between devices: 9.51 us -> 11.8 us  [move(): return lax.ppermute(x, ('seq', 'tp'), pairs)]
    ppermute x2, starting transfers between devices: 2.32 us -> 0.68 us  [swap_chip(): return lax.ppermute(x, 'tp', [(i, i ^ 2) for i in range(peers)])]
    ppermute x8 -> x12, starting transfers between devices: 7.92 us -> 9.37 us  [swap_core(): return lax.ppermute(x, 'tp', [(i, i ^ 1) for i in range(peers)])]
  transfers between devices with their start and end apart: 33 -> 40, of which waited for: 20 -> 15; matrix products, arithmetic and copies ran while one was open for 13% -> 13% of each run, Pallas kernels for 0% -> 0%
where the time goes in v5:
time: 150 us
  starting transfers between devices  81.1 us (54%)
  waiting for transfers between devices  43.2 us (29%)
  matrix products  16.5 us (11%)
  local copies, waits for them, and re-layouts  3.5 us (2%)
  other arithmetic  3.37 us (2%)
  between operations  2.33 us (2%)
    ppermute x8, starting transfers between devices, along(): return lax.ppermute(x, 'seq', [(i, i + by) for i in range(peers - by)])  27.2 us
    ppermute x12, starting transfers between devices, move(): return lax.ppermute(x, ('seq', 'tp'), pairs)  26.7 us
    ppermute x12, waiting for transfers between devices, move(): return lax.ppermute(x, ('seq', 'tp'), pairs)  11.8 us
    ppermute x12, starting transfers between devices, swap_core(): return lax.ppermute(x, 'tp', [(i, i ^ 1) for i in range(peers)])  9.37 us
    ppermute x2, waiting for transfers between devices, swap_chip(): return lax.ppermute(x, 'tp', [(i, i ^ 2) for i in range(peers)])  8.29 us
    dot_general x10, matrix products, weigh(): lax.dot_general(q, k, (((1,), (1,)), ((), ())), preferred_element_type=jn...  7.83 us
    ppermute x1, starting transfers between devices, cache_far(): got = lax.ppermute(given, 'seq', pairs)  7.8 us
    ppermute x1, waiting for transfers between devices, cache_far(): got = lax.ppermute(given, 'seq', pairs)  4.97 us
  transfers between devices with their start and end apart: 40, of which 15 were waited for; matrix products, arithmetic and copies ran while one was open for 13% of the time, Pallas kernels for 0%

profile of v5, /device:TPU:1, one launch (start us, length us, event | category | flops | bytes accessed | tf_op | source)
XLA Modules:
  0.0 149.9 jit_solution(18177993151064218565)
XLA Ops:
  0.7 4.5 %collective-permute-start.7 = (bf16[256,512]{1,0:T(8,128)(2,1)}, bf16[256,512]{1,0:T(8,128)(2,1)S(1)}, u32[]{:S(2)}, u32[]{:S(2)}) collective-permute-start(bf16[256,512]{1,0:T(8,128)(2,1)} %bitcast.58), channel_id=1, source_target_pairs={{0,16},{4,20},{8,24},{12,28},{16,32},{20,36},{24,40},{28,44},{32,4... | collective-permute-start | bytes 786440 | tf_op jit(solution)/shard_map/ppermute | solution.py:32
  5.2 3.5 %collective-permute-start.4 = (bf16[256,512]{1,0:T(8,128)(2,1)}, bf16[256,512]{1,0:T(8,128)(2,1)S(1)}, u32[]{:S(2)}, u32[]{:S(2)}) collective-permute-start(bf16[256,512]{1,0:T(8,128)(2,1)} %bitcast.60), channel_id=1, source_target_pairs={{0,16},{4,20},{8,24},{12,28},{16,32},{20,36},{24,40},{28,44},{32,4... | collective-permute-start | bytes 786440 | tf_op jit(solution)/shard_map/ppermute | solution.py:32
  9.9 2.8 %collective-permute-start.3 = (bf16[256,256]{1,0:T(8,128)(2,1)S(1)}, bf16[256,256]{1,0:T(8,128)(2,1)S(1)}, u32[]{:S(2)}, u32[]{:S(2)}) collective-permute-start(bf16[256,256]{1,0:T(8,128)(2,1)S(1)} %get-tuple-element.25), channel_id=1, source_target_pairs={{0,5},{1,13},{2,7},{3,15},{4,1},{5,9},{6,3},{7,11},{8,4},{9,12},{1... | collective-permute-start | bytes 393224 | tf_op jit(solution)/shard_map/ppermute | solution.py:53
  17.9 4.7 %collective-permute-start.34 = (bf16[128,1024]{1,0:T(8,128)(2,1)S(1)}, bf16[128,1024]{1,0:T(8,128)(2,1)S(1)}, u32[]{:S(2)}, u32[]{:S(2)}) collective-permute-start(bf16[128,1024]{1,0:T(8,128)(2,1)S(1)} %slice.170), channel_id=1, source_target_pairs={{0,128},{4,132},{8,136},{12,140},{16,144},{20,148},{24,152},{28,15... | collective-permute-start | bytes 786440 | tf_op jit(solution)/shard_map/ppermute | solution.py:118
  22.9 4.4 %collective-permute-done.34 = bf16[128,1024]{1,0:T(8,128)(2,1)S(1)} collective-permute-done((bf16[128,1024]{1,0:T(8,128)(2,1)S(1)}, bf16[128,1024]{1,0:T(8,128)(2,1)S(1)}, u32[]{:S(2)}, u32[]{:S(2)}) %collective-permute-start.34) | collective-permute-done | bytes 262176 | tf_op jit(solution)/shard_map/ppermute | solution.py:118
  32.0 2.5 %collective-permute-start.8 = (bf16[256,256]{1,0:T(8,128)(2,1)S(1)}, bf16[256,256]{1,0:T(8,128)(2,1)S(1)}, u32[]{:S(2)}, u32[]{:S(2)}) collective-permute-start(bf16[256,256]{1,0:T(8,128)(2,1)S(1)} %get-tuple-element.42), channel_id=1, source_target_pairs={{0,0},{1,8},{2,2},{3,10},{4,4},{5,12},{6,6},{7,14},{8,1},{9,9},{10... | collective-permute-start | bytes 393224 | tf_op jit(solution)/shard_map/ppermute | solution.py:53
  34.6 3.5 %collective-permute-done.35 = bf16[64,1024]{1,0:T(8,128)(2,1)S(1)} collective-permute-done((bf16[64,1024]{1,0:T(8,128)(2,1)S(1)}, bf16[64,1024]{1,0:T(8,128)(2,1)S(1)}, u32[]{:S(2)}, u32[]{:S(2)}) %collective-permute-start.35) | collective-permute-done | bytes 131104 | tf_op jit(solution)/shard_map/ppermute | solution.py:124
  38.1 3.5 %collective-permute-start.5 = (bf16[256,256]{1,0:T(8,128)(2,1)S(1)}, bf16[256,256]{1,0:T(8,128)(2,1)S(1)}, u32[]{:S(2)}, u32[]{:S(2)}) collective-permute-start(bf16[256,256]{1,0:T(8,128)(2,1)S(1)} %get-tuple-element.40), channel_id=1, source_target_pairs={{0,0},{1,8},{2,2},{3,10},{4,4},{5,12},{6,6},{7,14},{8,1},{9,9},{10... | collective-permute-start | bytes 393224 | tf_op jit(solution)/shard_map/ppermute | solution.py:53
  42.8 3.0 %collective-permute-done.5 = bf16[256,256]{1,0:T(8,128)(2,1)S(1)} collective-permute-done((bf16[256,256]{1,0:T(8,128)(2,1)S(1)}, bf16[256,256]{1,0:T(8,128)(2,1)S(1)}, u32[]{:S(2)}, u32[]{:S(2)}) %collective-permute-start.5) | collective-permute-done | bytes 131104 | tf_op jit(solution)/shard_map/ppermute | solution.py:53
  45.8 2.5 %collective-permute-start.6 = (bf16[256,256]{1,0:T(8,128)(2,1)S(1)}, bf16[256,256]{1,0:T(8,128)(2,1)S(1)}, u32[]{:S(2)}, u32[]{:S(2)}) collective-permute-start(bf16[256,256]{1,0:T(8,128)(2,1)S(1)} %get-tuple-element.39), channel_id=1, source_target_pairs={{0,4},{1,12},{2,6},{3,14},{4,0},{5,8},{6,2},{7,10},{8,5},{9,13},{1... | collective-permute-start | bytes 393224 | tf_op jit(solution)/shard_map/ppermute | solution.py:53
  51.4 2.7 %collective-permute-start.14 = (bf16[512,256]{1,0:T(8,128)(2,1)S(1)}, bf16[512,256]{1,0:T(8,128)(2,1)S(1)}, u32[]{:S(2)}, u32[]{:S(2)}) collective-permute-start(bf16[512,256]{1,0:T(8,128)(2,1)S(1)} %constant_dynamic-update-slice_fusion.2), channel_id=1, source_target_pairs={{0,16},{4,20},{8,24},{12,28},{16,32},{20,36},{24,40},{28,44},{32,4... | collective-permute-start | bytes 786440 | tf_op jit(solution)/shard_map/ppermute | solution.py:32
  54.3 4.7 %collective-permute-done = bf16[256,768]{1,0:T(8,128)(2,1)S(1)} collective-permute-done((bf16[256,768]{1,0:T(8,128)(2,1)S(1)}, bf16[256,768]{1,0:T(8,128)(2,1)S(1)}, u32[]{:S(2)}, u32[]{:S(2)}) %collective-permute-start) | collective-permute-done | bytes 393248 | tf_op jit(solution)/shard_map/ppermute | solution.py:53
  59.0 3.1 %collective-permute-start.13 = (bf16[512,256]{1,0:T(8,128)(2,1)S(1)}, bf16[512,256]{1,0:T(8,128)(2,1)S(1)}, u32[]{:S(2)}, u32[]{:S(2)}) collective-permute-start(bf16[512,256]{1,0:T(8,128)(2,1)S(1)} %constant_dynamic-update-slice_fusion), channel_id=1, source_target_pairs={{0,16},{4,20},{8,24},{12,28},{16,32},{20,36},{24,40},{28,44},{32,4... | collective-permute-start | bytes 786440 | tf_op jit(solution)/shard_map/ppermute | solution.py:32
  71.8 4.8 %collective-permute-start.18 = (bf16[512,256]{1,0:T(8,128)(2,1)S(1)}, bf16[512,256]{1,0:T(8,128)(2,1)S(1)}, u32[]{:S(2)}, u32[]{:S(2)}) collective-permute-start(bf16[512,256]{1,0:T(8,128)(2,1)S(1)} %collective-permute-done.14), channel_id=1, source_target_pairs={{0,16},{4,20},{8,24},{12,28},{16,32},{20,36},{24,40},{28,44},{32,4... | collective-permute-start | bytes 786440 | tf_op jit(solution)/shard_map/ppermute | solution.py:32
  77.0 2.6 %collective-permute-start.17 = (bf16[512,256]{1,0:T(8,128)(2,1)S(1)}, bf16[512,256]{1,0:T(8,128)(2,1)S(1)}, u32[]{:S(2)}, u32[]{:S(2)}) collective-permute-start(bf16[512,256]{1,0:T(8,128)(2,1)S(1)} %collective-permute-done.13), channel_id=1, source_target_pairs={{0,16},{4,20},{8,24},{12,28},{16,32},{20,36},{24,40},{28,44},{32,4... | collective-permute-start | bytes 786440 | tf_op jit(solution)/shard_map/ppermute | solution.py:32
  88.0 3.9 %collective-permute-start.21 = (bf16[512,256]{1,0:T(8,128)(2,1)S(1)}, bf16[512,256]{1,0:T(8,128)(2,1)S(1)}, u32[]{:S(2)}, u32[]{:S(2)}) collective-permute-start(bf16[512,256]{1,0:T(8,128)(2,1)S(1)} %collective-permute-done.17), channel_id=1, source_target_pairs={{0,16},{4,20},{8,24},{12,28},{16,32},{20,36},{24,40},{28,44},{32,4... | collective-permute-start | bytes 786440 | tf_op jit(solution)/shard_map/ppermute | solution.py:32
  96.2 2.9 %collective-permute-done.21 = bf16[512,256]{1,0:T(8,128)(2,1)S(1)} collective-permute-done((bf16[512,256]{1,0:T(8,128)(2,1)S(1)}, bf16[512,256]{1,0:T(8,128)(2,1)S(1)}, u32[]{:S(2)}, u32[]{:S(2)}) %collective-permute-start.21) | collective-permute-done | bytes 262176 | tf_op jit(solution)/shard_map/ppermute | solution.py:32
  103.0 3.4 %collective-permute-start.25 = (bf16[256,256]{1,0:T(8,128)(2,1)S(1)}, bf16[256,256]{1,0:T(8,128)(2,1)S(1)}, u32[]{:S(2)}, u32[]{:S(2)}) collective-permute-start(bf16[256,256]{1,0:T(8,128)(2,1)S(1)} %get-tuple-element.22), channel_id=1, source_target_pairs={{0,0},{8,1},{2,2},{10,3},{4,4},{12,5},{6,6},{14,7},{1,8},{9,9},{3,... | collective-permute-start | bytes 393224 | tf_op jit(solution)/shard_map/ppermute | solution.py:53
  107.8 2.5 %collective-permute-start.28 = (bf16[256,256]{1,0:T(8,128)(2,1)S(1)}, bf16[256,256]{1,0:T(8,128)(2,1)S(1)}, u32[]{:S(2)}, u32[]{:S(2)}) collective-permute-start(bf16[256,256]{1,0:T(8,128)(2,1)S(1)} %get-tuple-element.20), channel_id=1, source_target_pairs={{5,0},{13,1},{7,2},{15,3},{1,4},{9,5},{3,6},{11,7},{4,8},{12,9},{6... | collective-permute-start | bytes 393224 | tf_op jit(solution)/shard_map/ppermute | solution.py:53
  111.6 3.0 %collective-permute-done.26 = bf16[256,256]{1,0:T(8,128)(2,1)S(1)} collective-permute-done((bf16[256,256]{1,0:T(8,128)(2,1)S(1)}, bf16[256,256]{1,0:T(8,128)(2,1)S(1)}, u32[]{:S(2)}, u32[]{:S(2)}) %collective-permute-start.26) | collective-permute-done | bytes 131104 | tf_op jit(solution)/shard_map/ppermute | solution.py:53
  117.5 7.8 %collective-permute-start.37 = (bf16[64,1024]{1,0:T(8,128)(2,1)S(1)}, bf16[64,1024]{1,0:T(8,128)(2,1)S(1)}, u32[]{:S(2)}, u32[]{:S(2)}) collective-permute-start(bf16[64,1024]{1,0:T(8,128)(2,1)S(1)} %pad_maximum_fusion.5), channel_id=1, source_target_pairs={{0,112},{4,116},{8,120},{12,124},{16,96},{20,100},{24,104},{28,108... | collective-permute-start | bytes 393224 | tf_op jit(solution)/shard_map/ppermute | solution.py:140
  126.2 5.0 %collective-permute-done.37 = bf16[64,1024]{1,0:T(8,128)(2,1)S(1)} collective-permute-done((bf16[64,1024]{1,0:T(8,128)(2,1)S(1)}, bf16[64,1024]{1,0:T(8,128)(2,1)S(1)}, u32[]{:S(2)}, u32[]{:S(2)}) %collective-permute-start.37) | collective-permute-done | bytes 131104 | tf_op jit(solution)/shard_map/ppermute | solution.py:140
  132.9 4.0 %collective-permute-done.38 = bf16[32,1024]{1,0:T(8,128)(2,1)S(1)} collective-permute-done((bf16[32,1024]{1,0:T(8,128)(2,1)S(1)}, bf16[32,1024]{1,0:T(8,128)(2,1)S(1)}, u32[]{:S(2)}, u32[]{:S(2)}) %collective-permute-start.38) | collective-permute-done | bytes 65568 | tf_op jit(solution)/shard_map/ppermute | solution.py:146
  137.0 6.8 %collective-permute-done.31 = bf16[256,896]{1,0:T(8,128)(2,1)S(1)} collective-permute-done((bf16[256,896]{1,0:T(8,128)(2,1)S(1)}, bf16[256,896]{1,0:T(8,128)(2,1)S(1)}, u32[]{:S(2)}, u32[]{:S(2)}) %collective-permute-start.31) | collective-permute-done | bytes 458784 | tf_op jit(solution)/shard_map/ppermute | solution.py:27
  (146 shorter events, 55.4 us)
Async XLA Ops:
  0.7 28.8 %collective-permute-start.7 = (bf16[256,512]{1,0:T(8,128)(2,1)}, bf16[256,512]{1,0:T(8,128)(2,1)S(1)}, u32[]{:S(2)}, u32[]{:S(2)}) collective-permute-start(bf16[256,512]{1,0:T(8,128)(2,1)} %bitcast.58), channel_id=1, source_target_pairs={{0,16},{4,20},{8,24},{12,28},{16,32},{20,36},{24,40},{28,44},{32,4... | collective-permute-start | bytes 786440 | tf_op jit(solution)/shard_map/ppermute | solution.py:32
  5.2 26.9 %collective-permute-start.4 = (bf16[256,512]{1,0:T(8,128)(2,1)}, bf16[256,512]{1,0:T(8,128)(2,1)S(1)}, u32[]{:S(2)}, u32[]{:S(2)}) collective-permute-start(bf16[256,512]{1,0:T(8,128)(2,1)} %bitcast.60), channel_id=1, source_target_pairs={{0,16},{4,20},{8,24},{12,28},{16,32},{20,36},{24,40},{28,44},{32,4... | collective-permute-start | bytes 786440 | tf_op jit(solution)/shard_map/ppermute | solution.py:32
  9.9 52.2 %collective-permute-start.3 = (bf16[256,256]{1,0:T(8,128)(2,1)S(1)}, bf16[256,256]{1,0:T(8,128)(2,1)S(1)}, u32[]{:S(2)}, u32[]{:S(2)}) collective-permute-start(bf16[256,256]{1,0:T(8,128)(2,1)S(1)} %get-tuple-element.25), channel_id=1, source_target_pairs={{0,5},{1,13},{2,7},{3,15},{4,1},{5,9},{6,3},{7,11},{8,4},{9,12},{1... | collective-permute-start | bytes 393224 | tf_op jit(solution)/shard_map/ppermute | solution.py:53
  12.7 49.5 %collective-permute-start.2 = (bf16[256,256]{1,0:T(8,128)(2,1)S(1)}, bf16[256,256]{1,0:T(8,128)(2,1)S(1)}, u32[]{:S(2)}, u32[]{:S(2)}) collective-permute-start(bf16[256,256]{1,0:T(8,128)(2,1)S(1)} %get-tuple-element.26), channel_id=1, source_target_pairs={{0,1},{1,9},{2,3},{3,11},{4,5},{5,13},{6,7},{7,15},{8,0},{9,8},{10... | collective-permute-start | bytes 393224 | tf_op jit(solution)/shard_map/ppermute | solution.py:53
  17.9 9.4 %collective-permute-start.34 = (bf16[128,1024]{1,0:T(8,128)(2,1)S(1)}, bf16[128,1024]{1,0:T(8,128)(2,1)S(1)}, u32[]{:S(2)}, u32[]{:S(2)}) collective-permute-start(bf16[128,1024]{1,0:T(8,128)(2,1)S(1)} %slice.170), channel_id=1, source_target_pairs={{0,128},{4,132},{8,136},{12,140},{16,144},{20,148},{24,152},{28,15... | collective-permute-start | bytes 786440 | tf_op jit(solution)/shard_map/ppermute | solution.py:118
  27.4 26.8 %collective-permute-start.1 = (bf16[256,768]{1,0:T(8,128)(2,1)S(1)}, bf16[256,768]{1,0:T(8,128)(2,1)S(1)}, u32[]{:S(2)}, u32[]{:S(2)}) collective-permute-start(bf16[256,768]{1,0:T(8,128)(2,1)S(1)} %pad_maximum_fusion.3), channel_id=1, source_target_pairs={{0,4},{1,12},{2,6},{3,14},{4,0},{5,8},{6,2},{7,10},{8,5},{9,13},{1... | collective-permute-start | bytes 1179656 | tf_op jit(solution)/shard_map/ppermute | solution.py:53
  29.5 8.6 %collective-permute-start.35 = (bf16[64,1024]{1,0:T(8,128)(2,1)S(1)}, bf16[64,1024]{1,0:T(8,128)(2,1)S(1)}, u32[]{:S(2)}, u32[]{:S(2)}) collective-permute-start(bf16[64,1024]{1,0:T(8,128)(2,1)S(1)} %slice.172), channel_id=1, source_target_pairs={{0,8},{4,12},{8,0},{12,4},{16,24},{20,28},{24,16},{28,20},{32,40},... | collective-permute-start | bytes 393224 | tf_op jit(solution)/shard_map/ppermute | solution.py:124
  32.0 9.6 %collective-permute-start.8 = (bf16[256,256]{1,0:T(8,128)(2,1)S(1)}, bf16[256,256]{1,0:T(8,128)(2,1)S(1)}, u32[]{:S(2)}, u32[]{:S(2)}) collective-permute-start(bf16[256,256]{1,0:T(8,128)(2,1)S(1)} %get-tuple-element.42), channel_id=1, source_target_pairs={{0,0},{1,8},{2,2},{3,10},{4,4},{5,12},{6,6},{7,14},{8,1},{9,9},{10... | collective-permute-start | bytes 393224 | tf_op jit(solution)/shard_map/ppermute | solution.py:53
  48.4 10.6 %collective-permute-start = (bf16[256,768]{1,0:T(8,128)(2,1)S(1)}, bf16[256,768]{1,0:T(8,128)(2,1)S(1)}, u32[]{:S(2)}, u32[]{:S(2)}) collective-permute-start(bf16[256,768]{1,0:T(8,128)(2,1)S(1)} %pad_maximum_fusion.2), channel_id=1, source_target_pairs={{0,0},{1,8},{2,2},{3,10},{4,4},{5,12},{6,6},{7,14},{8,1},{9,9},{10... | collective-permute-start | bytes 1179656 | tf_op jit(solution)/shard_map/ppermute | solution.py:53
  51.4 20.4 %collective-permute-start.14 = (bf16[512,256]{1,0:T(8,128)(2,1)S(1)}, bf16[512,256]{1,0:T(8,128)(2,1)S(1)}, u32[]{:S(2)}, u32[]{:S(2)}) collective-permute-start(bf16[512,256]{1,0:T(8,128)(2,1)S(1)} %constant_dynamic-update-slice_fusion.2), channel_id=1, source_target_pairs={{0,16},{4,20},{8,24},{12,28},{16,32},{20,36},{24,40},{28,44},{32,4... | collective-permute-start | bytes 786440 | tf_op jit(solution)/shard_map/ppermute | solution.py:32
  54.2 16.7 %collective-permute-start.11 = (bf16[512,256]{1,0:T(8,128)(2,1)S(1)}, bf16[512,256]{1,0:T(8,128)(2,1)S(1)}, u32[]{:S(2)}, u32[]{:S(2)}) collective-permute-start(bf16[512,256]{1,0:T(8,128)(2,1)S(1)} %constant_dynamic-update-slice_fusion.2), channel_id=1, source_target_pairs={{0,1},{1,0},{2,3},{3,2},{4,5},{5,4},{6,7},{7,6},{8,9},{9,8},{10,11... | collective-permute-start | bytes 786440 | tf_op jit(solution)/shard_map/ppermute | solution.py:22
  59.0 18.0 %collective-permute-start.13 = (bf16[512,256]{1,0:T(8,128)(2,1)S(1)}, bf16[512,256]{1,0:T(8,128)(2,1)S(1)}, u32[]{:S(2)}, u32[]{:S(2)}) collective-permute-start(bf16[512,256]{1,0:T(8,128)(2,1)S(1)} %constant_dynamic-update-slice_fusion), channel_id=1, source_target_pairs={{0,16},{4,20},{8,24},{12,28},{16,32},{20,36},{24,40},{28,44},{32,4... | collective-permute-start | bytes 786440 | tf_op jit(solution)/shard_map/ppermute | solution.py:32
  68.7 12.9 %collective-permute-start.12 = (bf16[1024,256]{1,0:T(8,128)(2,1)S(1)}, bf16[1024,256]{1,0:T(8,128)(2,1)S(1)}, u32[]{:S(2)}, u32[]{:S(2)}) collective-permute-start(bf16[1024,256]{1,0:T(8,128)(2,1)S(1)} %pad_maximum_fusion.1), channel_id=1, source_target_pairs={{0,1},{1,0},{2,3},{3,2},{4,5},{5,4},{6,7},{7,6},{8,9},{9,8},{10,11... | collective-permute-start | bytes 1572872 | tf_op jit(solution)/shard_map/ppermute | solution.py:22
  71.8 12.4 %collective-permute-start.18 = (bf16[512,256]{1,0:T(8,128)(2,1)S(1)}, bf16[512,256]{1,0:T(8,128)(2,1)S(1)}, u32[]{:S(2)}, u32[]{:S(2)}) collective-permute-start(bf16[512,256]{1,0:T(8,128)(2,1)S(1)} %collective-permute-done.14), channel_id=1, source_target_pairs={{0,16},{4,20},{8,24},{12,28},{16,32},{20,36},{24,40},{28,44},{32,4... | collective-permute-start | bytes 786440 | tf_op jit(solution)/shard_map/ppermute | solution.py:32
  77.0 11.1 %collective-permute-start.17 = (bf16[512,256]{1,0:T(8,128)(2,1)S(1)}, bf16[512,256]{1,0:T(8,128)(2,1)S(1)}, u32[]{:S(2)}, u32[]{:S(2)}) collective-permute-start(bf16[512,256]{1,0:T(8,128)(2,1)S(1)} %collective-permute-done.13), channel_id=1, source_target_pairs={{0,16},{4,20},{8,24},{12,28},{16,32},{20,36},{24,40},{28,44},{32,4... | collective-permute-start | bytes 786440 | tf_op jit(solution)/shard_map/ppermute | solution.py:32
  84.2 16.5 %collective-permute-start.22 = (bf16[512,256]{1,0:T(8,128)(2,1)S(1)}, bf16[512,256]{1,0:T(8,128)(2,1)S(1)}, u32[]{:S(2)}, u32[]{:S(2)}) collective-permute-start(bf16[512,256]{1,0:T(8,128)(2,1)S(1)} %collective-permute-done.18), channel_id=1, source_target_pairs={{0,16},{4,20},{8,24},{12,28},{16,32},{20,36},{24,40},{28,44},{32,4... | collective-permute-start | bytes 786440 | tf_op jit(solution)/shard_map/ppermute | solution.py:32
  86.3 9.3 %collective-permute-start.20 = (bf16[512,256]{1,0:T(8,128)(2,1)S(1)}, bf16[512,256]{1,0:T(8,128)(2,1)S(1)}, u32[]{:S(2)}, u32[]{:S(2)}) collective-permute-start(bf16[512,256]{1,0:T(8,128)(2,1)S(1)} %collective-permute-done.18), channel_id=1, source_target_pairs={{0,1},{1,0},{2,3},{3,2},{4,5},{5,4},{6,7},{7,6},{8,9},{9,8},{10,11... | collective-permute-start | bytes 786440 | tf_op jit(solution)/shard_map/ppermute | solution.py:22
  88.0 11.0 %collective-permute-start.21 = (bf16[512,256]{1,0:T(8,128)(2,1)S(1)}, bf16[512,256]{1,0:T(8,128)(2,1)S(1)}, u32[]{:S(2)}, u32[]{:S(2)}) collective-permute-start(bf16[512,256]{1,0:T(8,128)(2,1)S(1)} %collective-permute-done.17), channel_id=1, source_target_pairs={{0,16},{4,20},{8,24},{12,28},{16,32},{20,36},{24,40},{28,44},{32,4... | collective-permute-start | bytes 786440 | tf_op jit(solution)/shard_map/ppermute | solution.py:32
  103.0 8.6 %collective-permute-start.25 = (bf16[256,256]{1,0:T(8,128)(2,1)S(1)}, bf16[256,256]{1,0:T(8,128)(2,1)S(1)}, u32[]{:S(2)}, u32[]{:S(2)}) collective-permute-start(bf16[256,256]{1,0:T(8,128)(2,1)S(1)} %get-tuple-element.22), channel_id=1, source_target_pairs={{0,0},{8,1},{2,2},{10,3},{4,4},{12,5},{6,6},{14,7},{1,8},{9,9},{3,... | collective-permute-start | bytes 393224 | tf_op jit(solution)/shard_map/ppermute | solution.py:53
  117.3 14.7 %collective-permute-start.30 = (bf16[256,896]{1,0:T(8,128)(2,1)S(1)}, bf16[256,896]{1,0:T(8,128)(2,1)S(1)}, u32[]{:S(2)}, u32[]{:S(2)}) collective-permute-start(bf16[256,896]{1,0:T(8,128)(2,1)S(1)} %get-tuple-element.14), channel_id=1, source_target_pairs={{0,1},{1,0},{2,3},{3,2},{4,5},{5,4},{6,7},{7,6},{8,9},{9,8},{10,11... | collective-permute-start | bytes 1376264 | tf_op jit(solution)/shard_map/ppermute | solution.py:22
  117.5 13.7 %collective-permute-start.37 = (bf16[64,1024]{1,0:T(8,128)(2,1)S(1)}, bf16[64,1024]{1,0:T(8,128)(2,1)S(1)}, u32[]{:S(2)}, u32[]{:S(2)}) collective-permute-start(bf16[64,1024]{1,0:T(8,128)(2,1)S(1)} %pad_maximum_fusion.5), channel_id=1, source_target_pairs={{0,112},{4,116},{8,120},{12,124},{16,96},{20,100},{24,104},{28,108... | collective-permute-start | bytes 393224 | tf_op jit(solution)/shard_map/ppermute | solution.py:140
  125.3 11.7 %collective-permute-start.29 = (bf16[256,896]{1,0:T(8,128)(2,1)S(1)}, bf16[256,896]{1,0:T(8,128)(2,1)S(1)}, u32[]{:S(2)}, u32[]{:S(2)}) collective-permute-start(bf16[256,896]{1,0:T(8,128)(2,1)S(1)} %get-tuple-element.13), channel_id=1, source_target_pairs={{0,1},{1,0},{2,3},{3,2},{4,5},{5,4},{6,7},{7,6},{8,9},{9,8},{10,11... | collective-permute-start | bytes 1376264 | tf_op jit(solution)/shard_map/ppermute | solution.py:22
  132.2 11.7 %collective-permute-start.31 = (bf16[256,896]{1,0:T(8,128)(2,1)S(1)}, bf16[256,896]{1,0:T(8,128)(2,1)S(1)}, u32[]{:S(2)}, u32[]{:S(2)}) collective-permute-start(bf16[256,896]{1,0:T(8,128)(2,1)S(1)} %add_convert_fusion), channel_id=1, source_target_pairs={{0,2},{1,3},{2,0},{3,1},{4,6},{5,7},{6,4},{7,5},{8,10},{9,11},{10,... | collective-permute-start | bytes 1376264 | tf_op jit(solution)/shard_map/ppermute | solution.py:27
  136.9 8.7 %collective-permute-start.39 = (bf16[32,1024]{1,0:T(8,128)(2,1)S(1)}, bf16[32,1024]{1,0:T(8,128)(2,1)S(1)}, u32[]{:S(2)}, u32[]{:S(2)}) collective-permute-start(bf16[32,1024]{1,0:T(8,128)(2,1)S(1)} %pad_maximum_fusion.6), channel_id=1, source_target_pairs={{0,16},{4,20},{8,24},{12,28},{16,0},{20,4},{24,8},{28,12},{32,48},... | collective-permute-start | bytes 196616 | tf_op jit(solution)/shard_map/ppermute | solution.py:146
  (22 other events, 187.2 us)
